TPU v7x, 32 devices: a whole 2x2x4 slice. The times are simulated.
32 devices in a mesh: row: 8 (over z, y), col: 4 (over x, core).
Axes of the slice: x: 2, y: 2, z: 4, core: 2. Of those that a mesh axis runs over, the one named last changes fastest.
Arguments:
- expression: bfloat16 [4096, 1024], P(('row', 'col')), as said below
- power_order: int32 [20], replicated, may hold values from 0 to 19, each once
Outputs:
- log_conn: float32 [4096, 20], P(('row', 'col'))
- fit: float32 [20], replicated
- slope: float32 [20], replicated
Inputs may be any that keep to these rules, and one draw needn't show every extreme that they name: `expression`: each gene's row has mean zero and unit variance over the samples, up to rounding.
All inputs are finite; a program needn't handle non-finite values.
Results may differ from a plain program's by a relative error of at most 0.0029.
Values may be sent and summed in bfloat16 or wider, within the bound.
No kernel may reach another device: no remote copies, remote signals or barrier semaphores. Data moves between devices by JAX's collectives and lax.ppermute only.
A program may use at most 64 MiB of HBM per device.

v0:
```python
import functools
import math

import jax
import jax.numpy as jnp
from jax import lax
from jax.experimental import pallas as pl
from jax.experimental.pallas import tpu as pltpu
from jax.sharding import PartitionSpec as P


AXES = ("row", "col")
BINS = 128
CHUNK = 8
VMEM = pl.BlockSpec(memory_space=pltpu.VMEM)
SMEM = pl.BlockSpec(memory_space=pltpu.SMEM)
PARAMS = pltpu.CompilerParams(vmem_limit_bytes=16 * 2**20)


def swap(x, mask, count):
    return lax.ppermute(x, AXES, [(i, i ^ mask) for i in range(count)])


def spread(block, masks, count):
    held = {0: block}
    for mask in masks:
        for key in list(held):
            held[key ^ mask] = swap(held[key], mask, count)
    return held


def plan(rows, cols):
    row_masks = [cols << i for i in range(rows.bit_length() - 1)]
    col_masks = [1 << i for i in range(cols.bit_length() - 1)]
    return [row_masks[-1]] + col_masks[1:], row_masks[-2::-1] + col_masks[:1]


def in_vmem(x):
    return pltpu.with_memory_space_constraint(x, pltpu.VMEM)


def pair_sum(values):
    while len(values) > 1:
        values = [a + b for a, b in zip(values[::2], values[1::2])]
    return values[0]


def joined(refs):
    return refs[0][...] if len(refs) == 1 else jnp.concatenate([r[...] for r in refs], axis=0)


def add_powers(panel_refs, partner_refs, total_ref):
    genes, samples = panel_refs[0].shape
    powers = total_ref.shape[1]
    panel = joined(panel_refs)
    many = len(panel_refs) > 1
    groups = [partner_refs] if many else [[ref] for ref in partner_refs]
    begun = False
    for group in groups:
        corr = lax.dot_general(
            joined(group), panel, (((1,), (1,)), ((), ())), preferred_element_type=jnp.float32
        )
        for low in range(0, corr.shape[0], genes):
            for i in range(len(panel_refs)):
                block = corr[low : low + genes, i * genes : (i + 1) * genes]
                magnitude = jnp.abs(block * (1.0 / samples))
                square = magnitude * magnitude
                current = [magnitude, square]
                for power in range(powers):
                    part = jnp.sum(current[power % 2].reshape(-1, 8, genes), axis=0)
                    total_ref[i, power] = total_ref[i, power] + part if begun else part
                    if power + 2 < powers:
                        current[power % 2] = current[power % 2] * square
            begun = True


def power_kernel(n_panel, *refs):
    out_ref, total_ref = refs[-2:]
    add_powers(refs[:n_panel], refs[n_panel:-2], total_ref)
    for i in range(n_panel):
        out_ref[i] = jnp.sum(total_ref[i], axis=1)


def power_sums(panels, partners, powers):
    genes, samples = panels[0].shape
    outs = []
    for first in range(0, len(partners), CHUNK):
        some = partners[first : first + CHUNK]
        flops = len(panels) * len(some) * genes * genes * 2 * samples
        outs.append(
            pl.pallas_call(
                functools.partial(power_kernel, len(panels)),
                out_shape=jax.ShapeDtypeStruct((len(panels), powers, genes), jnp.float32),
                in_specs=[VMEM] * (len(panels) + len(some)),
                out_specs=VMEM,
                scratch_shapes=[pltpu.VMEM((len(panels), powers, 8, genes), jnp.float32)],
                compiler_params=PARAMS,
                cost_estimate=pl.CostEstimate(flops=flops, bytes_accessed=0, transcendentals=0),
                name="power_sums",
            )(*map(in_vmem, panels), *map(in_vmem, some))
        )
    return functools.reduce(jnp.add, outs)


def last_kernel(n_panel, n_partner, parts, slot_ref, *refs):
    part_refs = refs[n_panel + n_partner : -2]
    conn_ref, total_ref = refs[-2:]
    slots = len(parts)
    powers = total_ref.shape[1]
    mine = slot_ref[0]
    add_powers(refs[:n_panel], refs[n_panel : n_panel + n_partner], total_ref)
    for i, where in enumerate(parts):
        slot = jnp.bitwise_xor(mine, i)
        values = [part_refs[a][b] for a, b in where if a is not None]
        values += [jnp.sum(total_ref[b], axis=1) for a, b in where if a is None]
        value = functools.reduce(jnp.add, values)
        for power in range(powers):
            conn_ref[pl.ds(power * slots + slot, 1), :] = value[power : power + 1]


def last_sums(slot, panels, partners, done, parts, powers):
    genes, samples = panels[0].shape
    flops = len(panels) * len(partners) * genes * genes * 2 * samples
    return pl.pallas_call(
        functools.partial(last_kernel, len(panels), len(partners), parts),
        out_shape=jax.ShapeDtypeStruct((powers * len(parts), genes), jnp.float32),
        in_specs=[SMEM] + [VMEM] * (len(panels) + len(partners) + len(done)),
        out_specs=VMEM,
        scratch_shapes=[pltpu.VMEM((len(panels), powers, 8, genes), jnp.float32)],
        compiler_params=PARAMS,
        cost_estimate=pl.CostEstimate(flops=flops, bytes_accessed=0, transcendentals=0),
        name="last_sums",
    )(slot, *map(in_vmem, panels), *map(in_vmem, partners), *map(in_vmem, done))


def hist_kernel(scale, power_ref, slot_ref, conn_ref, other_ref, log_ref, hist_ref, logs, places):
    rows, genes = conn_ref.shape
    powers = log_ref.shape[0]
    slots = rows // powers
    mine = slot_ref[0]
    logs[...] = jnp.log(conn_ref[...] + other_ref[...])
    places[...] = logs[...] * scale
    levels = lax.broadcasted_iota(jnp.int32, (BINS, genes), 0).astype(jnp.float32)
    lane = lax.broadcasted_iota(jnp.int32, (BINS, BINS), 1)
    table = jnp.zeros((BINS, BINS), jnp.float32)
    for t in range(powers):
        first = power_ref[t] * slots
        log_ref[pl.ds(t, 1), :] = logs[pl.ds(first + mine, 1), :]
        weights = pair_sum(
            [
                jnp.maximum(0.0, 1.0 - jnp.abs(places[pl.ds(first + m, 1), :] - levels))
                for m in range(slots)
            ]
        )
        table = jnp.where(lane == t, jnp.sum(weights, axis=1, keepdims=True), table)
    hist_ref[...] = table.T[:powers]


def histogram(power_order, slot, conn, other, scale):
    powers = power_order.shape[0]
    genes = conn.shape[1]
    return pl.pallas_call(
        functools.partial(hist_kernel, scale),
        out_shape=(
            pltpu.VMEM((powers, genes), jnp.float32),
            pltpu.VMEM((powers, BINS), jnp.float32),
        ),
        in_specs=[SMEM, SMEM, VMEM, VMEM],
        out_specs=(VMEM, VMEM),
        scratch_shapes=[pltpu.VMEM(conn.shape, jnp.float32)] * 2,
        compiler_params=PARAMS,
        name="histogram",
    )(power_order, slot, in_vmem(conn), in_vmem(other))


def fit_kernel(log_total, hist_ref, other_ref, fit_ref, slope_ref):
    hist = hist_ref[...] + other_ref[...]
    powers = hist.shape[0]
    lane = lax.broadcasted_iota(jnp.int32, (powers, BINS), 1)
    centers = lane.astype(jnp.float32) * (log_total / (BINS - 1))

    def total(x):
        return jnp.sum(x, axis=1, keepdims=True)

    weight_sum = total(hist)
    ylog = jnp.log(hist + 1.0) - log_total
    xdev = centers - total(hist * centers) / weight_sum
    ydev = ylog - total(hist * ylog) / weight_sum
    sxx = jnp.maximum(total(hist * xdev * xdev) / weight_sum, 0.05)
    syy = jnp.maximum(total(hist * ydev * ydev) / weight_sum, 0.05)
    sxy = total(hist * xdev * ydev) / weight_sum
    own = lax.broadcasted_iota(jnp.int32, (powers, BINS), 0) == lane

    def store(ref, column):
        ref[...] = jnp.sum(jnp.where(own, column, 0.0), axis=0)[:powers]

    store(fit_ref, -sxy * jnp.abs(sxy) / (sxx * syy))
    store(slope_ref, sxy / sxx)


def scale_free_fit(hist, other, log_total):
    powers = hist.shape[0]
    return pl.pallas_call(
        functools.partial(fit_kernel, log_total),
        out_shape=(jax.ShapeDtypeStruct((powers,), jnp.float32),) * 2,
        in_specs=[VMEM, VMEM],
        out_specs=(VMEM, VMEM),
        compiler_params=PARAMS,
        name="scale_free_fit",
    )(in_vmem(hist), in_vmem(other))


def on_device(expression, power_order):
    rows, cols = lax.axis_size("row"), lax.axis_size("col")
    count = rows * cols
    powers = power_order.shape[0]
    log_total = math.log(expression.shape[0] * count)
    panel_masks, partner_masks = plan(rows, cols)
    far, core = panel_masks[0], partner_masks[-1]
    low, sides = partner_masks[0], partner_masks[1:-1]

    partner = spread(expression, partner_masks, count)
    panel = spread(expression, panel_masks, count)
    keys = list(panel)
    front = [k for k in keys if not k & far] + [far]
    rear = [k for k in keys if k not in front]

    index = lax.axis_index(AXES)
    slot = sum(((index // mask) % 2) << i for i, mask in enumerate(panel_masks))
    slot = jnp.reshape(slot, (1,)).astype(jnp.int32)

    relayed = [k for k in partner if bin(k & ~core).count("1") > 1]
    waves = [
        ([0], [0]),
        (front, [core] + sides),
        (front[1:], [0]),
        (front, [k ^ core for k in sides] + [low, low ^ core]),
        (front, relayed),
    ]
    done = []
    parts = {k: [] for k in keys}
    for n, (panels, partners) in enumerate(waves):
        done.append(power_sums([panel[k] for k in panels], [partner[k] for k in partners], powers))
        for i, k in enumerate(panels):
            parts[k].append((n, i))
    everyone = list(partner)
    early, late = everyone[CHUNK:], everyone[:CHUNK]
    if early:
        done.append(power_sums([panel[k] for k in rear], [partner[k] for k in early], powers))
    for i, k in enumerate(rear):
        parts[k] += [(len(done) - 1, i)] * bool(early) + [(None, i)]
    conn = last_sums(
        slot,
        [panel[k] for k in rear],
        [partner[k] for k in late],
        done,
        [parts[k] for k in keys],
        powers,
    )

    for mask in panel_masks[:0:-1]:
        conn = conn + swap(conn, mask, count)
    log_conn, hist = histogram(
        power_order, slot, conn, swap(conn, far, count), (BINS - 1) / log_total
    )
    for mask in partner_masks[:-1]:
        hist = hist + swap(hist, mask, count)
    fit, slope = scale_free_fit(hist, swap(hist, core, count), log_total)
    return (log_conn.T, fit, slope)


def solution(mesh):
    placed = (P(AXES, None), P())
    return jax.shard_map(
        on_device,
        mesh=mesh,
        in_specs=placed,
        out_specs=(P(AXES, None), P(), P()),
        check_vma=False,
    )
```

profile of v0, /device:TPU:0, one launch (start us, length us, event | category | flops | bytes accessed | tf_op | source)
XLA Modules:
  0.0 53.0 jit_solution(12135377870960485462)
XLA Ops:
  0.6 3.1 %collective-permute-start.2 = (bf16[128,1024]{1,0:T(8,128)(2,1)}, bf16[128,1024]{1,0:T(8,128)(2,1)S(1)}, u32[]{:S(2)}, u32[]{:S(2)}) collective-permute-start(bf16[128,1024]{1,0:T(8,128)(2,1)} %refs_1_.3), channel_id=1, source_target_pairs={{0,8},{1,9},{2,10},{3,11},{4,12},{5,13},{6,14},{7,15},{8,0},{9,1},... | collective-permute-start | bytes 786440 | tf_op jit(solution)/shard_map/ppermute | solution.py:21
  3.7 2.6 %collective-permute-start = (bf16[128,1024]{1,0:T(8,128)(2,1)}, bf16[128,1024]{1,0:T(8,128)(2,1)S(1)}, u32[]{:S(2)}, u32[]{:S(2)}) collective-permute-start(bf16[128,1024]{1,0:T(8,128)(2,1)} %refs_1_.3), channel_id=1, source_target_pairs={{0,16},{1,17},{2,18},{3,19},{4,20},{5,21},{6,22},{7,23},{8,24},{9,... | collective-permute-start | bytes 786440 | tf_op jit(solution)/shard_map/ppermute | solution.py:21
  6.3 1.5 %collective-permute-start.3 = (bf16[128,1024]{1,0:T(8,128)(2,1)}, bf16[128,1024]{1,0:T(8,128)(2,1)S(1)}, u32[]{:S(2)}, u32[]{:S(2)}) collective-permute-start(bf16[128,1024]{1,0:T(8,128)(2,1)} %refs_1_.3), channel_id=1, source_target_pairs={{0,4},{1,5},{2,6},{3,7},{4,0},{5,1},{6,2},{7,3},{8,12},{9,13},{10,... | collective-permute-start | bytes 786440 | tf_op jit(solution)/shard_map/ppermute | solution.py:21
  7.9 7.9 %collective-permute-done.2.refs_4_.refs_2_ = bf16[128,1024]{1,0:T(8,128)(2,1)S(1)} collective-permute-done((bf16[128,1024]{1,0:T(8,128)(2,1)}, bf16[128,1024]{1,0:T(8,128)(2,1)S(1)}, u32[]{:S(2)}, u32[]{:S(2)}) %collective-permute-start.2) | collective-permute-done | bytes 262176 | tf_op jit(solution)/shard_map/ppermute | solution.py:21
  15.7 1.7 %collective-permute-start.4 = (bf16[128,1024]{1,0:T(8,128)(2,1)S(1)}, bf16[128,1024]{1,0:T(8,128)(2,1)S(1)}, u32[]{:S(2)}, u32[]{:S(2)}) collective-permute-start(bf16[128,1024]{1,0:T(8,128)(2,1)S(1)} %collective-permute-done.2.refs_4_.refs_2_), channel_id=1, source_target_pairs={{0,4},{1,5},{2,6},{3,7},{4,0},{5,1},{6,2},{7,3},{8,12},{9,13},{10,... | collective-permute-start | bytes 786440 | tf_op jit(solution)/shard_map/ppermute | solution.py:21
  17.4 1.5 %collective-permute-start.9 = (bf16[128,1024]{1,0:T(8,128)(2,1)}, bf16[128,1024]{1,0:T(8,128)(2,1)S(1)}, u32[]{:S(2)}, u32[]{:S(2)}) collective-permute-start(bf16[128,1024]{1,0:T(8,128)(2,1)} %refs_1_.3), channel_id=1, source_target_pairs={{0,2},{1,3},{2,0},{3,1},{4,6},{5,7},{6,4},{7,5},{8,10},{9,11},{10,... | collective-permute-start | bytes 786440 | tf_op jit(solution)/shard_map/ppermute | solution.py:21
  18.9 0.0 collective-permute-start.5
  18.9 0.0 collective-permute-done.refs_2_.refs_1_
  18.9 0.5 collective-permute-start.6
  19.4 0.0 collective-permute-done.3.refs_4_.refs_3_
  19.4 0.1 collective-permute-start.7
  19.5 3.7 %collective-permute-done.4.refs_3_.refs_4_ = bf16[128,1024]{1,0:T(8,128)(2,1)S(1)} collective-permute-done((bf16[128,1024]{1,0:T(8,128)(2,1)S(1)}, bf16[128,1024]{1,0:T(8,128)(2,1)S(1)}, u32[]{:S(2)}, u32[]{:S(2)}) %collective-permute-start.4) | collective-permute-done | bytes 262176 | tf_op jit(solution)/shard_map/ppermute | solution.py:21
  23.2 0.0 collective-permute-start.8
  23.2 1.3 %collective-permute-done.9.refs_1_.refs_0_ = bf16[128,1024]{1,0:T(8,128)(2,1)S(1)} collective-permute-done((bf16[128,1024]{1,0:T(8,128)(2,1)}, bf16[128,1024]{1,0:T(8,128)(2,1)S(1)}, u32[]{:S(2)}, u32[]{:S(2)}) %collective-permute-start.9) | collective-permute-done | bytes 262176 | tf_op jit(solution)/shard_map/ppermute | solution.py:21
  24.6 1.5 %collective-permute-start.1 = (bf16[128,1024]{1,0:T(8,128)(2,1)S(1)}, bf16[128,1024]{1,0:T(8,128)(2,1)S(1)}, u32[]{:S(2)}, u32[]{:S(2)}) collective-permute-start(bf16[128,1024]{1,0:T(8,128)(2,1)S(1)} %collective-permute-done.refs_2_.refs_1_), channel_id=1, source_target_pairs={{0,2},{1,3},{2,0},{3,1},{4,6},{5,7},{6,4},{7,5},{8,10},{9,11},{10,... | collective-permute-start | bytes 786440 | tf_op jit(solution)/shard_map/ppermute | solution.py:21
  26.0 0.0 copy-start
  26.0 0.9 %copy-done = bf16[128,1024]{1,0:T(8,128)(2,1)S(1)} copy-done((bf16[128,1024]{1,0:T(8,128)(2,1)S(1)}, bf16[128,1024]{1,0:T(8,128)(2,1)}, u32[]{:S(2)}) %copy-start) | copy-done | bytes 262168
  27.0 0.3 power_sums.5.refs_9_
  27.3 0.5 power_sums.7.refs_11_
  27.8 0.0 collective-permute-done.5.refs_3_.refs_5_
  27.8 0.9 %power_sums.6.refs_10_ = f32[3,20,128]{2,1,0:T(8,128)S(1)} custom-call(bf16[128,1024]{1,0:T(8,128)(2,1)S(1)} %copy-done, bf16[128,1024]{1,0:T(8,128)(2,1)S(1)} %collective-permute-done.9.refs_1_.refs_0_, bf16[128,1024]{1,0:T(8,128)(2,1)S(1)} %collective-permute-done.refs_2_.refs_1_, bf16[128,1024]{1,0:T(8,128)(2,1)S(1)} %collective-permute-done.5.refs_3_.refs_5_, ...), custom_call_target="tpu_custom_call" | custom-call | flops 201326592 | tf_op jit(solution)/shard_map/power_sums/pallas_call | solution.py:91
  28.8 0.0 collective-permute-done.6.refs_5_.refs_6_
  28.8 0.0 collective-permute-done.7.refs_3_.refs_7_
  28.8 1.3 %power_sums.8.refs_12_ = f32[3,20,128]{2,1,0:T(8,128)S(1)} custom-call(bf16[128,1024]{1,0:T(8,128)(2,1)S(1)} %copy-done, bf16[128,1024]{1,0:T(8,128)(2,1)S(1)} %collective-permute-done.9.refs_1_.refs_0_, bf16[128,1024]{1,0:T(8,128)(2,1)S(1)} %collective-permute-done.refs_2_.refs_1_, bf16[128,1024]{1,0:T(8,128)(2,1)S(1)} %collective-permute-done.7.refs_3_.refs_7_, ...), custom_call_target="tpu_custom_call" | custom-call | flops 301989888 | tf_op jit(solution)/shard_map/power_sums/pallas_call | solution.py:91
  30.1 0.0 collective-permute-done.8.refs_4_.refs_8_
  30.1 0.9 %power_sums.9.refs_13_ = f32[3,20,128]{2,1,0:T(8,128)S(1)} custom-call(bf16[128,1024]{1,0:T(8,128)(2,1)S(1)} %copy-done, bf16[128,1024]{1,0:T(8,128)(2,1)S(1)} %collective-permute-done.9.refs_1_.refs_0_, bf16[128,1024]{1,0:T(8,128)(2,1)S(1)} %collective-permute-done.refs_2_.refs_1_, bf16[128,1024]{1,0:T(8,128)(2,1)S(1)} %collective-permute-done.4.refs_3_.refs_4_, ...), custom_call_target="tpu_custom_call" | custom-call | flops 201326592 | tf_op jit(solution)/shard_map/power_sums/pallas_call | solution.py:91
  31.0 0.9 %collective-permute-done.1.refs_0_ = bf16[128,1024]{1,0:T(8,128)(2,1)S(1)} collective-permute-done((bf16[128,1024]{1,0:T(8,128)(2,1)S(1)}, bf16[128,1024]{1,0:T(8,128)(2,1)S(1)}, u32[]{:S(2)}, u32[]{:S(2)}) %collective-permute-start.1) | collective-permute-done | bytes 262176 | tf_op jit(solution)/shard_map/ppermute | solution.py:21
  31.9 1.3 %last_sums.1 = f32[80,128]{1,0:T(8,128)S(1)} custom-call(s32[1]{0:T(128)} %bitcast.slot_ref, bf16[128,1024]{1,0:T(8,128)(2,1)S(1)} %collective-permute-done.1.refs_0_, bf16[128,1024]{1,0:T(8,128)(2,1)S(1)} %copy-done, bf16[128,1024]{1,0:T(8,128)(2,1)S(1)} %collective-permute-done.2.refs_4_.refs_2_, ...), custom_call_target="tpu_custom_call" | custom-call | flops 268435456 | tf_op jit(solution)/shard_map/last_sums/pallas_call | solution.py:124
  33.2 0.0 copy-start.1
  33.3 1.4 %collective-permute-start.10 = (f32[80,128]{1,0:T(8,128)S(1)}, f32[80,128]{1,0:T(8,128)S(1)}, u32[]{:S(2)}, u32[]{:S(2)}) collective-permute-start(f32[80,128]{1,0:T(8,128)S(1)} %last_sums.1), channel_id=1, source_target_pairs={{0,2},{1,3},{2,0},{3,1},{4,6},{5,7},{6,4},{7,5},{8,10},{9,11},{10,... | collective-permute-start | bytes 122888 | tf_op jit(solution)/shard_map/ppermute | solution.py:21
  34.7 2.6 %collective-permute-done.10 = f32[80,128]{1,0:T(8,128)S(1)} collective-permute-done((f32[80,128]{1,0:T(8,128)S(1)}, f32[80,128]{1,0:T(8,128)S(1)}, u32[]{:S(2)}, u32[]{:S(2)}) %collective-permute-start.10) | collective-permute-done | bytes 40992 | tf_op jit(solution)/shard_map/ppermute | solution.py:21
  37.3 0.6 %collective-permute-start.11 = (f32[80,128]{1,0:T(8,128)S(1)}, f32[80,128]{1,0:T(8,128)S(1)}, u32[]{:S(2)}, u32[]{:S(2)}) collective-permute-start(f32[80,128]{1,0:T(8,128)S(1)} %add.28.conn_ref), channel_id=1, source_target_pairs={{0,16},{1,17},{2,18},{3,19},{4,20},{5,21},{6,22},{7,23},{8,24},{9,... | collective-permute-start | bytes 122888 | tf_op jit(solution)/shard_map/ppermute | solution.py:21
  37.9 4.3 %collective-permute-done.11.other_ref = f32[80,128]{1,0:T(8,128)S(1)} collective-permute-done((f32[80,128]{1,0:T(8,128)S(1)}, f32[80,128]{1,0:T(8,128)S(1)}, u32[]{:S(2)}, u32[]{:S(2)}) %collective-permute-start.11) | collective-permute-done | bytes 40992 | tf_op jit(solution)/shard_map/ppermute | solution.py:21
  42.2 0.0 copy-done.1
  42.2 1.5 %histogram.1 = (f32[20,128]{1,0:T(8,128)S(1)}, f32[20,128]{1,0:T(8,128)S(1)}) custom-call(s32[20]{0:T(128)S(1)} %copy-done.1, s32[1]{0:T(128)} %bitcast.slot_ref, f32[80,128]{1,0:T(8,128)S(1)} %add.28.conn_ref, f32[80,128]{1,0:T(8,128)S(1)} %collective-permute-done.11.other_ref), custom_call_target="tpu_custom_call" | custom-call | tf_op jit(solution)/shard_map/histogram/pallas_call | solution.py:162
  43.7 0.1 collective-permute-start.12
  43.8 3.7 %collective-permute-done.12 = f32[20,128]{1,0:T(8,128)S(1)} collective-permute-done((f32[20,128]{1,0:T(8,128)S(1)}, f32[20,128]{1,0:T(8,128)S(1)}, u32[]{:S(2)}, u32[]{:S(2)}) %collective-permute-start.12) | collective-permute-done | bytes 10272 | tf_op jit(solution)/shard_map/ppermute | solution.py:21
  47.5 1.4 %collective-permute-start.13 = (f32[20,128]{1,0:T(8,128)S(1)}, f32[20,128]{1,0:T(8,128)S(1)}, u32[]{:S(2)}, u32[]{:S(2)}) collective-permute-start(f32[20,128]{1,0:T(8,128)S(1)} %add.29), channel_id=1, source_target_pairs={{0,4},{1,5},{2,6},{3,7},{4,0},{5,1},{6,2},{7,3},{8,12},{9,13},{10,... | collective-permute-start | bytes 30728 | tf_op jit(solution)/shard_map/ppermute | solution.py:21
  48.9 2.3 %collective-permute-done.13 = f32[20,128]{1,0:T(8,128)S(1)} collective-permute-done((f32[20,128]{1,0:T(8,128)S(1)}, f32[20,128]{1,0:T(8,128)S(1)}, u32[]{:S(2)}, u32[]{:S(2)}) %collective-permute-start.13) | collective-permute-done | bytes 10272 | tf_op jit(solution)/shard_map/ppermute | solution.py:21
  51.2 0.0 collective-permute-start.14
  51.2 0.6 %copy.5 = f32[128,20]{0,1:T(8,128)} copy(f32[128,20]{0,1:T(8,128)S(1)} %bitcast.2) | data formatting | bytes 20480
  51.8 0.6 %collective-permute-done.14.other_ref = f32[20,128]{1,0:T(8,128)S(1)} collective-permute-done((f32[20,128]{1,0:T(8,128)S(1)}, f32[20,128]{1,0:T(8,128)S(1)}, u32[]{:S(2)}, u32[]{:S(2)}) %collective-permute-start.14) | collective-permute-done | bytes 10272 | tf_op jit(solution)/shard_map/ppermute | solution.py:21
  52.3 0.7 %scale_free_fit.1 = (f32[20]{0:T(128)}, f32[20]{0:T(128)}) custom-call(f32[20,128]{1,0:T(8,128)S(1)} %add.30.hist_ref, f32[20,128]{1,0:T(8,128)S(1)} %collective-permute-done.14.other_ref), custom_call_target="tpu_custom_call" | custom-call | tf_op jit(solution)/shard_map/scale_free_fit/pallas_call | solution.py:203
  (3 shorter events, 0.0 us)
Async XLA Ops:
  0.6 15.1 %collective-permute-start.2 = (bf16[128,1024]{1,0:T(8,128)(2,1)}, bf16[128,1024]{1,0:T(8,128)(2,1)S(1)}, u32[]{:S(2)}, u32[]{:S(2)}) collective-permute-start(bf16[128,1024]{1,0:T(8,128)(2,1)} %refs_1_.3), channel_id=1, source_target_pairs={{0,8},{1,9},{2,10},{3,11},{4,12},{5,13},{6,14},{7,15},{8,0},{9,1},... | collective-permute-start | bytes 786440 | tf_op jit(solution)/shard_map/ppermute | solution.py:21
  3.7 15.2 %collective-permute-start = (bf16[128,1024]{1,0:T(8,128)(2,1)}, bf16[128,1024]{1,0:T(8,128)(2,1)S(1)}, u32[]{:S(2)}, u32[]{:S(2)}) collective-permute-start(bf16[128,1024]{1,0:T(8,128)(2,1)} %refs_1_.3), channel_id=1, source_target_pairs={{0,16},{1,17},{2,18},{3,19},{4,20},{5,21},{6,22},{7,23},{8,24},{9,... | collective-permute-start | bytes 786440 | tf_op jit(solution)/shard_map/ppermute | solution.py:21
  6.3 13.1 %collective-permute-start.3 = (bf16[128,1024]{1,0:T(8,128)(2,1)}, bf16[128,1024]{1,0:T(8,128)(2,1)S(1)}, u32[]{:S(2)}, u32[]{:S(2)}) collective-permute-start(bf16[128,1024]{1,0:T(8,128)(2,1)} %refs_1_.3), channel_id=1, source_target_pairs={{0,4},{1,5},{2,6},{3,7},{4,0},{5,1},{6,2},{7,3},{8,12},{9,13},{10,... | collective-permute-start | bytes 786440 | tf_op jit(solution)/shard_map/ppermute | solution.py:21
  15.7 7.5 %collective-permute-start.4 = (bf16[128,1024]{1,0:T(8,128)(2,1)S(1)}, bf16[128,1024]{1,0:T(8,128)(2,1)S(1)}, u32[]{:S(2)}, u32[]{:S(2)}) collective-permute-start(bf16[128,1024]{1,0:T(8,128)(2,1)S(1)} %collective-permute-done.2.refs_4_.refs_2_), channel_id=1, source_target_pairs={{0,4},{1,5},{2,6},{3,7},{4,0},{5,1},{6,2},{7,3},{8,12},{9,13},{10,... | collective-permute-start | bytes 786440 | tf_op jit(solution)/shard_map/ppermute | solution.py:21
  17.4 7.1 %collective-permute-start.9 = (bf16[128,1024]{1,0:T(8,128)(2,1)}, bf16[128,1024]{1,0:T(8,128)(2,1)S(1)}, u32[]{:S(2)}, u32[]{:S(2)}) collective-permute-start(bf16[128,1024]{1,0:T(8,128)(2,1)} %refs_1_.3), channel_id=1, source_target_pairs={{0,2},{1,3},{2,0},{3,1},{4,6},{5,7},{6,4},{7,5},{8,10},{9,11},{10,... | collective-permute-start | bytes 786440 | tf_op jit(solution)/shard_map/ppermute | solution.py:21
  18.9 8.9 %collective-permute-start.5 = (bf16[128,1024]{1,0:T(8,128)(2,1)}, bf16[128,1024]{1,0:T(8,128)(2,1)S(1)}, u32[]{:S(2)}, u32[]{:S(2)}) collective-permute-start(bf16[128,1024]{1,0:T(8,128)(2,1)} %refs_1_.3), channel_id=1, source_target_pairs={{0,1},{1,0},{2,3},{3,2},{4,5},{5,4},{6,7},{7,6},{8,9},{9,8},{10,11... | collective-permute-start | bytes 786440 | tf_op jit(solution)/shard_map/ppermute | solution.py:21
  18.9 9.8 %collective-permute-start.6 = (bf16[128,1024]{1,0:T(8,128)(2,1)S(1)}, bf16[128,1024]{1,0:T(8,128)(2,1)S(1)}, u32[]{:S(2)}, u32[]{:S(2)}) collective-permute-start(bf16[128,1024]{1,0:T(8,128)(2,1)S(1)} %collective-permute-done.2.refs_4_.refs_2_), channel_id=1, source_target_pairs={{0,1},{1,0},{2,3},{3,2},{4,5},{5,4},{6,7},{7,6},{8,9},{9,8},{10,11... | collective-permute-start | bytes 786440 | tf_op jit(solution)/shard_map/ppermute | solution.py:21
  19.4 9.3 %collective-permute-start.7 = (bf16[128,1024]{1,0:T(8,128)(2,1)S(1)}, bf16[128,1024]{1,0:T(8,128)(2,1)S(1)}, u32[]{:S(2)}, u32[]{:S(2)}) collective-permute-start(bf16[128,1024]{1,0:T(8,128)(2,1)S(1)} %collective-permute-done.3.refs_4_.refs_3_), channel_id=1, source_target_pairs={{0,1},{1,0},{2,3},{3,2},{4,5},{5,4},{6,7},{7,6},{8,9},{9,8},{10,11... | collective-permute-start | bytes 786440 | tf_op jit(solution)/shard_map/ppermute | solution.py:21
  23.2 6.9 %collective-permute-start.8 = (bf16[128,1024]{1,0:T(8,128)(2,1)S(1)}, bf16[128,1024]{1,0:T(8,128)(2,1)S(1)}, u32[]{:S(2)}, u32[]{:S(2)}) collective-permute-start(bf16[128,1024]{1,0:T(8,128)(2,1)S(1)} %collective-permute-done.4.refs_3_.refs_4_), channel_id=1, source_target_pairs={{0,1},{1,0},{2,3},{3,2},{4,5},{5,4},{6,7},{7,6},{8,9},{9,8},{10,11... | collective-permute-start | bytes 786440 | tf_op jit(solution)/shard_map/ppermute | solution.py:21
  24.6 7.4 %collective-permute-start.1 = (bf16[128,1024]{1,0:T(8,128)(2,1)S(1)}, bf16[128,1024]{1,0:T(8,128)(2,1)S(1)}, u32[]{:S(2)}, u32[]{:S(2)}) collective-permute-start(bf16[128,1024]{1,0:T(8,128)(2,1)S(1)} %collective-permute-done.refs_2_.refs_1_), channel_id=1, source_target_pairs={{0,2},{1,3},{2,0},{3,1},{4,6},{5,7},{6,4},{7,5},{8,10},{9,11},{10,... | collective-permute-start | bytes 786440 | tf_op jit(solution)/shard_map/ppermute | solution.py:21
  26.0 0.9 %copy-start = (bf16[128,1024]{1,0:T(8,128)(2,1)S(1)}, bf16[128,1024]{1,0:T(8,128)(2,1)}, u32[]{:S(2)}) copy-start(bf16[128,1024]{1,0:T(8,128)(2,1)} %refs_1_.3) | copy-start | bytes 786436
  33.2 9.0 %copy-start.1 = (s32[20]{0:T(128)S(1)}, s32[20]{0:T(128)}, u32[]{:S(2)}) copy-start(s32[20]{0:T(128)} %power_ref.1) | copy-start | bytes 244
  33.3 4.1 %collective-permute-start.10 = (f32[80,128]{1,0:T(8,128)S(1)}, f32[80,128]{1,0:T(8,128)S(1)}, u32[]{:S(2)}, u32[]{:S(2)}) collective-permute-start(f32[80,128]{1,0:T(8,128)S(1)} %last_sums.1), channel_id=1, source_target_pairs={{0,2},{1,3},{2,0},{3,1},{4,6},{5,7},{6,4},{7,5},{8,10},{9,11},{10,... | collective-permute-start | bytes 122888 | tf_op jit(solution)/shard_map/ppermute | solution.py:21
  37.3 4.9 %collective-permute-start.11 = (f32[80,128]{1,0:T(8,128)S(1)}, f32[80,128]{1,0:T(8,128)S(1)}, u32[]{:S(2)}, u32[]{:S(2)}) collective-permute-start(f32[80,128]{1,0:T(8,128)S(1)} %add.28.conn_ref), channel_id=1, source_target_pairs={{0,16},{1,17},{2,18},{3,19},{4,20},{5,21},{6,22},{7,23},{8,24},{9,... | collective-permute-start | bytes 122888 | tf_op jit(solution)/shard_map/ppermute | solution.py:21
  43.7 3.7 %collective-permute-start.12 = (f32[20,128]{1,0:T(8,128)S(1)}, f32[20,128]{1,0:T(8,128)S(1)}, u32[]{:S(2)}, u32[]{:S(2)}) collective-permute-start(f32[20,128]{1,0:T(8,128)S(1)} %get-tuple-element.8), channel_id=1, source_target_pairs={{0,8},{1,9},{2,10},{3,11},{4,12},{5,13},{6,14},{7,15},{8,0},{9,1},... | collective-permute-start | bytes 30728 | tf_op jit(solution)/shard_map/ppermute | solution.py:21
  47.5 3.7 %collective-permute-start.13 = (f32[20,128]{1,0:T(8,128)S(1)}, f32[20,128]{1,0:T(8,128)S(1)}, u32[]{:S(2)}, u32[]{:S(2)}) collective-permute-start(f32[20,128]{1,0:T(8,128)S(1)} %add.29), channel_id=1, source_target_pairs={{0,4},{1,5},{2,6},{3,7},{4,0},{5,1},{6,2},{7,3},{8,12},{9,13},{10,... | collective-permute-start | bytes 30728 | tf_op jit(solution)/shard_map/ppermute | solution.py:21
  51.2 1.2 %collective-permute-start.14 = (f32[20,128]{1,0:T(8,128)S(1)}, f32[20,128]{1,0:T(8,128)S(1)}, u32[]{:S(2)}, u32[]{:S(2)}) collective-permute-start(f32[20,128]{1,0:T(8,128)S(1)} %add.30.hist_ref), channel_id=1, source_target_pairs={{0,1},{1,0},{2,3},{3,2},{4,5},{5,4},{6,7},{7,6},{8,9},{9,8},{10,11... | collective-permute-start | bytes 30728 | tf_op jit(solution)/shard_map/ppermute | solution.py:21
where the time goes:
time: 53.2 us; the launch traced here: 53 us
  waiting for transfers between devices  27.3 us (51%)
  starting transfers between devices  16 us (30%)
  Pallas kernels  7.45 us (14%)
  local copies, waits for them, and re-layouts  1.56 us (3%)
  between operations  0.73 us (1%)
    ppermute x15, waiting for transfers between devices, swap(): return lax.ppermute(x, AXES, [(i, i ^ mask) for i in range(count)])  27.3 us
    ppermute x15, starting transfers between devices, swap(): return lax.ppermute(x, AXES, [(i, i ^ mask) for i in range(count)])  16 us
    pallas_call x5, Pallas kernels, power_sums(): pl.pallas_call(functools.partial(power_kernel, len(panels)), out_shape=ja...  3.97 us
    unnamed x5, local copies, waits for them, and re-layouts  1.56 us
    pallas_call x1, Pallas kernels, histogram(): pl.pallas_call(functools.partial(hist_kernel, scale), out_shape=(pltpu.VM...  1.49 us
    pallas_call x1, Pallas kernels, last_sums(): pl.pallas_call(functools.partial(last_kernel, len(panels), len(partners),...  1.3 us
  transfers between devices with their start and end apart: 15, of which 9 were waited for; matrix products, arithmetic and copies ran while one was open for 1% of the time, Pallas kernels for 7%

commit v1 on v0

--- a/solution.py
+++ b/solution.py
@@ -31,8 +31,10 @@
 
 def plan(rows, cols):
     row_masks = [cols << i for i in range(rows.bit_length() - 1)]
-    col_masks = [1 << i for i in range(cols.bit_length() - 1)]
-    return [row_masks[-1]] + col_masks[1:], row_masks[-2::-1] + col_masks[:1]
+    core, *col_masks = [1 << i for i in range(cols.bit_length() - 1)]
+    panel_masks = [row_masks[-1]] + col_masks
+    partner_masks = row_masks[-2::-1] + [core]
+    return panel_masks, partner_masks
 
 
 def in_vmem(x):
@@ -146,12 +148,13 @@
     for t in range(powers):
         first = power_ref[t] * slots
         log_ref[pl.ds(t, 1), :] = logs[pl.ds(first + mine, 1), :]
-        weights = pair_sum(
+        away = pair_sum(
             [
-                jnp.maximum(0.0, 1.0 - jnp.abs(places[pl.ds(first + m, 1), :] - levels))
+                jnp.minimum(jnp.abs(places[pl.ds(first + m, 1), :] - levels), 1.0)
                 for m in range(slots)
             ]
         )
+        weights = slots - away
         table = jnp.where(lane == t, jnp.sum(weights, axis=1, keepdims=True), table)
     hist_ref[...] = table.T[:powers]
 
@@ -222,11 +225,11 @@
     partner = spread(expression, partner_masks, count)
     panel = spread(expression, panel_masks, count)
     keys = list(panel)
-    front = [k for k in keys if not k & far] + [far]
+    front = [k for k in keys if not k & far & ~core] + [far]
     rear = [k for k in keys if k not in front]
 
     index = lax.axis_index(AXES)
-    slot = sum(((index // mask) % 2) << i for i, mask in enumerate(panel_masks))
+    slot = sum(((index // (mask & ~core)) % 2) << i for i, mask in enumerate(panel_masks))
     slot = jnp.reshape(slot, (1,)).astype(jnp.int32)
 
     relayed = [k for k in partner if bin(k & ~core).count("1") > 1]
@@ -235,7 +238,8 @@
         (front, [core] + sides),
         (front[1:], [0]),
         (front, [k ^ core for k in sides] + [low, low ^ core]),
-        (front, relayed),
+        (front, [k for k in relayed if not k & core]),
+        (front, [k for k in relayed if k & core]),
     ]
     done = []
     parts = {k: [] for k in keys}
@@ -264,7 +268,7 @@
         power_order, slot, conn, swap(conn, far, count), (BINS - 1) / log_total
     )
     for mask in partner_masks[:-1]:
-        hist = hist + swap(hist, mask, count)
+        hist = hist + swap(hist, (mask & ~core) ^ core, count)
     fit, slope = scale_free_fit(hist, swap(hist, core, count), log_total)
     return (log_conn.T, fit, slope)
 

time: 53.2 us -> 52 us (0.977)
  starting transfers between devices: 16 us -> 14.6 us
    ppermute x15, starting transfers between devices: 16 us -> 14.6 us  [swap(): return lax.ppermute(x, AXES, [(i, i ^ mask) for i in range(count)])]
    pallas_call x5 -> x6, Pallas kernels: 3.97 us -> 4.34 us  [power_sums(): pl.pallas_call(functools.partial(power_kernel, len(panels)), out_shape=ja...]
  transfers between devices with their start and end apart: 15 -> 15, of which waited for: 9 -> 9; matrix products, arithmetic and copies ran while one was open for 1% -> 1% of each run, Pallas kernels for 7% -> 8%
where the time goes in v1:
time: 52 us; the launch traced here: 51.9 us
  waiting for transfers between devices  27.2 us (52%)
  starting transfers between devices  14.6 us (28%)
  Pallas kernels  7.69 us (15%)
  local copies, waits for them, and re-layouts  1.55 us (3%)
  between operations  0.75 us (1%)
    ppermute x15, waiting for transfers between devices, swap(): return lax.ppermute(x, AXES, [(i, i ^ mask) for i in range(count)])  27.2 us
    ppermute x15, starting transfers between devices, swap(): return lax.ppermute(x, AXES, [(i, i ^ mask) for i in range(count)])  14.6 us
    pallas_call x6, Pallas kernels, power_sums(): pl.pallas_call(functools.partial(power_kernel, len(panels)), out_shape=ja...  4.34 us
    unnamed x5, local copies, waits for them, and re-layouts  1.55 us
    pallas_call x1, Pallas kernels, histogram(): pl.pallas_call(functools.partial(hist_kernel, scale), out_shape=(pltpu.VM...  1.36 us
    pallas_call x1, Pallas kernels, last_sums(): pl.pallas_call(functools.partial(last_kernel, len(panels), len(partners),...  1.3 us
  transfers between devices with their start and end apart: 15, of which 9 were waited for; matrix products, arithmetic and copies ran while one was open for 1% of the time, Pallas kernels for 8%

profile of v1, /device:TPU:0, one launch (start us, length us, event | category | flops | bytes accessed | tf_op | source)
XLA Modules:
  0.0 51.9 jit_solution(13064935552123922827)
XLA Ops:
  0.6 3.1 %collective-permute-start.2 = (bf16[128,1024]{1,0:T(8,128)(2,1)}, bf16[128,1024]{1,0:T(8,128)(2,1)S(1)}, u32[]{:S(2)}, u32[]{:S(2)}) collective-permute-start(bf16[128,1024]{1,0:T(8,128)(2,1)} %refs_1_.3), channel_id=1, source_target_pairs={{0,8},{1,9},{2,10},{3,11},{4,12},{5,13},{6,14},{7,15},{8,0},{9,1},... | collective-permute-start | bytes 786440 | tf_op jit(solution)/shard_map/ppermute | solution.py:21
  3.7 2.6 %collective-permute-start = (bf16[128,1024]{1,0:T(8,128)(2,1)}, bf16[128,1024]{1,0:T(8,128)(2,1)S(1)}, u32[]{:S(2)}, u32[]{:S(2)}) collective-permute-start(bf16[128,1024]{1,0:T(8,128)(2,1)} %refs_1_.3), channel_id=1, source_target_pairs={{0,16},{1,17},{2,18},{3,19},{4,20},{5,21},{6,22},{7,23},{8,24},{9,... | collective-permute-start | bytes 786440 | tf_op jit(solution)/shard_map/ppermute | solution.py:21
  6.3 1.5 %collective-permute-start.3 = (bf16[128,1024]{1,0:T(8,128)(2,1)}, bf16[128,1024]{1,0:T(8,128)(2,1)S(1)}, u32[]{:S(2)}, u32[]{:S(2)}) collective-permute-start(bf16[128,1024]{1,0:T(8,128)(2,1)} %refs_1_.3), channel_id=1, source_target_pairs={{0,4},{1,5},{2,6},{3,7},{4,0},{5,1},{6,2},{7,3},{8,12},{9,13},{10,... | collective-permute-start | bytes 786440 | tf_op jit(solution)/shard_map/ppermute | solution.py:21
  7.9 7.9 %collective-permute-done.2.refs_4_.refs_2_ = bf16[128,1024]{1,0:T(8,128)(2,1)S(1)} collective-permute-done((bf16[128,1024]{1,0:T(8,128)(2,1)}, bf16[128,1024]{1,0:T(8,128)(2,1)S(1)}, u32[]{:S(2)}, u32[]{:S(2)}) %collective-permute-start.2) | collective-permute-done | bytes 262176 | tf_op jit(solution)/shard_map/ppermute | solution.py:21
  15.7 1.7 %collective-permute-start.4 = (bf16[128,1024]{1,0:T(8,128)(2,1)S(1)}, bf16[128,1024]{1,0:T(8,128)(2,1)S(1)}, u32[]{:S(2)}, u32[]{:S(2)}) collective-permute-start(bf16[128,1024]{1,0:T(8,128)(2,1)S(1)} %collective-permute-done.2.refs_4_.refs_2_), channel_id=1, source_target_pairs={{0,4},{1,5},{2,6},{3,7},{4,0},{5,1},{6,2},{7,3},{8,12},{9,13},{10,... | collective-permute-start | bytes 786440 | tf_op jit(solution)/shard_map/ppermute | solution.py:21
  17.4 1.5 %collective-permute-start.9 = (bf16[128,1024]{1,0:T(8,128)(2,1)}, bf16[128,1024]{1,0:T(8,128)(2,1)S(1)}, u32[]{:S(2)}, u32[]{:S(2)}) collective-permute-start(bf16[128,1024]{1,0:T(8,128)(2,1)} %refs_1_.3), channel_id=1, source_target_pairs={{0,2},{1,3},{2,0},{3,1},{4,6},{5,7},{6,4},{7,5},{8,10},{9,11},{10,... | collective-permute-start | bytes 786440 | tf_op jit(solution)/shard_map/ppermute | solution.py:21
  18.9 0.0 collective-permute-start.5
  18.9 0.0 collective-permute-done.refs_2_.refs_1_
  18.9 0.5 collective-permute-start.6
  19.4 0.0 collective-permute-done.3.refs_4_.refs_3_
  19.4 0.1 collective-permute-start.7
  19.5 3.7 %collective-permute-done.4.refs_3_.refs_4_ = bf16[128,1024]{1,0:T(8,128)(2,1)S(1)} collective-permute-done((bf16[128,1024]{1,0:T(8,128)(2,1)S(1)}, bf16[128,1024]{1,0:T(8,128)(2,1)S(1)}, u32[]{:S(2)}, u32[]{:S(2)}) %collective-permute-start.4) | collective-permute-done | bytes 262176 | tf_op jit(solution)/shard_map/ppermute | solution.py:21
  23.2 0.0 collective-permute-start.8
  23.2 1.3 %collective-permute-done.9.refs_1_.refs_0_ = bf16[128,1024]{1,0:T(8,128)(2,1)S(1)} collective-permute-done((bf16[128,1024]{1,0:T(8,128)(2,1)}, bf16[128,1024]{1,0:T(8,128)(2,1)S(1)}, u32[]{:S(2)}, u32[]{:S(2)}) %collective-permute-start.9) | collective-permute-done | bytes 262176 | tf_op jit(solution)/shard_map/ppermute | solution.py:21
  24.6 1.5 %collective-permute-start.1 = (bf16[128,1024]{1,0:T(8,128)(2,1)S(1)}, bf16[128,1024]{1,0:T(8,128)(2,1)S(1)}, u32[]{:S(2)}, u32[]{:S(2)}) collective-permute-start(bf16[128,1024]{1,0:T(8,128)(2,1)S(1)} %collective-permute-done.refs_2_.refs_1_), channel_id=1, source_target_pairs={{0,2},{1,3},{2,0},{3,1},{4,6},{5,7},{6,4},{7,5},{8,10},{9,11},{10,... | collective-permute-start | bytes 786440 | tf_op jit(solution)/shard_map/ppermute | solution.py:21
  26.0 0.0 copy-start
  26.0 0.9 %copy-done = bf16[128,1024]{1,0:T(8,128)(2,1)S(1)} copy-done((bf16[128,1024]{1,0:T(8,128)(2,1)S(1)}, bf16[128,1024]{1,0:T(8,128)(2,1)}, u32[]{:S(2)}) %copy-start) | copy-done | bytes 262168
  27.0 0.3 power_sums.6.refs_9_
  27.3 0.5 power_sums.8.refs_11_
  27.8 0.0 collective-permute-done.5.refs_3_.refs_5_
  27.8 0.9 %power_sums.7.refs_10_ = f32[3,20,128]{2,1,0:T(8,128)S(1)} custom-call(bf16[128,1024]{1,0:T(8,128)(2,1)S(1)} %copy-done, bf16[128,1024]{1,0:T(8,128)(2,1)S(1)} %collective-permute-done.9.refs_1_.refs_0_, bf16[128,1024]{1,0:T(8,128)(2,1)S(1)} %collective-permute-done.refs_2_.refs_1_, bf16[128,1024]{1,0:T(8,128)(2,1)S(1)} %collective-permute-done.5.refs_3_.refs_5_, ...), custom_call_target="tpu_custom_call" | custom-call | flops 201326592 | tf_op jit(solution)/shard_map/power_sums/pallas_call | solution.py:93
  28.8 0.7 %power_sums.10.refs_13_ = f32[3,20,128]{2,1,0:T(8,128)S(1)} custom-call(bf16[128,1024]{1,0:T(8,128)(2,1)S(1)} %copy-done, bf16[128,1024]{1,0:T(8,128)(2,1)S(1)} %collective-permute-done.9.refs_1_.refs_0_, bf16[128,1024]{1,0:T(8,128)(2,1)S(1)} %collective-permute-done.refs_2_.refs_1_, bf16[128,1024]{1,0:T(8,128)(2,1)S(1)} %collective-permute-done.4.refs_3_.refs_4_), custom_call_target="tpu_custom_call" | custom-call | flops 100663296 | tf_op jit(solution)/shard_map/power_sums/pallas_call | solution.py:93
  29.4 0.0 collective-permute-done.6.refs_5_.refs_6_
  29.4 0.0 collective-permute-done.7.refs_3_.refs_7_
  29.4 1.3 %power_sums.9.refs_12_ = f32[3,20,128]{2,1,0:T(8,128)S(1)} custom-call(bf16[128,1024]{1,0:T(8,128)(2,1)S(1)} %copy-done, bf16[128,1024]{1,0:T(8,128)(2,1)S(1)} %collective-permute-done.9.refs_1_.refs_0_, bf16[128,1024]{1,0:T(8,128)(2,1)S(1)} %collective-permute-done.refs_2_.refs_1_, bf16[128,1024]{1,0:T(8,128)(2,1)S(1)} %collective-permute-done.7.refs_3_.refs_7_, ...), custom_call_target="tpu_custom_call" | custom-call | flops 301989888 | tf_op jit(solution)/shard_map/power_sums/pallas_call | solution.py:93
  30.7 0.0 collective-permute-done.8.refs_3_.refs_8_
  30.8 0.7 %power_sums.11.refs_14_ = f32[3,20,128]{2,1,0:T(8,128)S(1)} custom-call(bf16[128,1024]{1,0:T(8,128)(2,1)S(1)} %copy-done, bf16[128,1024]{1,0:T(8,128)(2,1)S(1)} %collective-permute-done.9.refs_1_.refs_0_, bf16[128,1024]{1,0:T(8,128)(2,1)S(1)} %collective-permute-done.refs_2_.refs_1_, bf16[128,1024]{1,0:T(8,128)(2,1)S(1)} %collective-permute-done.8.refs_3_.refs_8_), custom_call_target="tpu_custom_call" | custom-call | flops 100663296 | tf_op jit(solution)/shard_map/power_sums/pallas_call | solution.py:93
  31.4 0.5 %collective-permute-done.1.refs_0_ = bf16[128,1024]{1,0:T(8,128)(2,1)S(1)} collective-permute-done((bf16[128,1024]{1,0:T(8,128)(2,1)S(1)}, bf16[128,1024]{1,0:T(8,128)(2,1)S(1)}, u32[]{:S(2)}, u32[]{:S(2)}) %collective-permute-start.1) | collective-permute-done | bytes 262176 | tf_op jit(solution)/shard_map/ppermute | solution.py:21
  31.9 1.3 %last_sums.1 = f32[80,128]{1,0:T(8,128)S(1)} custom-call(s32[1]{0:T(128)} %bitcast.slot_ref, bf16[128,1024]{1,0:T(8,128)(2,1)S(1)} %collective-permute-done.1.refs_0_, bf16[128,1024]{1,0:T(8,128)(2,1)S(1)} %copy-done, bf16[128,1024]{1,0:T(8,128)(2,1)S(1)} %collective-permute-done.2.refs_4_.refs_2_, ...), custom_call_target="tpu_custom_call" | custom-call | flops 268435456 | tf_op jit(solution)/shard_map/last_sums/pallas_call | solution.py:126
  33.2 0.0 copy-start.1
  33.3 1.5 %collective-permute-start.10 = (f32[80,128]{1,0:T(8,128)S(1)}, f32[80,128]{1,0:T(8,128)S(1)}, u32[]{:S(2)}, u32[]{:S(2)}) collective-permute-start(f32[80,128]{1,0:T(8,128)S(1)} %last_sums.1), channel_id=1, source_target_pairs={{0,2},{1,3},{2,0},{3,1},{4,6},{5,7},{6,4},{7,5},{8,10},{9,11},{10,... | collective-permute-start | bytes 122888 | tf_op jit(solution)/shard_map/ppermute | solution.py:21
  34.7 2.6 %collective-permute-done.10 = f32[80,128]{1,0:T(8,128)S(1)} collective-permute-done((f32[80,128]{1,0:T(8,128)S(1)}, f32[80,128]{1,0:T(8,128)S(1)}, u32[]{:S(2)}, u32[]{:S(2)}) %collective-permute-start.10) | collective-permute-done | bytes 40992 | tf_op jit(solution)/shard_map/ppermute | solution.py:21
  37.3 0.6 %collective-permute-start.11 = (f32[80,128]{1,0:T(8,128)S(1)}, f32[80,128]{1,0:T(8,128)S(1)}, u32[]{:S(2)}, u32[]{:S(2)}) collective-permute-start(f32[80,128]{1,0:T(8,128)S(1)} %add.28.conn_ref), channel_id=1, source_target_pairs={{0,16},{1,17},{2,18},{3,19},{4,20},{5,21},{6,22},{7,23},{8,24},{9,... | collective-permute-start | bytes 122888 | tf_op jit(solution)/shard_map/ppermute | solution.py:21
  37.9 4.3 %collective-permute-done.11.other_ref = f32[80,128]{1,0:T(8,128)S(1)} collective-permute-done((f32[80,128]{1,0:T(8,128)S(1)}, f32[80,128]{1,0:T(8,128)S(1)}, u32[]{:S(2)}, u32[]{:S(2)}) %collective-permute-start.11) | collective-permute-done | bytes 40992 | tf_op jit(solution)/shard_map/ppermute | solution.py:21
  42.2 0.0 copy-done.1
  42.2 1.4 %histogram.1 = (f32[20,128]{1,0:T(8,128)S(1)}, f32[20,128]{1,0:T(8,128)S(1)}) custom-call(s32[20]{0:T(128)S(1)} %copy-done.1, s32[1]{0:T(128)} %bitcast.slot_ref, f32[80,128]{1,0:T(8,128)S(1)} %add.28.conn_ref, f32[80,128]{1,0:T(8,128)S(1)} %collective-permute-done.11.other_ref), custom_call_target="tpu_custom_call" | custom-call | tf_op jit(solution)/shard_map/histogram/pallas_call | solution.py:165
  43.6 0.0 collective-permute-start.12
  43.6 3.1 %collective-permute-done.12 = f32[20,128]{1,0:T(8,128)S(1)} collective-permute-done((f32[20,128]{1,0:T(8,128)S(1)}, f32[20,128]{1,0:T(8,128)S(1)}, u32[]{:S(2)}, u32[]{:S(2)}) %collective-permute-start.12) | collective-permute-done | bytes 10272 | tf_op jit(solution)/shard_map/ppermute | solution.py:21
  46.8 0.0 collective-permute-start.13
  46.8 3.2 %collective-permute-done.13 = f32[20,128]{1,0:T(8,128)S(1)} collective-permute-done((f32[20,128]{1,0:T(8,128)S(1)}, f32[20,128]{1,0:T(8,128)S(1)}, u32[]{:S(2)}, u32[]{:S(2)}) %collective-permute-start.13) | collective-permute-done | bytes 10272 | tf_op jit(solution)/shard_map/ppermute | solution.py:21
  50.0 0.1 collective-permute-start.14
  50.1 0.6 %copy.5 = f32[128,20]{0,1:T(8,128)} copy(f32[128,20]{0,1:T(8,128)S(1)} %bitcast.2) | data formatting | bytes 20480
  50.7 0.5 collective-permute-done.14.other_ref
  51.2 0.7 %scale_free_fit.1 = (f32[20]{0:T(128)}, f32[20]{0:T(128)}) custom-call(f32[20,128]{1,0:T(8,128)S(1)} %add.30.hist_ref, f32[20,128]{1,0:T(8,128)S(1)} %collective-permute-done.14.other_ref), custom_call_target="tpu_custom_call" | custom-call | tf_op jit(solution)/shard_map/scale_free_fit/pallas_call | solution.py:206
  (3 shorter events, 0.0 us)
Async XLA Ops:
  0.6 15.1 %collective-permute-start.2 = (bf16[128,1024]{1,0:T(8,128)(2,1)}, bf16[128,1024]{1,0:T(8,128)(2,1)S(1)}, u32[]{:S(2)}, u32[]{:S(2)}) collective-permute-start(bf16[128,1024]{1,0:T(8,128)(2,1)} %refs_1_.3), channel_id=1, source_target_pairs={{0,8},{1,9},{2,10},{3,11},{4,12},{5,13},{6,14},{7,15},{8,0},{9,1},... | collective-permute-start | bytes 786440 | tf_op jit(solution)/shard_map/ppermute | solution.py:21
  3.7 15.2 %collective-permute-start = (bf16[128,1024]{1,0:T(8,128)(2,1)}, bf16[128,1024]{1,0:T(8,128)(2,1)S(1)}, u32[]{:S(2)}, u32[]{:S(2)}) collective-permute-start(bf16[128,1024]{1,0:T(8,128)(2,1)} %refs_1_.3), channel_id=1, source_target_pairs={{0,16},{1,17},{2,18},{3,19},{4,20},{5,21},{6,22},{7,23},{8,24},{9,... | collective-permute-start | bytes 786440 | tf_op jit(solution)/shard_map/ppermute | solution.py:21
  6.3 13.1 %collective-permute-start.3 = (bf16[128,1024]{1,0:T(8,128)(2,1)}, bf16[128,1024]{1,0:T(8,128)(2,1)S(1)}, u32[]{:S(2)}, u32[]{:S(2)}) collective-permute-start(bf16[128,1024]{1,0:T(8,128)(2,1)} %refs_1_.3), channel_id=1, source_target_pairs={{0,4},{1,5},{2,6},{3,7},{4,0},{5,1},{6,2},{7,3},{8,12},{9,13},{10,... | collective-permute-start | bytes 786440 | tf_op jit(solution)/shard_map/ppermute | solution.py:21
  15.7 7.5 %collective-permute-start.4 = (bf16[128,1024]{1,0:T(8,128)(2,1)S(1)}, bf16[128,1024]{1,0:T(8,128)(2,1)S(1)}, u32[]{:S(2)}, u32[]{:S(2)}) collective-permute-start(bf16[128,1024]{1,0:T(8,128)(2,1)S(1)} %collective-permute-done.2.refs_4_.refs_2_), channel_id=1, source_target_pairs={{0,4},{1,5},{2,6},{3,7},{4,0},{5,1},{6,2},{7,3},{8,12},{9,13},{10,... | collective-permute-start | bytes 786440 | tf_op jit(solution)/shard_map/ppermute | solution.py:21
  17.4 7.1 %collective-permute-start.9 = (bf16[128,1024]{1,0:T(8,128)(2,1)}, bf16[128,1024]{1,0:T(8,128)(2,1)S(1)}, u32[]{:S(2)}, u32[]{:S(2)}) collective-permute-start(bf16[128,1024]{1,0:T(8,128)(2,1)} %refs_1_.3), channel_id=1, source_target_pairs={{0,2},{1,3},{2,0},{3,1},{4,6},{5,7},{6,4},{7,5},{8,10},{9,11},{10,... | collective-permute-start | bytes 786440 | tf_op jit(solution)/shard_map/ppermute | solution.py:21
  18.9 8.9 %collective-permute-start.5 = (bf16[128,1024]{1,0:T(8,128)(2,1)}, bf16[128,1024]{1,0:T(8,128)(2,1)S(1)}, u32[]{:S(2)}, u32[]{:S(2)}) collective-permute-start(bf16[128,1024]{1,0:T(8,128)(2,1)} %refs_1_.3), channel_id=1, source_target_pairs={{0,1},{1,0},{2,3},{3,2},{4,5},{5,4},{6,7},{7,6},{8,9},{9,8},{10,11... | collective-permute-start | bytes 786440 | tf_op jit(solution)/shard_map/ppermute | solution.py:21
  18.9 10.5 %collective-permute-start.6 = (bf16[128,1024]{1,0:T(8,128)(2,1)S(1)}, bf16[128,1024]{1,0:T(8,128)(2,1)S(1)}, u32[]{:S(2)}, u32[]{:S(2)}) collective-permute-start(bf16[128,1024]{1,0:T(8,128)(2,1)S(1)} %collective-permute-done.2.refs_4_.refs_2_), channel_id=1, source_target_pairs={{0,1},{1,0},{2,3},{3,2},{4,5},{5,4},{6,7},{7,6},{8,9},{9,8},{10,11... | collective-permute-start | bytes 786440 | tf_op jit(solution)/shard_map/ppermute | solution.py:21
  19.4 10.0 %collective-permute-start.7 = (bf16[128,1024]{1,0:T(8,128)(2,1)S(1)}, bf16[128,1024]{1,0:T(8,128)(2,1)S(1)}, u32[]{:S(2)}, u32[]{:S(2)}) collective-permute-start(bf16[128,1024]{1,0:T(8,128)(2,1)S(1)} %collective-permute-done.3.refs_4_.refs_3_), channel_id=1, source_target_pairs={{0,1},{1,0},{2,3},{3,2},{4,5},{5,4},{6,7},{7,6},{8,9},{9,8},{10,11... | collective-permute-start | bytes 786440 | tf_op jit(solution)/shard_map/ppermute | solution.py:21
  23.2 7.5 %collective-permute-start.8 = (bf16[128,1024]{1,0:T(8,128)(2,1)S(1)}, bf16[128,1024]{1,0:T(8,128)(2,1)S(1)}, u32[]{:S(2)}, u32[]{:S(2)}) collective-permute-start(bf16[128,1024]{1,0:T(8,128)(2,1)S(1)} %collective-permute-done.4.refs_3_.refs_4_), channel_id=1, source_target_pairs={{0,1},{1,0},{2,3},{3,2},{4,5},{5,4},{6,7},{7,6},{8,9},{9,8},{10,11... | collective-permute-start | bytes 786440 | tf_op jit(solution)/shard_map/ppermute | solution.py:21
  24.6 7.4 %collective-permute-start.1 = (bf16[128,1024]{1,0:T(8,128)(2,1)S(1)}, bf16[128,1024]{1,0:T(8,128)(2,1)S(1)}, u32[]{:S(2)}, u32[]{:S(2)}) collective-permute-start(bf16[128,1024]{1,0:T(8,128)(2,1)S(1)} %collective-permute-done.refs_2_.refs_1_), channel_id=1, source_target_pairs={{0,2},{1,3},{2,0},{3,1},{4,6},{5,7},{6,4},{7,5},{8,10},{9,11},{10,... | collective-permute-start | bytes 786440 | tf_op jit(solution)/shard_map/ppermute | solution.py:21
  26.0 0.9 %copy-start = (bf16[128,1024]{1,0:T(8,128)(2,1)S(1)}, bf16[128,1024]{1,0:T(8,128)(2,1)}, u32[]{:S(2)}) copy-start(bf16[128,1024]{1,0:T(8,128)(2,1)} %refs_1_.3) | copy-start | bytes 786436
  33.2 9.0 %copy-start.1 = (s32[20]{0:T(128)S(1)}, s32[20]{0:T(128)}, u32[]{:S(2)}) copy-start(s32[20]{0:T(128)} %power_ref.1) | copy-start | bytes 244
  33.3 4.1 %collective-permute-start.10 = (f32[80,128]{1,0:T(8,128)S(1)}, f32[80,128]{1,0:T(8,128)S(1)}, u32[]{:S(2)}, u32[]{:S(2)}) collective-permute-start(f32[80,128]{1,0:T(8,128)S(1)} %last_sums.1), channel_id=1, source_target_pairs={{0,2},{1,3},{2,0},{3,1},{4,6},{5,7},{6,4},{7,5},{8,10},{9,11},{10,... | collective-permute-start | bytes 122888 | tf_op jit(solution)/shard_map/ppermute | solution.py:21
  37.3 4.9 %collective-permute-start.11 = (f32[80,128]{1,0:T(8,128)S(1)}, f32[80,128]{1,0:T(8,128)S(1)}, u32[]{:S(2)}, u32[]{:S(2)}) collective-permute-start(f32[80,128]{1,0:T(8,128)S(1)} %add.28.conn_ref), channel_id=1, source_target_pairs={{0,16},{1,17},{2,18},{3,19},{4,20},{5,21},{6,22},{7,23},{8,24},{9,... | collective-permute-start | bytes 122888 | tf_op jit(solution)/shard_map/ppermute | solution.py:21
  43.6 3.2 %collective-permute-start.12 = (f32[20,128]{1,0:T(8,128)S(1)}, f32[20,128]{1,0:T(8,128)S(1)}, u32[]{:S(2)}, u32[]{:S(2)}) collective-permute-start(f32[20,128]{1,0:T(8,128)S(1)} %get-tuple-element.8), channel_id=1, source_target_pairs={{0,9},{1,8},{2,11},{3,10},{4,13},{5,12},{6,15},{7,14},{8,1},{9,0},... | collective-permute-start | bytes 30728 | tf_op jit(solution)/shard_map/ppermute | solution.py:21
  46.8 3.2 %collective-permute-start.13 = (f32[20,128]{1,0:T(8,128)S(1)}, f32[20,128]{1,0:T(8,128)S(1)}, u32[]{:S(2)}, u32[]{:S(2)}) collective-permute-start(f32[20,128]{1,0:T(8,128)S(1)} %add.29), channel_id=1, source_target_pairs={{0,5},{1,4},{2,7},{3,6},{4,1},{5,0},{6,3},{7,2},{8,13},{9,12},{10,... | collective-permute-start | bytes 30728 | tf_op jit(solution)/shard_map/ppermute | solution.py:21
  50.0 1.2 %collective-permute-start.14 = (f32[20,128]{1,0:T(8,128)S(1)}, f32[20,128]{1,0:T(8,128)S(1)}, u32[]{:S(2)}, u32[]{:S(2)}) collective-permute-start(f32[20,128]{1,0:T(8,128)S(1)} %add.30.hist_ref), channel_id=1, source_target_pairs={{0,1},{1,0},{2,3},{3,2},{4,5},{5,4},{6,7},{7,6},{8,9},{9,8},{10,11... | collective-permute-start | bytes 30728 | tf_op jit(solution)/shard_map/ppermute | solution.py:21

commit v2 on v1

--- a/solution.py
+++ b/solution.py
@@ -104,49 +104,66 @@
     return functools.reduce(jnp.add, outs)
 
 
-def last_kernel(n_panel, n_partner, parts, slot_ref, *refs):
-    part_refs = refs[n_panel + n_partner : -2]
-    conn_ref, total_ref = refs[-2:]
+def own_slot(panel_bits):
+    index = lax.axis_index("row") * lax.axis_size("col") + lax.axis_index("col")
+    return sum(((index // bit) % 2) << i for i, bit in enumerate(panel_bits))
+
+
+def last_kernel(panel_bits, n_panel, n_partner, parts, order_hbm, *refs):
+    part_refs = refs[n_panel + n_partner : -5]
+    conn_ref, total_ref, natural, order, arrived = refs[-5:]
     slots = len(parts)
     powers = total_ref.shape[1]
-    mine = slot_ref[0]
+    fetch = pltpu.make_async_copy(order_hbm, order, arrived)
+    fetch.start()
+    mine = own_slot(panel_bits)
     add_powers(refs[:n_panel], refs[n_panel : n_panel + n_partner], total_ref)
     for i, where in enumerate(parts):
-        slot = jnp.bitwise_xor(mine, i)
         values = [part_refs[a][b] for a, b in where if a is not None]
         values += [jnp.sum(total_ref[b], axis=1) for a, b in where if a is None]
-        value = functools.reduce(jnp.add, values)
-        for power in range(powers):
-            conn_ref[pl.ds(power * slots + slot, 1), :] = value[power : power + 1]
-
-
-def last_sums(slot, panels, partners, done, parts, powers):
+        natural[i] = functools.reduce(jnp.add, values)
+    fetch.wait()
+    for t in range(powers):
+        at = order[t]
+        for i in range(slots):
+            slot = jnp.bitwise_xor(mine, i)
+            conn_ref[pl.ds(t * slots + slot, 1), :] = natural[i, pl.ds(at, 1), :]
+
+
+def last_sums(panel_bits, power_order, panels, partners, done, parts):
     genes, samples = panels[0].shape
+    powers = power_order.shape[0]
     flops = len(panels) * len(partners) * genes * genes * 2 * samples
     return pl.pallas_call(
-        functools.partial(last_kernel, len(panels), len(partners), parts),
+        functools.partial(last_kernel, panel_bits, len(panels), len(partners), parts),
         out_shape=jax.ShapeDtypeStruct((powers * len(parts), genes), jnp.float32),
-        in_specs=[SMEM] + [VMEM] * (len(panels) + len(partners) + len(done)),
+        in_specs=[pl.BlockSpec(memory_space=pltpu.HBM)]
+        + [VMEM] * (len(panels) + len(partners) + len(done)),
         out_specs=VMEM,
-        scratch_shapes=[pltpu.VMEM((len(panels), powers, 8, genes), jnp.float32)],
+        scratch_shapes=[
+            pltpu.VMEM((len(panels), powers, 8, genes), jnp.float32),
+            pltpu.VMEM((len(parts), powers, genes), jnp.float32),
+            pltpu.SMEM((powers,), jnp.int32),
+            pltpu.SemaphoreType.DMA(()),
+        ],
         compiler_params=PARAMS,
         cost_estimate=pl.CostEstimate(flops=flops, bytes_accessed=0, transcendentals=0),
         name="last_sums",
-    )(slot, *map(in_vmem, panels), *map(in_vmem, partners), *map(in_vmem, done))
-
-
-def hist_kernel(scale, power_ref, slot_ref, conn_ref, other_ref, log_ref, hist_ref, logs, places):
+    )(power_order, *map(in_vmem, panels), *map(in_vmem, partners), *map(in_vmem, done))
+
+
+def hist_kernel(scale, panel_bits, conn_ref, other_ref, log_ref, hist_ref, logs, places):
     rows, genes = conn_ref.shape
     powers = log_ref.shape[0]
     slots = rows // powers
-    mine = slot_ref[0]
+    mine = own_slot(panel_bits)
     logs[...] = jnp.log(conn_ref[...] + other_ref[...])
     places[...] = logs[...] * scale
     levels = lax.broadcasted_iota(jnp.int32, (BINS, genes), 0).astype(jnp.float32)
     lane = lax.broadcasted_iota(jnp.int32, (BINS, BINS), 1)
     table = jnp.zeros((BINS, BINS), jnp.float32)
     for t in range(powers):
-        first = power_ref[t] * slots
+        first = t * slots
         log_ref[pl.ds(t, 1), :] = logs[pl.ds(first + mine, 1), :]
         away = pair_sum(
             [
@@ -154,26 +171,24 @@
                 for m in range(slots)
             ]
         )
-        weights = slots - away
-        table = jnp.where(lane == t, jnp.sum(weights, axis=1, keepdims=True), table)
+        table = jnp.where(lane == t, jnp.sum(slots - away, axis=1, keepdims=True), table)
     hist_ref[...] = table.T[:powers]
 
 
-def histogram(power_order, slot, conn, other, scale):
-    powers = power_order.shape[0]
+def histogram(panel_bits, powers, conn, other, scale):
     genes = conn.shape[1]
     return pl.pallas_call(
-        functools.partial(hist_kernel, scale),
+        functools.partial(hist_kernel, scale, panel_bits),
         out_shape=(
             pltpu.VMEM((powers, genes), jnp.float32),
             pltpu.VMEM((powers, BINS), jnp.float32),
         ),
-        in_specs=[SMEM, SMEM, VMEM, VMEM],
+        in_specs=[VMEM, VMEM],
         out_specs=(VMEM, VMEM),
         scratch_shapes=[pltpu.VMEM(conn.shape, jnp.float32)] * 2,
         compiler_params=PARAMS,
         name="histogram",
-    )(power_order, slot, in_vmem(conn), in_vmem(other))
+    )(in_vmem(conn), in_vmem(other))
 
 
 def fit_kernel(log_total, hist_ref, other_ref, fit_ref, slope_ref):
@@ -228,9 +243,7 @@
     front = [k for k in keys if not k & far & ~core] + [far]
     rear = [k for k in keys if k not in front]
 
-    index = lax.axis_index(AXES)
-    slot = sum(((index // (mask & ~core)) % 2) << i for i, mask in enumerate(panel_masks))
-    slot = jnp.reshape(slot, (1,)).astype(jnp.int32)
+    panel_bits = [mask & ~core for mask in panel_masks]
 
     relayed = [k for k in partner if bin(k & ~core).count("1") > 1]
     waves = [
@@ -254,18 +267,18 @@
     for i, k in enumerate(rear):
         parts[k] += [(len(done) - 1, i)] * bool(early) + [(None, i)]
     conn = last_sums(
-        slot,
+        panel_bits,
+        power_order,
         [panel[k] for k in rear],
         [partner[k] for k in late],
         done,
         [parts[k] for k in keys],
-        powers,
     )
 
     for mask in panel_masks[:0:-1]:
         conn = conn + swap(conn, mask, count)
     log_conn, hist = histogram(
-        power_order, slot, conn, swap(conn, far, count), (BINS - 1) / log_total
+        panel_bits, powers, conn, swap(conn, far, count), (BINS - 1) / log_total
     )
     for mask in partner_masks[:-1]:
         hist = hist + swap(hist, (mask & ~core) ^ core, count)

time: 52 us -> 51.5 us (level)
  Pallas kernels: 7.69 us -> 7.16 us
    pallas_call x2, Pallas kernels: 2.66 us -> 2.11 us  [the longest x1 1.21 us: last_sums(): pl.pallas_call(functools.partial(last_kernel, panel_bits, len(panels), le...]
where the time goes in v2:
time: 51.5 us; the launch traced here: 51.3 us
  waiting for transfers between devices  27.2 us (53%)
  starting transfers between devices  14.6 us (28%)
  Pallas kernels  7.16 us (14%)
  local copies, waits for them, and re-layouts  1.55 us (3%)
  between operations  0.75 us (1%)
    ppermute x15, waiting for transfers between devices, swap(): return lax.ppermute(x, AXES, [(i, i ^ mask) for i in range(count)])  27.2 us
    ppermute x15, starting transfers between devices, swap(): return lax.ppermute(x, AXES, [(i, i ^ mask) for i in range(count)])  14.6 us
    pallas_call x6, Pallas kernels, power_sums(): pl.pallas_call(functools.partial(power_kernel, len(panels)), out_shape=ja...  4.34 us
    unnamed x5, local copies, waits for them, and re-layouts  1.55 us
    pallas_call x1, Pallas kernels, last_sums(): pl.pallas_call(functools.partial(last_kernel, panel_bits, len(panels), le...  1.21 us
  transfers between devices with their start and end apart: 15, of which 9 were waited for; matrix products, arithmetic and copies ran while one was open for 1% of the time, Pallas kernels for 8%

profile of v2, /device:TPU:0, one launch (start us, length us, event | category | flops | bytes accessed | tf_op | source)
XLA Modules:
  0.0 51.3 jit_solution(11749564095428579392)
XLA Ops:
  0.6 3.1 %collective-permute-start.2 = (bf16[128,1024]{1,0:T(8,128)(2,1)}, bf16[128,1024]{1,0:T(8,128)(2,1)S(1)}, u32[]{:S(2)}, u32[]{:S(2)}) collective-permute-start(bf16[128,1024]{1,0:T(8,128)(2,1)} %refs_1_.3), channel_id=1, source_target_pairs={{0,8},{1,9},{2,10},{3,11},{4,12},{5,13},{6,14},{7,15},{8,0},{9,1},... | collective-permute-start | bytes 786440 | tf_op jit(solution)/shard_map/ppermute | solution.py:21
  3.7 2.6 %collective-permute-start = (bf16[128,1024]{1,0:T(8,128)(2,1)}, bf16[128,1024]{1,0:T(8,128)(2,1)S(1)}, u32[]{:S(2)}, u32[]{:S(2)}) collective-permute-start(bf16[128,1024]{1,0:T(8,128)(2,1)} %refs_1_.3), channel_id=1, source_target_pairs={{0,16},{1,17},{2,18},{3,19},{4,20},{5,21},{6,22},{7,23},{8,24},{9,... | collective-permute-start | bytes 786440 | tf_op jit(solution)/shard_map/ppermute | solution.py:21
  6.3 1.5 %collective-permute-start.3 = (bf16[128,1024]{1,0:T(8,128)(2,1)}, bf16[128,1024]{1,0:T(8,128)(2,1)S(1)}, u32[]{:S(2)}, u32[]{:S(2)}) collective-permute-start(bf16[128,1024]{1,0:T(8,128)(2,1)} %refs_1_.3), channel_id=1, source_target_pairs={{0,4},{1,5},{2,6},{3,7},{4,0},{5,1},{6,2},{7,3},{8,12},{9,13},{10,... | collective-permute-start | bytes 786440 | tf_op jit(solution)/shard_map/ppermute | solution.py:21
  7.9 7.9 %collective-permute-done.2.refs_4_.refs_2_ = bf16[128,1024]{1,0:T(8,128)(2,1)S(1)} collective-permute-done((bf16[128,1024]{1,0:T(8,128)(2,1)}, bf16[128,1024]{1,0:T(8,128)(2,1)S(1)}, u32[]{:S(2)}, u32[]{:S(2)}) %collective-permute-start.2) | collective-permute-done | bytes 262176 | tf_op jit(solution)/shard_map/ppermute | solution.py:21
  15.7 1.7 %collective-permute-start.4 = (bf16[128,1024]{1,0:T(8,128)(2,1)S(1)}, bf16[128,1024]{1,0:T(8,128)(2,1)S(1)}, u32[]{:S(2)}, u32[]{:S(2)}) collective-permute-start(bf16[128,1024]{1,0:T(8,128)(2,1)S(1)} %collective-permute-done.2.refs_4_.refs_2_), channel_id=1, source_target_pairs={{0,4},{1,5},{2,6},{3,7},{4,0},{5,1},{6,2},{7,3},{8,12},{9,13},{10,... | collective-permute-start | bytes 786440 | tf_op jit(solution)/shard_map/ppermute | solution.py:21
  17.4 1.5 %collective-permute-start.9 = (bf16[128,1024]{1,0:T(8,128)(2,1)}, bf16[128,1024]{1,0:T(8,128)(2,1)S(1)}, u32[]{:S(2)}, u32[]{:S(2)}) collective-permute-start(bf16[128,1024]{1,0:T(8,128)(2,1)} %refs_1_.3), channel_id=1, source_target_pairs={{0,2},{1,3},{2,0},{3,1},{4,6},{5,7},{6,4},{7,5},{8,10},{9,11},{10,... | collective-permute-start | bytes 786440 | tf_op jit(solution)/shard_map/ppermute | solution.py:21
  18.9 0.0 collective-permute-start.5
  18.9 0.0 collective-permute-done.refs_2_.refs_1_
  18.9 0.5 collective-permute-start.6
  19.4 0.0 collective-permute-done.3.refs_4_.refs_3_
  19.4 0.1 collective-permute-start.7
  19.5 3.7 %collective-permute-done.4.refs_3_.refs_4_ = bf16[128,1024]{1,0:T(8,128)(2,1)S(1)} collective-permute-done((bf16[128,1024]{1,0:T(8,128)(2,1)S(1)}, bf16[128,1024]{1,0:T(8,128)(2,1)S(1)}, u32[]{:S(2)}, u32[]{:S(2)}) %collective-permute-start.4) | collective-permute-done | bytes 262176 | tf_op jit(solution)/shard_map/ppermute | solution.py:21
  23.2 0.0 collective-permute-start.8
  23.2 1.3 %collective-permute-done.9.refs_1_.refs_0_ = bf16[128,1024]{1,0:T(8,128)(2,1)S(1)} collective-permute-done((bf16[128,1024]{1,0:T(8,128)(2,1)}, bf16[128,1024]{1,0:T(8,128)(2,1)S(1)}, u32[]{:S(2)}, u32[]{:S(2)}) %collective-permute-start.9) | collective-permute-done | bytes 262176 | tf_op jit(solution)/shard_map/ppermute | solution.py:21
  24.6 1.5 %collective-permute-start.1 = (bf16[128,1024]{1,0:T(8,128)(2,1)S(1)}, bf16[128,1024]{1,0:T(8,128)(2,1)S(1)}, u32[]{:S(2)}, u32[]{:S(2)}) collective-permute-start(bf16[128,1024]{1,0:T(8,128)(2,1)S(1)} %collective-permute-done.refs_2_.refs_1_), channel_id=1, source_target_pairs={{0,2},{1,3},{2,0},{3,1},{4,6},{5,7},{6,4},{7,5},{8,10},{9,11},{10,... | collective-permute-start | bytes 786440 | tf_op jit(solution)/shard_map/ppermute | solution.py:21
  26.0 0.0 copy-start
  26.0 0.9 %copy-done = bf16[128,1024]{1,0:T(8,128)(2,1)S(1)} copy-done((bf16[128,1024]{1,0:T(8,128)(2,1)S(1)}, bf16[128,1024]{1,0:T(8,128)(2,1)}, u32[]{:S(2)}) %copy-start) | copy-done | bytes 262168
  27.0 0.3 power_sums.6.refs_9_
  27.3 0.5 power_sums.8.refs_11_
  27.8 0.0 collective-permute-done.5.refs_3_.refs_5_
  27.8 0.9 %power_sums.7.refs_10_ = f32[3,20,128]{2,1,0:T(8,128)S(1)} custom-call(bf16[128,1024]{1,0:T(8,128)(2,1)S(1)} %copy-done, bf16[128,1024]{1,0:T(8,128)(2,1)S(1)} %collective-permute-done.9.refs_1_.refs_0_, bf16[128,1024]{1,0:T(8,128)(2,1)S(1)} %collective-permute-done.refs_2_.refs_1_, bf16[128,1024]{1,0:T(8,128)(2,1)S(1)} %collective-permute-done.5.refs_3_.refs_5_, ...), custom_call_target="tpu_custom_call" | custom-call | flops 201326592 | tf_op jit(solution)/shard_map/power_sums/pallas_call | solution.py:93
  28.8 0.7 %power_sums.10.refs_13_ = f32[3,20,128]{2,1,0:T(8,128)S(1)} custom-call(bf16[128,1024]{1,0:T(8,128)(2,1)S(1)} %copy-done, bf16[128,1024]{1,0:T(8,128)(2,1)S(1)} %collective-permute-done.9.refs_1_.refs_0_, bf16[128,1024]{1,0:T(8,128)(2,1)S(1)} %collective-permute-done.refs_2_.refs_1_, bf16[128,1024]{1,0:T(8,128)(2,1)S(1)} %collective-permute-done.4.refs_3_.refs_4_), custom_call_target="tpu_custom_call" | custom-call | flops 100663296 | tf_op jit(solution)/shard_map/power_sums/pallas_call | solution.py:93
  29.4 0.0 collective-permute-done.6.refs_5_.refs_6_
  29.4 0.0 collective-permute-done.7.refs_3_.refs_7_
  29.4 1.3 %power_sums.9.refs_12_ = f32[3,20,128]{2,1,0:T(8,128)S(1)} custom-call(bf16[128,1024]{1,0:T(8,128)(2,1)S(1)} %copy-done, bf16[128,1024]{1,0:T(8,128)(2,1)S(1)} %collective-permute-done.9.refs_1_.refs_0_, bf16[128,1024]{1,0:T(8,128)(2,1)S(1)} %collective-permute-done.refs_2_.refs_1_, bf16[128,1024]{1,0:T(8,128)(2,1)S(1)} %collective-permute-done.7.refs_3_.refs_7_, ...), custom_call_target="tpu_custom_call" | custom-call | flops 301989888 | tf_op jit(solution)/shard_map/power_sums/pallas_call | solution.py:93
  30.8 0.0 copy-start.1
  30.8 0.0 collective-permute-done.8.refs_3_.refs_8_
  30.8 0.7 %power_sums.11.refs_14_ = f32[3,20,128]{2,1,0:T(8,128)S(1)} custom-call(bf16[128,1024]{1,0:T(8,128)(2,1)S(1)} %copy-done, bf16[128,1024]{1,0:T(8,128)(2,1)S(1)} %collective-permute-done.9.refs_1_.refs_0_, bf16[128,1024]{1,0:T(8,128)(2,1)S(1)} %collective-permute-done.refs_2_.refs_1_, bf16[128,1024]{1,0:T(8,128)(2,1)S(1)} %collective-permute-done.8.refs_3_.refs_8_), custom_call_target="tpu_custom_call" | custom-call | flops 100663296 | tf_op jit(solution)/shard_map/power_sums/pallas_call | solution.py:93
  31.4 0.5 collective-permute-done.1.refs_0_
  31.9 0.0 copy-done.1
  31.9 1.2 %last_sums.1 = f32[80,128]{1,0:T(8,128)S(1)} custom-call(s32[20]{0:T(128)S(1)} %copy-done.1, bf16[128,1024]{1,0:T(8,128)(2,1)S(1)} %collective-permute-done.1.refs_0_, bf16[128,1024]{1,0:T(8,128)(2,1)S(1)} %copy-done, bf16[128,1024]{1,0:T(8,128)(2,1)S(1)} %collective-permute-done.2.refs_4_.refs_2_, ...), custom_call_target="tpu_custom_call" | custom-call | flops 268435456 | tf_op jit(solution)/shard_map/last_sums/pallas_call | solution.py:137
  33.2 1.4 %collective-permute-start.10 = (f32[80,128]{1,0:T(8,128)S(1)}, f32[80,128]{1,0:T(8,128)S(1)}, u32[]{:S(2)}, u32[]{:S(2)}) collective-permute-start(f32[80,128]{1,0:T(8,128)S(1)} %last_sums.1), channel_id=1, source_target_pairs={{0,2},{1,3},{2,0},{3,1},{4,6},{5,7},{6,4},{7,5},{8,10},{9,11},{10,... | collective-permute-start | bytes 122888 | tf_op jit(solution)/shard_map/ppermute | solution.py:21
  34.6 2.6 %collective-permute-done.10 = f32[80,128]{1,0:T(8,128)S(1)} collective-permute-done((f32[80,128]{1,0:T(8,128)S(1)}, f32[80,128]{1,0:T(8,128)S(1)}, u32[]{:S(2)}, u32[]{:S(2)}) %collective-permute-start.10) | collective-permute-done | bytes 40992 | tf_op jit(solution)/shard_map/ppermute | solution.py:21
  37.2 0.6 %collective-permute-start.11 = (f32[80,128]{1,0:T(8,128)S(1)}, f32[80,128]{1,0:T(8,128)S(1)}, u32[]{:S(2)}, u32[]{:S(2)}) collective-permute-start(f32[80,128]{1,0:T(8,128)S(1)} %add.9.conn_ref), channel_id=1, source_target_pairs={{0,16},{1,17},{2,18},{3,19},{4,20},{5,21},{6,22},{7,23},{8,24},{9,... | collective-permute-start | bytes 122888 | tf_op jit(solution)/shard_map/ppermute | solution.py:21
  37.8 4.3 %collective-permute-done.11.other_ref = f32[80,128]{1,0:T(8,128)S(1)} collective-permute-done((f32[80,128]{1,0:T(8,128)S(1)}, f32[80,128]{1,0:T(8,128)S(1)}, u32[]{:S(2)}, u32[]{:S(2)}) %collective-permute-start.11) | collective-permute-done | bytes 40992 | tf_op jit(solution)/shard_map/ppermute | solution.py:21
  42.1 0.9 %histogram.1 = (f32[20,128]{1,0:T(8,128)S(1)}, f32[20,128]{1,0:T(8,128)S(1)}) custom-call(f32[80,128]{1,0:T(8,128)S(1)} %add.9.conn_ref, f32[80,128]{1,0:T(8,128)S(1)} %collective-permute-done.11.other_ref), custom_call_target="tpu_custom_call" | custom-call | tf_op jit(solution)/shard_map/histogram/pallas_call | solution.py:180
  43.0 0.0 collective-permute-start.12
  43.1 3.1 %collective-permute-done.12 = f32[20,128]{1,0:T(8,128)S(1)} collective-permute-done((f32[20,128]{1,0:T(8,128)S(1)}, f32[20,128]{1,0:T(8,128)S(1)}, u32[]{:S(2)}, u32[]{:S(2)}) %collective-permute-start.12) | collective-permute-done | bytes 10272 | tf_op jit(solution)/shard_map/ppermute | solution.py:21
  46.2 0.0 collective-permute-start.13
  46.2 3.2 %collective-permute-done.13 = f32[20,128]{1,0:T(8,128)S(1)} collective-permute-done((f32[20,128]{1,0:T(8,128)S(1)}, f32[20,128]{1,0:T(8,128)S(1)}, u32[]{:S(2)}, u32[]{:S(2)}) %collective-permute-start.13) | collective-permute-done | bytes 10272 | tf_op jit(solution)/shard_map/ppermute | solution.py:21
  49.4 0.1 collective-permute-start.14
  49.5 0.6 %copy.5 = f32[128,20]{0,1:T(8,128)} copy(f32[128,20]{0,1:T(8,128)S(1)} %bitcast.1) | data formatting | bytes 20480
  50.1 0.5 collective-permute-done.14.other_ref
  50.6 0.7 %scale_free_fit.1 = (f32[20]{0:T(128)}, f32[20]{0:T(128)}) custom-call(f32[20,128]{1,0:T(8,128)S(1)} %add.11.hist_ref, f32[20,128]{1,0:T(8,128)S(1)} %collective-permute-done.14.other_ref), custom_call_target="tpu_custom_call" | custom-call | tf_op jit(solution)/shard_map/scale_free_fit/pallas_call | solution.py:221
  (3 shorter events, 0.0 us)
Async XLA Ops:
  0.6 15.1 %collective-permute-start.2 = (bf16[128,1024]{1,0:T(8,128)(2,1)}, bf16[128,1024]{1,0:T(8,128)(2,1)S(1)}, u32[]{:S(2)}, u32[]{:S(2)}) collective-permute-start(bf16[128,1024]{1,0:T(8,128)(2,1)} %refs_1_.3), channel_id=1, source_target_pairs={{0,8},{1,9},{2,10},{3,11},{4,12},{5,13},{6,14},{7,15},{8,0},{9,1},... | collective-permute-start | bytes 786440 | tf_op jit(solution)/shard_map/ppermute | solution.py:21
  3.7 15.2 %collective-permute-start = (bf16[128,1024]{1,0:T(8,128)(2,1)}, bf16[128,1024]{1,0:T(8,128)(2,1)S(1)}, u32[]{:S(2)}, u32[]{:S(2)}) collective-permute-start(bf16[128,1024]{1,0:T(8,128)(2,1)} %refs_1_.3), channel_id=1, source_target_pairs={{0,16},{1,17},{2,18},{3,19},{4,20},{5,21},{6,22},{7,23},{8,24},{9,... | collective-permute-start | bytes 786440 | tf_op jit(solution)/shard_map/ppermute | solution.py:21
  6.3 13.1 %collective-permute-start.3 = (bf16[128,1024]{1,0:T(8,128)(2,1)}, bf16[128,1024]{1,0:T(8,128)(2,1)S(1)}, u32[]{:S(2)}, u32[]{:S(2)}) collective-permute-start(bf16[128,1024]{1,0:T(8,128)(2,1)} %refs_1_.3), channel_id=1, source_target_pairs={{0,4},{1,5},{2,6},{3,7},{4,0},{5,1},{6,2},{7,3},{8,12},{9,13},{10,... | collective-permute-start | bytes 786440 | tf_op jit(solution)/shard_map/ppermute | solution.py:21
  15.7 7.5 %collective-permute-start.4 = (bf16[128,1024]{1,0:T(8,128)(2,1)S(1)}, bf16[128,1024]{1,0:T(8,128)(2,1)S(1)}, u32[]{:S(2)}, u32[]{:S(2)}) collective-permute-start(bf16[128,1024]{1,0:T(8,128)(2,1)S(1)} %collective-permute-done.2.refs_4_.refs_2_), channel_id=1, source_target_pairs={{0,4},{1,5},{2,6},{3,7},{4,0},{5,1},{6,2},{7,3},{8,12},{9,13},{10,... | collective-permute-start | bytes 786440 | tf_op jit(solution)/shard_map/ppermute | solution.py:21
  17.4 7.1 %collective-permute-start.9 = (bf16[128,1024]{1,0:T(8,128)(2,1)}, bf16[128,1024]{1,0:T(8,128)(2,1)S(1)}, u32[]{:S(2)}, u32[]{:S(2)}) collective-permute-start(bf16[128,1024]{1,0:T(8,128)(2,1)} %refs_1_.3), channel_id=1, source_target_pairs={{0,2},{1,3},{2,0},{3,1},{4,6},{5,7},{6,4},{7,5},{8,10},{9,11},{10,... | collective-permute-start | bytes 786440 | tf_op jit(solution)/shard_map/ppermute | solution.py:21
  18.9 8.9 %collective-permute-start.5 = (bf16[128,1024]{1,0:T(8,128)(2,1)}, bf16[128,1024]{1,0:T(8,128)(2,1)S(1)}, u32[]{:S(2)}, u32[]{:S(2)}) collective-permute-start(bf16[128,1024]{1,0:T(8,128)(2,1)} %refs_1_.3), channel_id=1, source_target_pairs={{0,1},{1,0},{2,3},{3,2},{4,5},{5,4},{6,7},{7,6},{8,9},{9,8},{10,11... | collective-permute-start | bytes 786440 | tf_op jit(solution)/shard_map/ppermute | solution.py:21
  18.9 10.5 %collective-permute-start.6 = (bf16[128,1024]{1,0:T(8,128)(2,1)S(1)}, bf16[128,1024]{1,0:T(8,128)(2,1)S(1)}, u32[]{:S(2)}, u32[]{:S(2)}) collective-permute-start(bf16[128,1024]{1,0:T(8,128)(2,1)S(1)} %collective-permute-done.2.refs_4_.refs_2_), channel_id=1, source_target_pairs={{0,1},{1,0},{2,3},{3,2},{4,5},{5,4},{6,7},{7,6},{8,9},{9,8},{10,11... | collective-permute-start | bytes 786440 | tf_op jit(solution)/shard_map/ppermute | solution.py:21
  19.4 10.0 %collective-permute-start.7 = (bf16[128,1024]{1,0:T(8,128)(2,1)S(1)}, bf16[128,1024]{1,0:T(8,128)(2,1)S(1)}, u32[]{:S(2)}, u32[]{:S(2)}) collective-permute-start(bf16[128,1024]{1,0:T(8,128)(2,1)S(1)} %collective-permute-done.3.refs_4_.refs_3_), channel_id=1, source_target_pairs={{0,1},{1,0},{2,3},{3,2},{4,5},{5,4},{6,7},{7,6},{8,9},{9,8},{10,11... | collective-permute-start | bytes 786440 | tf_op jit(solution)/shard_map/ppermute | solution.py:21
  23.2 7.5 %collective-permute-start.8 = (bf16[128,1024]{1,0:T(8,128)(2,1)S(1)}, bf16[128,1024]{1,0:T(8,128)(2,1)S(1)}, u32[]{:S(2)}, u32[]{:S(2)}) collective-permute-start(bf16[128,1024]{1,0:T(8,128)(2,1)S(1)} %collective-permute-done.4.refs_3_.refs_4_), channel_id=1, source_target_pairs={{0,1},{1,0},{2,3},{3,2},{4,5},{5,4},{6,7},{7,6},{8,9},{9,8},{10,11... | collective-permute-start | bytes 786440 | tf_op jit(solution)/shard_map/ppermute | solution.py:21
  24.6 7.4 %collective-permute-start.1 = (bf16[128,1024]{1,0:T(8,128)(2,1)S(1)}, bf16[128,1024]{1,0:T(8,128)(2,1)S(1)}, u32[]{:S(2)}, u32[]{:S(2)}) collective-permute-start(bf16[128,1024]{1,0:T(8,128)(2,1)S(1)} %collective-permute-done.refs_2_.refs_1_), channel_id=1, source_target_pairs={{0,2},{1,3},{2,0},{3,1},{4,6},{5,7},{6,4},{7,5},{8,10},{9,11},{10,... | collective-permute-start | bytes 786440 | tf_op jit(solution)/shard_map/ppermute | solution.py:21
  26.0 0.9 %copy-start = (bf16[128,1024]{1,0:T(8,128)(2,1)S(1)}, bf16[128,1024]{1,0:T(8,128)(2,1)}, u32[]{:S(2)}) copy-start(bf16[128,1024]{1,0:T(8,128)(2,1)} %refs_1_.3) | copy-start | bytes 786436
  30.8 1.2 %copy-start.1 = (s32[20]{0:T(128)S(1)}, s32[20]{0:T(128)}, u32[]{:S(2)}) copy-start(s32[20]{0:T(128)} %order_hbm.1) | copy-start | bytes 244
  33.2 4.1 %collective-permute-start.10 = (f32[80,128]{1,0:T(8,128)S(1)}, f32[80,128]{1,0:T(8,128)S(1)}, u32[]{:S(2)}, u32[]{:S(2)}) collective-permute-start(f32[80,128]{1,0:T(8,128)S(1)} %last_sums.1), channel_id=1, source_target_pairs={{0,2},{1,3},{2,0},{3,1},{4,6},{5,7},{6,4},{7,5},{8,10},{9,11},{10,... | collective-permute-start | bytes 122888 | tf_op jit(solution)/shard_map/ppermute | solution.py:21
  37.2 4.9 %collective-permute-start.11 = (f32[80,128]{1,0:T(8,128)S(1)}, f32[80,128]{1,0:T(8,128)S(1)}, u32[]{:S(2)}, u32[]{:S(2)}) collective-permute-start(f32[80,128]{1,0:T(8,128)S(1)} %add.9.conn_ref), channel_id=1, source_target_pairs={{0,16},{1,17},{2,18},{3,19},{4,20},{5,21},{6,22},{7,23},{8,24},{9,... | collective-permute-start | bytes 122888 | tf_op jit(solution)/shard_map/ppermute | solution.py:21
  43.0 3.2 %collective-permute-start.12 = (f32[20,128]{1,0:T(8,128)S(1)}, f32[20,128]{1,0:T(8,128)S(1)}, u32[]{:S(2)}, u32[]{:S(2)}) collective-permute-start(f32[20,128]{1,0:T(8,128)S(1)} %get-tuple-element.8), channel_id=1, source_target_pairs={{0,9},{1,8},{2,11},{3,10},{4,13},{5,12},{6,15},{7,14},{8,1},{9,0},... | collective-permute-start | bytes 30728 | tf_op jit(solution)/shard_map/ppermute | solution.py:21
  46.2 3.2 %collective-permute-start.13 = (f32[20,128]{1,0:T(8,128)S(1)}, f32[20,128]{1,0:T(8,128)S(1)}, u32[]{:S(2)}, u32[]{:S(2)}) collective-permute-start(f32[20,128]{1,0:T(8,128)S(1)} %add.10), channel_id=1, source_target_pairs={{0,5},{1,4},{2,7},{3,6},{4,1},{5,0},{6,3},{7,2},{8,13},{9,12},{10,... | collective-permute-start | bytes 30728 | tf_op jit(solution)/shard_map/ppermute | solution.py:21
  49.4 1.2 %collective-permute-start.14 = (f32[20,128]{1,0:T(8,128)S(1)}, f32[20,128]{1,0:T(8,128)S(1)}, u32[]{:S(2)}, u32[]{:S(2)}) collective-permute-start(f32[20,128]{1,0:T(8,128)S(1)} %add.11.hist_ref), channel_id=1, source_target_pairs={{0,1},{1,0},{2,3},{3,2},{4,5},{5,4},{6,7},{7,6},{8,9},{9,8},{10,11... | collective-permute-start | bytes 30728 | tf_op jit(solution)/shard_map/ppermute | solution.py:21

commit v3 on v2

--- a/solution.py
+++ b/solution.py
@@ -110,8 +110,8 @@
 
 
 def last_kernel(panel_bits, n_panel, n_partner, parts, order_hbm, *refs):
-    part_refs = refs[n_panel + n_partner : -5]
-    conn_ref, total_ref, natural, order, arrived = refs[-5:]
+    part_refs = refs[n_panel + n_partner : -6]
+    conn_ref, total_ref, natural, packed, order, arrived = refs[-6:]
     slots = len(parts)
     powers = total_ref.shape[1]
     fetch = pltpu.make_async_copy(order_hbm, order, arrived)
@@ -121,13 +121,14 @@
     for i, where in enumerate(parts):
         values = [part_refs[a][b] for a, b in where if a is not None]
         values += [jnp.sum(total_ref[b], axis=1) for a, b in where if a is None]
-        natural[i] = functools.reduce(jnp.add, values)
+        natural[i] = functools.reduce(jnp.add, values) - (0.0 if i else 1.0)
     fetch.wait()
     for t in range(powers):
         at = order[t]
         for i in range(slots):
             slot = jnp.bitwise_xor(mine, i)
-            conn_ref[pl.ds(t * slots + slot, 1), :] = natural[i, pl.ds(at, 1), :]
+            packed[pl.ds(t * slots + slot, 1), :] = natural[i, pl.ds(at, 1), :]
+    conn_ref[...] = packed[...].astype(conn_ref.dtype)
 
 
 def last_sums(panel_bits, power_order, panels, partners, done, parts):
@@ -136,13 +137,14 @@
     flops = len(panels) * len(partners) * genes * genes * 2 * samples
     return pl.pallas_call(
         functools.partial(last_kernel, panel_bits, len(panels), len(partners), parts),
-        out_shape=jax.ShapeDtypeStruct((powers * len(parts), genes), jnp.float32),
+        out_shape=jax.ShapeDtypeStruct((powers * len(parts), genes), jnp.bfloat16),
         in_specs=[pl.BlockSpec(memory_space=pltpu.HBM)]
         + [VMEM] * (len(panels) + len(partners) + len(done)),
         out_specs=VMEM,
         scratch_shapes=[
             pltpu.VMEM((len(panels), powers, 8, genes), jnp.float32),
             pltpu.VMEM((len(parts), powers, genes), jnp.float32),
+            pltpu.VMEM((powers * len(parts), genes), jnp.float32),
             pltpu.SMEM((powers,), jnp.int32),
             pltpu.SemaphoreType.DMA(()),
         ],
@@ -157,7 +159,8 @@
     powers = log_ref.shape[0]
     slots = rows // powers
     mine = own_slot(panel_bits)
-    logs[...] = jnp.log(conn_ref[...] + other_ref[...])
+    less = conn_ref[...].astype(jnp.float32) + other_ref[...].astype(jnp.float32)
+    logs[...] = jnp.log(less + 1.0)
     places[...] = logs[...] * scale
     levels = lax.broadcasted_iota(jnp.int32, (BINS, genes), 0).astype(jnp.float32)
     lane = lax.broadcasted_iota(jnp.int32, (BINS, BINS), 1)
@@ -276,7 +279,8 @@
     )
 
     for mask in panel_masks[:0:-1]:
-        conn = conn + swap(conn, mask, count)
+        other = swap(conn, mask, count)
+        conn = (conn.astype(jnp.float32) + other.astype(jnp.float32)).astype(conn.dtype)
     log_conn, hist = histogram(
         panel_bits, powers, conn, swap(conn, far, count), (BINS - 1) / log_total
     )

time: 51.5 us -> 51.1 us (level)
  transfers between devices with their start and end apart: 15 -> 15, of which waited for: 9 -> 9; matrix products, arithmetic and copies ran while one was open for 1% -> 1% of each run, Pallas kernels for 8% -> 9%
where the time goes in v3:
time: 51.1 us; the launch traced here: 51 us
  waiting for transfers between devices  26.8 us (52%)
  starting transfers between devices  14.7 us (29%)
  Pallas kernels  7.19 us (14%)
  local copies, waits for them, and re-layouts  1.55 us (3%)
  between operations  0.75 us (1%)
    ppermute x15, waiting for transfers between devices, swap(): return lax.ppermute(x, AXES, [(i, i ^ mask) for i in range(count)])  26.8 us
    ppermute x15, starting transfers between devices, swap(): return lax.ppermute(x, AXES, [(i, i ^ mask) for i in range(count)])  14.7 us
    pallas_call x6, Pallas kernels, power_sums(): pl.pallas_call(functools.partial(power_kernel, len(panels)), out_shape=ja...  4.34 us
    unnamed x5, local copies, waits for them, and re-layouts  1.55 us
    pallas_call x1, Pallas kernels, last_sums(): pl.pallas_call(functools.partial(last_kernel, panel_bits, len(panels), le...  1.23 us
  transfers between devices with their start and end apart: 15, of which 9 were waited for; matrix products, arithmetic and copies ran while one was open for 1% of the time, Pallas kernels for 9%

profile of v3, /device:TPU:0, one launch (start us, length us, event | category | flops | bytes accessed | tf_op | source)
XLA Modules:
  0.0 51.0 jit_solution(2507485390160492352)
XLA Ops:
  0.6 3.1 %collective-permute-start.2 = (bf16[128,1024]{1,0:T(8,128)(2,1)}, bf16[128,1024]{1,0:T(8,128)(2,1)S(1)}, u32[]{:S(2)}, u32[]{:S(2)}) collective-permute-start(bf16[128,1024]{1,0:T(8,128)(2,1)} %refs_1_.3), channel_id=1, source_target_pairs={{0,8},{1,9},{2,10},{3,11},{4,12},{5,13},{6,14},{7,15},{8,0},{9,1},... | collective-permute-start | bytes 786440 | tf_op jit(solution)/shard_map/ppermute | solution.py:21
  3.7 2.6 %collective-permute-start = (bf16[128,1024]{1,0:T(8,128)(2,1)}, bf16[128,1024]{1,0:T(8,128)(2,1)S(1)}, u32[]{:S(2)}, u32[]{:S(2)}) collective-permute-start(bf16[128,1024]{1,0:T(8,128)(2,1)} %refs_1_.3), channel_id=1, source_target_pairs={{0,16},{1,17},{2,18},{3,19},{4,20},{5,21},{6,22},{7,23},{8,24},{9,... | collective-permute-start | bytes 786440 | tf_op jit(solution)/shard_map/ppermute | solution.py:21
  6.3 1.5 %collective-permute-start.3 = (bf16[128,1024]{1,0:T(8,128)(2,1)}, bf16[128,1024]{1,0:T(8,128)(2,1)S(1)}, u32[]{:S(2)}, u32[]{:S(2)}) collective-permute-start(bf16[128,1024]{1,0:T(8,128)(2,1)} %refs_1_.3), channel_id=1, source_target_pairs={{0,4},{1,5},{2,6},{3,7},{4,0},{5,1},{6,2},{7,3},{8,12},{9,13},{10,... | collective-permute-start | bytes 786440 | tf_op jit(solution)/shard_map/ppermute | solution.py:21
  7.9 7.9 %collective-permute-done.2.refs_4_.refs_2_ = bf16[128,1024]{1,0:T(8,128)(2,1)S(1)} collective-permute-done((bf16[128,1024]{1,0:T(8,128)(2,1)}, bf16[128,1024]{1,0:T(8,128)(2,1)S(1)}, u32[]{:S(2)}, u32[]{:S(2)}) %collective-permute-start.2) | collective-permute-done | bytes 262176 | tf_op jit(solution)/shard_map/ppermute | solution.py:21
  15.7 1.7 %collective-permute-start.4 = (bf16[128,1024]{1,0:T(8,128)(2,1)S(1)}, bf16[128,1024]{1,0:T(8,128)(2,1)S(1)}, u32[]{:S(2)}, u32[]{:S(2)}) collective-permute-start(bf16[128,1024]{1,0:T(8,128)(2,1)S(1)} %collective-permute-done.2.refs_4_.refs_2_), channel_id=1, source_target_pairs={{0,4},{1,5},{2,6},{3,7},{4,0},{5,1},{6,2},{7,3},{8,12},{9,13},{10,... | collective-permute-start | bytes 786440 | tf_op jit(solution)/shard_map/ppermute | solution.py:21
  17.4 1.5 %collective-permute-start.9 = (bf16[128,1024]{1,0:T(8,128)(2,1)}, bf16[128,1024]{1,0:T(8,128)(2,1)S(1)}, u32[]{:S(2)}, u32[]{:S(2)}) collective-permute-start(bf16[128,1024]{1,0:T(8,128)(2,1)} %refs_1_.3), channel_id=1, source_target_pairs={{0,2},{1,3},{2,0},{3,1},{4,6},{5,7},{6,4},{7,5},{8,10},{9,11},{10,... | collective-permute-start | bytes 786440 | tf_op jit(solution)/shard_map/ppermute | solution.py:21
  18.9 0.0 collective-permute-start.5
  18.9 0.0 collective-permute-done.refs_2_.refs_1_
  18.9 0.5 collective-permute-start.6
  19.4 0.0 collective-permute-done.3.refs_4_.refs_3_
  19.4 0.1 collective-permute-start.7
  19.5 3.7 %collective-permute-done.4.refs_3_.refs_4_ = bf16[128,1024]{1,0:T(8,128)(2,1)S(1)} collective-permute-done((bf16[128,1024]{1,0:T(8,128)(2,1)S(1)}, bf16[128,1024]{1,0:T(8,128)(2,1)S(1)}, u32[]{:S(2)}, u32[]{:S(2)}) %collective-permute-start.4) | collective-permute-done | bytes 262176 | tf_op jit(solution)/shard_map/ppermute | solution.py:21
  23.2 0.0 collective-permute-start.8
  23.2 1.3 %collective-permute-done.9.refs_1_.refs_0_ = bf16[128,1024]{1,0:T(8,128)(2,1)S(1)} collective-permute-done((bf16[128,1024]{1,0:T(8,128)(2,1)}, bf16[128,1024]{1,0:T(8,128)(2,1)S(1)}, u32[]{:S(2)}, u32[]{:S(2)}) %collective-permute-start.9) | collective-permute-done | bytes 262176 | tf_op jit(solution)/shard_map/ppermute | solution.py:21
  24.6 1.5 %collective-permute-start.1 = (bf16[128,1024]{1,0:T(8,128)(2,1)S(1)}, bf16[128,1024]{1,0:T(8,128)(2,1)S(1)}, u32[]{:S(2)}, u32[]{:S(2)}) collective-permute-start(bf16[128,1024]{1,0:T(8,128)(2,1)S(1)} %collective-permute-done.refs_2_.refs_1_), channel_id=1, source_target_pairs={{0,2},{1,3},{2,0},{3,1},{4,6},{5,7},{6,4},{7,5},{8,10},{9,11},{10,... | collective-permute-start | bytes 786440 | tf_op jit(solution)/shard_map/ppermute | solution.py:21
  26.0 0.0 copy-start
  26.0 0.9 %copy-done = bf16[128,1024]{1,0:T(8,128)(2,1)S(1)} copy-done((bf16[128,1024]{1,0:T(8,128)(2,1)S(1)}, bf16[128,1024]{1,0:T(8,128)(2,1)}, u32[]{:S(2)}) %copy-start) | copy-done | bytes 262168
  27.0 0.3 power_sums.6.refs_9_
  27.3 0.5 power_sums.8.refs_11_
  27.8 0.0 collective-permute-done.5.refs_3_.refs_5_
  27.8 0.9 %power_sums.7.refs_10_ = f32[3,20,128]{2,1,0:T(8,128)S(1)} custom-call(bf16[128,1024]{1,0:T(8,128)(2,1)S(1)} %copy-done, bf16[128,1024]{1,0:T(8,128)(2,1)S(1)} %collective-permute-done.9.refs_1_.refs_0_, bf16[128,1024]{1,0:T(8,128)(2,1)S(1)} %collective-permute-done.refs_2_.refs_1_, bf16[128,1024]{1,0:T(8,128)(2,1)S(1)} %collective-permute-done.5.refs_3_.refs_5_, ...), custom_call_target="tpu_custom_call" | custom-call | flops 201326592 | tf_op jit(solution)/shard_map/power_sums/pallas_call | solution.py:93
  28.8 0.7 %power_sums.10.refs_13_ = f32[3,20,128]{2,1,0:T(8,128)S(1)} custom-call(bf16[128,1024]{1,0:T(8,128)(2,1)S(1)} %copy-done, bf16[128,1024]{1,0:T(8,128)(2,1)S(1)} %collective-permute-done.9.refs_1_.refs_0_, bf16[128,1024]{1,0:T(8,128)(2,1)S(1)} %collective-permute-done.refs_2_.refs_1_, bf16[128,1024]{1,0:T(8,128)(2,1)S(1)} %collective-permute-done.4.refs_3_.refs_4_), custom_call_target="tpu_custom_call" | custom-call | flops 100663296 | tf_op jit(solution)/shard_map/power_sums/pallas_call | solution.py:93
  29.4 0.0 collective-permute-done.6.refs_5_.refs_6_
  29.4 0.0 collective-permute-done.7.refs_3_.refs_7_
  29.4 1.3 %power_sums.9.refs_12_ = f32[3,20,128]{2,1,0:T(8,128)S(1)} custom-call(bf16[128,1024]{1,0:T(8,128)(2,1)S(1)} %copy-done, bf16[128,1024]{1,0:T(8,128)(2,1)S(1)} %collective-permute-done.9.refs_1_.refs_0_, bf16[128,1024]{1,0:T(8,128)(2,1)S(1)} %collective-permute-done.refs_2_.refs_1_, bf16[128,1024]{1,0:T(8,128)(2,1)S(1)} %collective-permute-done.7.refs_3_.refs_7_, ...), custom_call_target="tpu_custom_call" | custom-call | flops 301989888 | tf_op jit(solution)/shard_map/power_sums/pallas_call | solution.py:93
  30.8 0.0 copy-start.1
  30.8 0.0 collective-permute-done.8.refs_3_.refs_8_
  30.8 0.7 %power_sums.11.refs_14_ = f32[3,20,128]{2,1,0:T(8,128)S(1)} custom-call(bf16[128,1024]{1,0:T(8,128)(2,1)S(1)} %copy-done, bf16[128,1024]{1,0:T(8,128)(2,1)S(1)} %collective-permute-done.9.refs_1_.refs_0_, bf16[128,1024]{1,0:T(8,128)(2,1)S(1)} %collective-permute-done.refs_2_.refs_1_, bf16[128,1024]{1,0:T(8,128)(2,1)S(1)} %collective-permute-done.8.refs_3_.refs_8_), custom_call_target="tpu_custom_call" | custom-call | flops 100663296 | tf_op jit(solution)/shard_map/power_sums/pallas_call | solution.py:93
  31.4 0.5 collective-permute-done.1.refs_0_
  31.9 0.0 copy-done.1
  31.9 1.2 %last_sums.1 = bf16[80,128]{1,0:T(8,128)(2,1)S(1)} custom-call(s32[20]{0:T(128)S(1)} %copy-done.1, bf16[128,1024]{1,0:T(8,128)(2,1)S(1)} %collective-permute-done.1.refs_0_, bf16[128,1024]{1,0:T(8,128)(2,1)S(1)} %copy-done, bf16[128,1024]{1,0:T(8,128)(2,1)S(1)} %collective-permute-done.2.refs_4_.refs_2_, ...), custom_call_target="tpu_custom_call" | custom-call | flops 268435456 | tf_op jit(solution)/shard_map/last_sums/pallas_call | solution.py:138
  33.2 1.4 %collective-permute-start.10 = (bf16[80,128]{1,0:T(8,128)(2,1)S(1)}, bf16[80,128]{1,0:T(8,128)(2,1)S(1)}, u32[]{:S(2)}, u32[]{:S(2)}) collective-permute-start(bf16[80,128]{1,0:T(8,128)(2,1)S(1)} %last_sums.1), channel_id=1, source_target_pairs={{0,2},{1,3},{2,0},{3,1},{4,6},{5,7},{6,4},{7,5},{8,10},{9,11},{10,... | collective-permute-start | bytes 61448 | tf_op jit(solution)/shard_map/ppermute | solution.py:21
  34.6 2.4 %collective-permute-done.10 = bf16[80,128]{1,0:T(8,128)(2,1)S(1)} collective-permute-done((bf16[80,128]{1,0:T(8,128)(2,1)S(1)}, bf16[80,128]{1,0:T(8,128)(2,1)S(1)}, u32[]{:S(2)}, u32[]{:S(2)}) %collective-permute-start.10) | collective-permute-done | bytes 20512 | tf_op jit(solution)/shard_map/ppermute | solution.py:21
  37.0 0.6 %collective-permute-start.11 = (bf16[80,128]{1,0:T(8,128)(2,1)S(1)}, bf16[80,128]{1,0:T(8,128)(2,1)S(1)}, u32[]{:S(2)}, u32[]{:S(2)}) collective-permute-start(bf16[80,128]{1,0:T(8,128)(2,1)S(1)} %add_convert_fusion.conn_ref), channel_id=1, source_target_pairs={{0,16},{1,17},{2,18},{3,19},{4,20},{5,21},{6,22},{7,23},{8,24},{9,... | collective-permute-start | bytes 61448 | tf_op jit(solution)/shard_map/ppermute | solution.py:21
  37.7 4.1 %collective-permute-done.11.other_ref = bf16[80,128]{1,0:T(8,128)(2,1)S(1)} collective-permute-done((bf16[80,128]{1,0:T(8,128)(2,1)S(1)}, bf16[80,128]{1,0:T(8,128)(2,1)S(1)}, u32[]{:S(2)}, u32[]{:S(2)}) %collective-permute-start.11) | collective-permute-done | bytes 20512 | tf_op jit(solution)/shard_map/ppermute | solution.py:21
  41.8 0.9 %histogram.1 = (f32[20,128]{1,0:T(8,128)S(1)}, f32[20,128]{1,0:T(8,128)S(1)}) custom-call(bf16[80,128]{1,0:T(8,128)(2,1)S(1)} %add_convert_fusion.conn_ref, bf16[80,128]{1,0:T(8,128)(2,1)S(1)} %collective-permute-done.11.other_ref), custom_call_target="tpu_custom_call" | custom-call | tf_op jit(solution)/shard_map/histogram/pallas_call | solution.py:183
  42.7 0.0 collective-permute-start.12
  42.8 3.1 %collective-permute-done.12 = f32[20,128]{1,0:T(8,128)S(1)} collective-permute-done((f32[20,128]{1,0:T(8,128)S(1)}, f32[20,128]{1,0:T(8,128)S(1)}, u32[]{:S(2)}, u32[]{:S(2)}) %collective-permute-start.12) | collective-permute-done | bytes 10272 | tf_op jit(solution)/shard_map/ppermute | solution.py:21
  45.9 0.0 collective-permute-start.13
  45.9 3.2 %collective-permute-done.13 = f32[20,128]{1,0:T(8,128)S(1)} collective-permute-done((f32[20,128]{1,0:T(8,128)S(1)}, f32[20,128]{1,0:T(8,128)S(1)}, u32[]{:S(2)}, u32[]{:S(2)}) %collective-permute-start.13) | collective-permute-done | bytes 10272 | tf_op jit(solution)/shard_map/ppermute | solution.py:21
  49.1 0.1 collective-permute-start.14
  49.1 0.6 %copy.5 = f32[128,20]{0,1:T(8,128)} copy(f32[128,20]{0,1:T(8,128)S(1)} %bitcast.1) | data formatting | bytes 20480
  49.7 0.5 %collective-permute-done.14.other_ref = f32[20,128]{1,0:T(8,128)S(1)} collective-permute-done((f32[20,128]{1,0:T(8,128)S(1)}, f32[20,128]{1,0:T(8,128)S(1)}, u32[]{:S(2)}, u32[]{:S(2)}) %collective-permute-start.14) | collective-permute-done | bytes 10272 | tf_op jit(solution)/shard_map/ppermute | solution.py:21
  50.3 0.7 %scale_free_fit.1 = (f32[20]{0:T(128)}, f32[20]{0:T(128)}) custom-call(f32[20,128]{1,0:T(8,128)S(1)} %add.11.hist_ref, f32[20,128]{1,0:T(8,128)S(1)} %collective-permute-done.14.other_ref), custom_call_target="tpu_custom_call" | custom-call | tf_op jit(solution)/shard_map/scale_free_fit/pallas_call | solution.py:224
  (3 shorter events, 0.0 us)
Async XLA Ops:
  0.6 15.1 %collective-permute-start.2 = (bf16[128,1024]{1,0:T(8,128)(2,1)}, bf16[128,1024]{1,0:T(8,128)(2,1)S(1)}, u32[]{:S(2)}, u32[]{:S(2)}) collective-permute-start(bf16[128,1024]{1,0:T(8,128)(2,1)} %refs_1_.3), channel_id=1, source_target_pairs={{0,8},{1,9},{2,10},{3,11},{4,12},{5,13},{6,14},{7,15},{8,0},{9,1},... | collective-permute-start | bytes 786440 | tf_op jit(solution)/shard_map/ppermute | solution.py:21
  3.7 15.2 %collective-permute-start = (bf16[128,1024]{1,0:T(8,128)(2,1)}, bf16[128,1024]{1,0:T(8,128)(2,1)S(1)}, u32[]{:S(2)}, u32[]{:S(2)}) collective-permute-start(bf16[128,1024]{1,0:T(8,128)(2,1)} %refs_1_.3), channel_id=1, source_target_pairs={{0,16},{1,17},{2,18},{3,19},{4,20},{5,21},{6,22},{7,23},{8,24},{9,... | collective-permute-start | bytes 786440 | tf_op jit(solution)/shard_map/ppermute | solution.py:21
  6.3 13.1 %collective-permute-start.3 = (bf16[128,1024]{1,0:T(8,128)(2,1)}, bf16[128,1024]{1,0:T(8,128)(2,1)S(1)}, u32[]{:S(2)}, u32[]{:S(2)}) collective-permute-start(bf16[128,1024]{1,0:T(8,128)(2,1)} %refs_1_.3), channel_id=1, source_target_pairs={{0,4},{1,5},{2,6},{3,7},{4,0},{5,1},{6,2},{7,3},{8,12},{9,13},{10,... | collective-permute-start | bytes 786440 | tf_op jit(solution)/shard_map/ppermute | solution.py:21
  15.7 7.5 %collective-permute-start.4 = (bf16[128,1024]{1,0:T(8,128)(2,1)S(1)}, bf16[128,1024]{1,0:T(8,128)(2,1)S(1)}, u32[]{:S(2)}, u32[]{:S(2)}) collective-permute-start(bf16[128,1024]{1,0:T(8,128)(2,1)S(1)} %collective-permute-done.2.refs_4_.refs_2_), channel_id=1, source_target_pairs={{0,4},{1,5},{2,6},{3,7},{4,0},{5,1},{6,2},{7,3},{8,12},{9,13},{10,... | collective-permute-start | bytes 786440 | tf_op jit(solution)/shard_map/ppermute | solution.py:21
  17.4 7.1 %collective-permute-start.9 = (bf16[128,1024]{1,0:T(8,128)(2,1)}, bf16[128,1024]{1,0:T(8,128)(2,1)S(1)}, u32[]{:S(2)}, u32[]{:S(2)}) collective-permute-start(bf16[128,1024]{1,0:T(8,128)(2,1)} %refs_1_.3), channel_id=1, source_target_pairs={{0,2},{1,3},{2,0},{3,1},{4,6},{5,7},{6,4},{7,5},{8,10},{9,11},{10,... | collective-permute-start | bytes 786440 | tf_op jit(solution)/shard_map/ppermute | solution.py:21
  18.9 8.9 %collective-permute-start.5 = (bf16[128,1024]{1,0:T(8,128)(2,1)}, bf16[128,1024]{1,0:T(8,128)(2,1)S(1)}, u32[]{:S(2)}, u32[]{:S(2)}) collective-permute-start(bf16[128,1024]{1,0:T(8,128)(2,1)} %refs_1_.3), channel_id=1, source_target_pairs={{0,1},{1,0},{2,3},{3,2},{4,5},{5,4},{6,7},{7,6},{8,9},{9,8},{10,11... | collective-permute-start | bytes 786440 | tf_op jit(solution)/shard_map/ppermute | solution.py:21
  18.9 10.5 %collective-permute-start.6 = (bf16[128,1024]{1,0:T(8,128)(2,1)S(1)}, bf16[128,1024]{1,0:T(8,128)(2,1)S(1)}, u32[]{:S(2)}, u32[]{:S(2)}) collective-permute-start(bf16[128,1024]{1,0:T(8,128)(2,1)S(1)} %collective-permute-done.2.refs_4_.refs_2_), channel_id=1, source_target_pairs={{0,1},{1,0},{2,3},{3,2},{4,5},{5,4},{6,7},{7,6},{8,9},{9,8},{10,11... | collective-permute-start | bytes 786440 | tf_op jit(solution)/shard_map/ppermute | solution.py:21
  19.4 10.0 %collective-permute-start.7 = (bf16[128,1024]{1,0:T(8,128)(2,1)S(1)}, bf16[128,1024]{1,0:T(8,128)(2,1)S(1)}, u32[]{:S(2)}, u32[]{:S(2)}) collective-permute-start(bf16[128,1024]{1,0:T(8,128)(2,1)S(1)} %collective-permute-done.3.refs_4_.refs_3_), channel_id=1, source_target_pairs={{0,1},{1,0},{2,3},{3,2},{4,5},{5,4},{6,7},{7,6},{8,9},{9,8},{10,11... | collective-permute-start | bytes 786440 | tf_op jit(solution)/shard_map/ppermute | solution.py:21
  23.2 7.5 %collective-permute-start.8 = (bf16[128,1024]{1,0:T(8,128)(2,1)S(1)}, bf16[128,1024]{1,0:T(8,128)(2,1)S(1)}, u32[]{:S(2)}, u32[]{:S(2)}) collective-permute-start(bf16[128,1024]{1,0:T(8,128)(2,1)S(1)} %collective-permute-done.4.refs_3_.refs_4_), channel_id=1, source_target_pairs={{0,1},{1,0},{2,3},{3,2},{4,5},{5,4},{6,7},{7,6},{8,9},{9,8},{10,11... | collective-permute-start | bytes 786440 | tf_op jit(solution)/shard_map/ppermute | solution.py:21
  24.6 7.4 %collective-permute-start.1 = (bf16[128,1024]{1,0:T(8,128)(2,1)S(1)}, bf16[128,1024]{1,0:T(8,128)(2,1)S(1)}, u32[]{:S(2)}, u32[]{:S(2)}) collective-permute-start(bf16[128,1024]{1,0:T(8,128)(2,1)S(1)} %collective-permute-done.refs_2_.refs_1_), channel_id=1, source_target_pairs={{0,2},{1,3},{2,0},{3,1},{4,6},{5,7},{6,4},{7,5},{8,10},{9,11},{10,... | collective-permute-start | bytes 786440 | tf_op jit(solution)/shard_map/ppermute | solution.py:21
  26.0 0.9 %copy-start = (bf16[128,1024]{1,0:T(8,128)(2,1)S(1)}, bf16[128,1024]{1,0:T(8,128)(2,1)}, u32[]{:S(2)}) copy-start(bf16[128,1024]{1,0:T(8,128)(2,1)} %refs_1_.3) | copy-start | bytes 786436
  30.8 1.2 %copy-start.1 = (s32[20]{0:T(128)S(1)}, s32[20]{0:T(128)}, u32[]{:S(2)}) copy-start(s32[20]{0:T(128)} %order_hbm.1) | copy-start | bytes 244
  33.2 3.8 %collective-permute-start.10 = (bf16[80,128]{1,0:T(8,128)(2,1)S(1)}, bf16[80,128]{1,0:T(8,128)(2,1)S(1)}, u32[]{:S(2)}, u32[]{:S(2)}) collective-permute-start(bf16[80,128]{1,0:T(8,128)(2,1)S(1)} %last_sums.1), channel_id=1, source_target_pairs={{0,2},{1,3},{2,0},{3,1},{4,6},{5,7},{6,4},{7,5},{8,10},{9,11},{10,... | collective-permute-start | bytes 61448 | tf_op jit(solution)/shard_map/ppermute | solution.py:21
  37.0 4.7 %collective-permute-start.11 = (bf16[80,128]{1,0:T(8,128)(2,1)S(1)}, bf16[80,128]{1,0:T(8,128)(2,1)S(1)}, u32[]{:S(2)}, u32[]{:S(2)}) collective-permute-start(bf16[80,128]{1,0:T(8,128)(2,1)S(1)} %add_convert_fusion.conn_ref), channel_id=1, source_target_pairs={{0,16},{1,17},{2,18},{3,19},{4,20},{5,21},{6,22},{7,23},{8,24},{9,... | collective-permute-start | bytes 61448 | tf_op jit(solution)/shard_map/ppermute | solution.py:21
  42.7 3.2 %collective-permute-start.12 = (f32[20,128]{1,0:T(8,128)S(1)}, f32[20,128]{1,0:T(8,128)S(1)}, u32[]{:S(2)}, u32[]{:S(2)}) collective-permute-start(f32[20,128]{1,0:T(8,128)S(1)} %get-tuple-element.8), channel_id=1, source_target_pairs={{0,9},{1,8},{2,11},{3,10},{4,13},{5,12},{6,15},{7,14},{8,1},{9,0},... | collective-permute-start | bytes 30728 | tf_op jit(solution)/shard_map/ppermute | solution.py:21
  45.9 3.2 %collective-permute-start.13 = (f32[20,128]{1,0:T(8,128)S(1)}, f32[20,128]{1,0:T(8,128)S(1)}, u32[]{:S(2)}, u32[]{:S(2)}) collective-permute-start(f32[20,128]{1,0:T(8,128)S(1)} %add.10), channel_id=1, source_target_pairs={{0,5},{1,4},{2,7},{3,6},{4,1},{5,0},{6,3},{7,2},{8,13},{9,12},{10,... | collective-permute-start | bytes 30728 | tf_op jit(solution)/shard_map/ppermute | solution.py:21
  49.1 1.2 %collective-permute-start.14 = (f32[20,128]{1,0:T(8,128)S(1)}, f32[20,128]{1,0:T(8,128)S(1)}, u32[]{:S(2)}, u32[]{:S(2)}) collective-permute-start(f32[20,128]{1,0:T(8,128)S(1)} %add.11.hist_ref), channel_id=1, source_target_pairs={{0,1},{1,0},{2,3},{3,2},{4,5},{5,4},{6,7},{7,6},{8,9},{9,8},{10,11... | collective-permute-start | bytes 30728 | tf_op jit(solution)/shard_map/ppermute | solution.py:21

commit v4 on v2

--- a/solution.py
+++ b/solution.py
@@ -12,6 +12,7 @@
 AXES = ("row", "col")
 BINS = 128
 CHUNK = 8
+FRONT, REAR = -1, -2
 VMEM = pl.BlockSpec(memory_space=pltpu.VMEM)
 SMEM = pl.BlockSpec(memory_space=pltpu.SMEM)
 PARAMS = pltpu.CompilerParams(vmem_limit_bytes=16 * 2**20)
@@ -109,18 +110,21 @@
     return sum(((index // bit) % 2) << i for i, bit in enumerate(panel_bits))
 
 
-def last_kernel(panel_bits, n_panel, n_partner, parts, order_hbm, *refs):
-    part_refs = refs[n_panel + n_partner : -5]
-    conn_ref, total_ref, natural, order, arrived = refs[-5:]
+def last_kernel(panel_bits, n_front, n_panel, n_partner, parts, order_hbm, *refs):
+    front_refs, tail_ref, refs = refs[:n_front], refs[n_front], refs[n_front + 1 :]
+    part_refs = refs[n_panel + n_partner : -6]
+    conn_ref, front_total, total_ref, natural, order, arrived = refs[-6:]
     slots = len(parts)
     powers = total_ref.shape[1]
     fetch = pltpu.make_async_copy(order_hbm, order, arrived)
     fetch.start()
     mine = own_slot(panel_bits)
+    add_powers(front_refs, [tail_ref], front_total)
     add_powers(refs[:n_panel], refs[n_panel : n_panel + n_partner], total_ref)
     for i, where in enumerate(parts):
-        values = [part_refs[a][b] for a, b in where if a is not None]
-        values += [jnp.sum(total_ref[b], axis=1) for a, b in where if a is None]
+        values = [part_refs[a][b] for a, b in where if a >= 0]
+        values += [jnp.sum(front_total[b], axis=1) for a, b in where if a == FRONT]
+        values += [jnp.sum(total_ref[b], axis=1) for a, b in where if a == REAR]
         natural[i] = functools.reduce(jnp.add, values)
     fetch.wait()
     for t in range(powers):
@@ -130,17 +134,20 @@
             conn_ref[pl.ds(t * slots + slot, 1), :] = natural[i, pl.ds(at, 1), :]
 
 
-def last_sums(panel_bits, power_order, panels, partners, done, parts):
+def last_sums(panel_bits, power_order, front, tail, panels, partners, done, parts):
     genes, samples = panels[0].shape
     powers = power_order.shape[0]
     flops = len(panels) * len(partners) * genes * genes * 2 * samples
     return pl.pallas_call(
-        functools.partial(last_kernel, panel_bits, len(panels), len(partners), parts),
+        functools.partial(
+            last_kernel, panel_bits, len(front), len(panels), len(partners), parts
+        ),
         out_shape=jax.ShapeDtypeStruct((powers * len(parts), genes), jnp.float32),
         in_specs=[pl.BlockSpec(memory_space=pltpu.HBM)]
-        + [VMEM] * (len(panels) + len(partners) + len(done)),
+        + [VMEM] * (len(front) + 1 + len(panels) + len(partners) + len(done)),
         out_specs=VMEM,
         scratch_shapes=[
+            pltpu.VMEM((len(front), powers, 8, genes), jnp.float32),
             pltpu.VMEM((len(panels), powers, 8, genes), jnp.float32),
             pltpu.VMEM((len(parts), powers, genes), jnp.float32),
             pltpu.SMEM((powers,), jnp.int32),
@@ -149,7 +156,7 @@
         compiler_params=PARAMS,
         cost_estimate=pl.CostEstimate(flops=flops, bytes_accessed=0, transcendentals=0),
         name="last_sums",
-    )(power_order, *map(in_vmem, panels), *map(in_vmem, partners), *map(in_vmem, done))
+    )(power_order, *map(in_vmem, [*front, tail, *panels, *partners, *done]))
 
 
 def hist_kernel(scale, panel_bits, conn_ref, other_ref, log_ref, hist_ref, logs, places):
@@ -252,11 +259,12 @@
         (front[1:], [0]),
         (front, [k ^ core for k in sides] + [low, low ^ core]),
         (front, [k for k in relayed if not k & core]),
-        (front, [k for k in relayed if k & core]),
+        (front, [k for k in relayed if k & core][:-1]),
     ]
+    tail = [k for k in relayed if k & core][-1]
     done = []
     parts = {k: [] for k in keys}
-    for n, (panels, partners) in enumerate(waves):
+    for n, (panels, partners) in enumerate(wave for wave in waves if wave[1]):
         done.append(power_sums([panel[k] for k in panels], [partner[k] for k in partners], powers))
         for i, k in enumerate(panels):
             parts[k].append((n, i))
@@ -265,10 +273,14 @@
     if early:
         done.append(power_sums([panel[k] for k in rear], [partner[k] for k in early], powers))
     for i, k in enumerate(rear):
-        parts[k] += [(len(done) - 1, i)] * bool(early) + [(None, i)]
+        parts[k] += [(len(done) - 1, i)] * bool(early) + [(REAR, i)]
+    for i, k in enumerate(front):
+        parts[k].append((FRONT, i))
     conn = last_sums(
         panel_bits,
         power_order,
+        [panel[k] for k in front],
+        partner[tail],
         [panel[k] for k in rear],
         [partner[k] for k in late],
         done,

time: 51.5 us -> 48.2 us (0.936)
  waiting for transfers between devices: 27.2 us -> 23.7 us
    ppermute x15, waiting for transfers between devices: 27.2 us -> 23.7 us  [swap(): return lax.ppermute(x, AXES, [(i, i ^ mask) for i in range(count)])]
    pallas_call x6 -> x5, Pallas kernels: 4.34 us -> 3.7 us  [power_sums(): pl.pallas_call(functools.partial(power_kernel, len(panels)), out_shape=ja...]
    pallas_call x1, Pallas kernels: 1.21 us -> 1.76 us  [last_sums(): pl.pallas_call(functools.partial(last_kernel, panel_bits, len(front), len...]
where the time goes in v4:
time: 48.2 us; the launch traced here: 48.1 us
  waiting for transfers between devices  23.7 us (49%)
  starting transfers between devices  15 us (31%)
  Pallas kernels  7.06 us (15%)
  local copies, waits for them, and re-layouts  1.56 us (3%)
  between operations  0.74 us (2%)
    ppermute x15, waiting for transfers between devices, swap(): return lax.ppermute(x, AXES, [(i, i ^ mask) for i in range(count)])  23.7 us
    ppermute x15, starting transfers between devices, swap(): return lax.ppermute(x, AXES, [(i, i ^ mask) for i in range(count)])  15 us
    pallas_call x5, Pallas kernels, power_sums(): pl.pallas_call(functools.partial(power_kernel, len(panels)), out_shape=ja...  3.7 us
    pallas_call x1, Pallas kernels, last_sums(): pl.pallas_call(functools.partial(last_kernel, panel_bits, len(front), len...  1.76 us
    unnamed x5, local copies, waits for them, and re-layouts  1.56 us
  transfers between devices with their start and end apart: 15, of which 9 were waited for; matrix products, arithmetic and copies ran while one was open for 1% of the time, Pallas kernels for 8%

profile of v4, /device:TPU:0, one launch (start us, length us, event | category | flops | bytes accessed | tf_op | source)
XLA Modules:
  0.0 48.1 jit_solution(7070933630352268424)
XLA Ops:
  0.6 3.1 %collective-permute-start.2 = (bf16[128,1024]{1,0:T(8,128)(2,1)}, bf16[128,1024]{1,0:T(8,128)(2,1)S(1)}, u32[]{:S(2)}, u32[]{:S(2)}) collective-permute-start(bf16[128,1024]{1,0:T(8,128)(2,1)} %refs_5_.1), channel_id=1, source_target_pairs={{0,8},{1,9},{2,10},{3,11},{4,12},{5,13},{6,14},{7,15},{8,0},{9,1},... | collective-permute-start | bytes 786440 | tf_op jit(solution)/shard_map/ppermute | solution.py:22
  3.7 1.5 %collective-permute-start.6 = (bf16[128,1024]{1,0:T(8,128)(2,1)}, bf16[128,1024]{1,0:T(8,128)(2,1)S(1)}, u32[]{:S(2)}, u32[]{:S(2)}) collective-permute-start(bf16[128,1024]{1,0:T(8,128)(2,1)} %refs_5_.1), channel_id=1, source_target_pairs={{0,4},{1,5},{2,6},{3,7},{4,0},{5,1},{6,2},{7,3},{8,12},{9,13},{10,... | collective-permute-start | bytes 786440 | tf_op jit(solution)/shard_map/ppermute | solution.py:22
  5.3 2.6 %collective-permute-start.1 = (bf16[128,1024]{1,0:T(8,128)(2,1)}, bf16[128,1024]{1,0:T(8,128)(2,1)S(1)}, u32[]{:S(2)}, u32[]{:S(2)}) collective-permute-start(bf16[128,1024]{1,0:T(8,128)(2,1)} %refs_5_.1), channel_id=1, source_target_pairs={{0,16},{1,17},{2,18},{3,19},{4,20},{5,21},{6,22},{7,23},{8,24},{9,... | collective-permute-start | bytes 786440 | tf_op jit(solution)/shard_map/ppermute | solution.py:22
  7.9 1.5 %collective-permute-start = (bf16[128,1024]{1,0:T(8,128)(2,1)}, bf16[128,1024]{1,0:T(8,128)(2,1)S(1)}, u32[]{:S(2)}, u32[]{:S(2)}) collective-permute-start(bf16[128,1024]{1,0:T(8,128)(2,1)} %refs_5_.1), channel_id=1, source_target_pairs={{0,2},{1,3},{2,0},{3,1},{4,6},{5,7},{6,4},{7,5},{8,10},{9,11},{10,... | collective-permute-start | bytes 786440 | tf_op jit(solution)/shard_map/ppermute | solution.py:22
  9.3 5.2 %collective-permute-done.2.refs_4_.refs_6_ = bf16[128,1024]{1,0:T(8,128)(2,1)S(1)} collective-permute-done((bf16[128,1024]{1,0:T(8,128)(2,1)}, bf16[128,1024]{1,0:T(8,128)(2,1)S(1)}, u32[]{:S(2)}, u32[]{:S(2)}) %collective-permute-start.2) | collective-permute-done | bytes 262176 | tf_op jit(solution)/shard_map/ppermute | solution.py:22
  14.5 2.7 %collective-permute-start.3 = (bf16[128,1024]{1,0:T(8,128)(2,1)S(1)}, bf16[128,1024]{1,0:T(8,128)(2,1)S(1)}, u32[]{:S(2)}, u32[]{:S(2)}) collective-permute-start(bf16[128,1024]{1,0:T(8,128)(2,1)S(1)} %collective-permute-done.2.refs_4_.refs_6_), channel_id=1, source_target_pairs={{0,4},{1,5},{2,6},{3,7},{4,0},{5,1},{6,2},{7,3},{8,12},{9,13},{10,... | collective-permute-start | bytes 786440 | tf_op jit(solution)/shard_map/ppermute | solution.py:22
  17.2 0.0 collective-permute-start.7
  17.2 0.0 collective-permute-done.6.refs_4_.refs_7_
  17.2 0.5 %collective-permute-start.9 = (bf16[128,1024]{1,0:T(8,128)(2,1)S(1)}, bf16[128,1024]{1,0:T(8,128)(2,1)S(1)}, u32[]{:S(2)}, u32[]{:S(2)}) collective-permute-start(bf16[128,1024]{1,0:T(8,128)(2,1)S(1)} %collective-permute-done.6.refs_4_.refs_7_), channel_id=1, source_target_pairs={{0,1},{1,0},{2,3},{3,2},{4,5},{5,4},{6,7},{7,6},{8,9},{9,8},{10,11... | collective-permute-start | bytes 786440 | tf_op jit(solution)/shard_map/ppermute | solution.py:22
  17.7 1.8 %collective-permute-done.1.refs_2_.refs_1_ = bf16[128,1024]{1,0:T(8,128)(2,1)S(1)} collective-permute-done((bf16[128,1024]{1,0:T(8,128)(2,1)}, bf16[128,1024]{1,0:T(8,128)(2,1)S(1)}, u32[]{:S(2)}, u32[]{:S(2)}) %collective-permute-start.1) | collective-permute-done | bytes 262176 | tf_op jit(solution)/shard_map/ppermute | solution.py:22
  19.5 0.0 collective-permute-start.8
  19.5 0.0 collective-permute-done.refs_1_.refs_0_
  19.6 1.5 %collective-permute-start.5 = (bf16[128,1024]{1,0:T(8,128)(2,1)S(1)}, bf16[128,1024]{1,0:T(8,128)(2,1)S(1)}, u32[]{:S(2)}, u32[]{:S(2)}) collective-permute-start(bf16[128,1024]{1,0:T(8,128)(2,1)S(1)} %collective-permute-done.1.refs_2_.refs_1_), channel_id=1, source_target_pairs={{0,2},{1,3},{2,0},{3,1},{4,6},{5,7},{6,4},{7,5},{8,10},{9,11},{10,... | collective-permute-start | bytes 786440 | tf_op jit(solution)/shard_map/ppermute | solution.py:22
  21.0 1.6 %collective-permute-done.3.refs_3_.refs_8_ = bf16[128,1024]{1,0:T(8,128)(2,1)S(1)} collective-permute-done((bf16[128,1024]{1,0:T(8,128)(2,1)S(1)}, bf16[128,1024]{1,0:T(8,128)(2,1)S(1)}, u32[]{:S(2)}, u32[]{:S(2)}) %collective-permute-start.3) | collective-permute-done | bytes 262176 | tf_op jit(solution)/shard_map/ppermute | solution.py:22
  22.7 0.0 collective-permute-start.4
  22.7 0.0 copy-start
  22.7 0.9 %copy-done = bf16[128,1024]{1,0:T(8,128)(2,1)S(1)} copy-done((bf16[128,1024]{1,0:T(8,128)(2,1)S(1)}, bf16[128,1024]{1,0:T(8,128)(2,1)}, u32[]{:S(2)}) %copy-start) | copy-done | bytes 262168
  23.6 0.3 power_sums.5.refs_13_
  23.9 0.5 %power_sums.7.refs_15_ = f32[2,20,128]{2,1,0:T(8,128)S(1)} custom-call(bf16[128,1024]{1,0:T(8,128)(2,1)S(1)} %collective-permute-done.refs_1_.refs_0_, bf16[128,1024]{1,0:T(8,128)(2,1)S(1)} %collective-permute-done.1.refs_2_.refs_1_, bf16[128,1024]{1,0:T(8,128)(2,1)S(1)} %copy-done), custom_call_target="tpu_custom_call" | custom-call | flops 67108864 | tf_op jit(solution)/shard_map/power_sums/pallas_call | solution.py:94
  24.4 0.0 collective-permute-done.7.refs_3_.refs_9_
  24.4 0.9 %power_sums.6.refs_14_ = f32[3,20,128]{2,1,0:T(8,128)S(1)} custom-call(bf16[128,1024]{1,0:T(8,128)(2,1)S(1)} %copy-done, bf16[128,1024]{1,0:T(8,128)(2,1)S(1)} %collective-permute-done.refs_1_.refs_0_, bf16[128,1024]{1,0:T(8,128)(2,1)S(1)} %collective-permute-done.1.refs_2_.refs_1_, bf16[128,1024]{1,0:T(8,128)(2,1)S(1)} %collective-permute-done.7.refs_3_.refs_9_, ...), custom_call_target="tpu_custom_call" | custom-call | flops 201326592 | tf_op jit(solution)/shard_map/power_sums/pallas_call | solution.py:94
  25.4 0.7 %power_sums.9.refs_17_ = f32[3,20,128]{2,1,0:T(8,128)S(1)} custom-call(bf16[128,1024]{1,0:T(8,128)(2,1)S(1)} %copy-done, bf16[128,1024]{1,0:T(8,128)(2,1)S(1)} %collective-permute-done.refs_1_.refs_0_, bf16[128,1024]{1,0:T(8,128)(2,1)S(1)} %collective-permute-done.1.refs_2_.refs_1_, bf16[128,1024]{1,0:T(8,128)(2,1)S(1)} %collective-permute-done.3.refs_3_.refs_8_), custom_call_target="tpu_custom_call" | custom-call | flops 100663296 | tf_op jit(solution)/shard_map/power_sums/pallas_call | solution.py:94
  26.0 0.0 copy-start.1
  26.1 0.0 collective-permute-done.9.refs_3_.refs_11_
  26.1 0.0 collective-permute-done.8.refs_5_.refs_10_
  26.1 1.3 %power_sums.8.refs_16_ = f32[3,20,128]{2,1,0:T(8,128)S(1)} custom-call(bf16[128,1024]{1,0:T(8,128)(2,1)S(1)} %copy-done, bf16[128,1024]{1,0:T(8,128)(2,1)S(1)} %collective-permute-done.refs_1_.refs_0_, bf16[128,1024]{1,0:T(8,128)(2,1)S(1)} %collective-permute-done.1.refs_2_.refs_1_, bf16[128,1024]{1,0:T(8,128)(2,1)S(1)} %collective-permute-done.9.refs_3_.refs_11_, ...), custom_call_target="tpu_custom_call" | custom-call | flops 301989888 | tf_op jit(solution)/shard_map/power_sums/pallas_call | solution.py:94
  27.4 0.9 %collective-permute-done.5.refs_4_ = bf16[128,1024]{1,0:T(8,128)(2,1)S(1)} collective-permute-done((bf16[128,1024]{1,0:T(8,128)(2,1)S(1)}, bf16[128,1024]{1,0:T(8,128)(2,1)S(1)}, u32[]{:S(2)}, u32[]{:S(2)}) %collective-permute-start.5) | collective-permute-done | bytes 262176 | tf_op jit(solution)/shard_map/ppermute | solution.py:22
  28.3 0.0 collective-permute-done.4.refs_3_.refs_12_
  28.3 0.0 copy-done.1
  28.3 1.8 %last_sums.1 = f32[80,128]{1,0:T(8,128)S(1)} custom-call(s32[20]{0:T(128)S(1)} %copy-done.1, bf16[128,1024]{1,0:T(8,128)(2,1)S(1)} %copy-done, bf16[128,1024]{1,0:T(8,128)(2,1)S(1)} %collective-permute-done.refs_1_.refs_0_, bf16[128,1024]{1,0:T(8,128)(2,1)S(1)} %collective-permute-done.1.refs_2_.refs_1_, ...), custom_call_target="tpu_custom_call" | custom-call | flops 268435456 | tf_op jit(solution)/shard_map/last_sums/pallas_call | solution.py:141
  30.0 1.6 %collective-permute-start.10 = (f32[80,128]{1,0:T(8,128)S(1)}, f32[80,128]{1,0:T(8,128)S(1)}, u32[]{:S(2)}, u32[]{:S(2)}) collective-permute-start(f32[80,128]{1,0:T(8,128)S(1)} %last_sums.1), channel_id=1, source_target_pairs={{0,2},{1,3},{2,0},{3,1},{4,6},{5,7},{6,4},{7,5},{8,10},{9,11},{10,... | collective-permute-start | bytes 122888 | tf_op jit(solution)/shard_map/ppermute | solution.py:22
  31.6 2.5 %collective-permute-done.10 = f32[80,128]{1,0:T(8,128)S(1)} collective-permute-done((f32[80,128]{1,0:T(8,128)S(1)}, f32[80,128]{1,0:T(8,128)S(1)}, u32[]{:S(2)}, u32[]{:S(2)}) %collective-permute-start.10) | collective-permute-done | bytes 40992 | tf_op jit(solution)/shard_map/ppermute | solution.py:22
  34.1 0.0 collective-permute-start.11
  34.1 4.9 %collective-permute-done.11.other_ref = f32[80,128]{1,0:T(8,128)S(1)} collective-permute-done((f32[80,128]{1,0:T(8,128)S(1)}, f32[80,128]{1,0:T(8,128)S(1)}, u32[]{:S(2)}, u32[]{:S(2)}) %collective-permute-start.11) | collective-permute-done | bytes 40992 | tf_op jit(solution)/shard_map/ppermute | solution.py:22
  39.0 0.9 %histogram.1 = (f32[20,128]{1,0:T(8,128)S(1)}, f32[20,128]{1,0:T(8,128)S(1)}) custom-call(f32[80,128]{1,0:T(8,128)S(1)} %add.9.conn_ref, f32[80,128]{1,0:T(8,128)S(1)} %collective-permute-done.11.other_ref), custom_call_target="tpu_custom_call" | custom-call | tf_op jit(solution)/shard_map/histogram/pallas_call | solution.py:187
  39.9 0.0 collective-permute-start.12
  40.0 3.1 %collective-permute-done.12 = f32[20,128]{1,0:T(8,128)S(1)} collective-permute-done((f32[20,128]{1,0:T(8,128)S(1)}, f32[20,128]{1,0:T(8,128)S(1)}, u32[]{:S(2)}, u32[]{:S(2)}) %collective-permute-start.12) | collective-permute-done | bytes 10272 | tf_op jit(solution)/shard_map/ppermute | solution.py:22
  43.1 0.0 collective-permute-start.13
  43.1 3.1 %collective-permute-done.13 = f32[20,128]{1,0:T(8,128)S(1)} collective-permute-done((f32[20,128]{1,0:T(8,128)S(1)}, f32[20,128]{1,0:T(8,128)S(1)}, u32[]{:S(2)}, u32[]{:S(2)}) %collective-permute-start.13) | collective-permute-done | bytes 10272 | tf_op jit(solution)/shard_map/ppermute | solution.py:22
  46.2 0.0 collective-permute-start.14
  46.2 0.6 %copy.5 = f32[128,20]{0,1:T(8,128)} copy(f32[128,20]{0,1:T(8,128)S(1)} %bitcast.1) | data formatting | bytes 20480
  46.8 0.6 %collective-permute-done.14.other_ref = f32[20,128]{1,0:T(8,128)S(1)} collective-permute-done((f32[20,128]{1,0:T(8,128)S(1)}, f32[20,128]{1,0:T(8,128)S(1)}, u32[]{:S(2)}, u32[]{:S(2)}) %collective-permute-start.14) | collective-permute-done | bytes 10272 | tf_op jit(solution)/shard_map/ppermute | solution.py:22
  47.4 0.7 %scale_free_fit.1 = (f32[20]{0:T(128)}, f32[20]{0:T(128)}) custom-call(f32[20,128]{1,0:T(8,128)S(1)} %add.11.hist_ref, f32[20,128]{1,0:T(8,128)S(1)} %collective-permute-done.14.other_ref), custom_call_target="tpu_custom_call" | custom-call | tf_op jit(solution)/shard_map/scale_free_fit/pallas_call | solution.py:228
  (3 shorter events, 0.0 us)
Async XLA Ops:
  0.6 13.9 %collective-permute-start.2 = (bf16[128,1024]{1,0:T(8,128)(2,1)}, bf16[128,1024]{1,0:T(8,128)(2,1)S(1)}, u32[]{:S(2)}, u32[]{:S(2)}) collective-permute-start(bf16[128,1024]{1,0:T(8,128)(2,1)} %refs_5_.1), channel_id=1, source_target_pairs={{0,8},{1,9},{2,10},{3,11},{4,12},{5,13},{6,14},{7,15},{8,0},{9,1},... | collective-permute-start | bytes 786440 | tf_op jit(solution)/shard_map/ppermute | solution.py:22
  3.7 13.5 %collective-permute-start.6 = (bf16[128,1024]{1,0:T(8,128)(2,1)}, bf16[128,1024]{1,0:T(8,128)(2,1)S(1)}, u32[]{:S(2)}, u32[]{:S(2)}) collective-permute-start(bf16[128,1024]{1,0:T(8,128)(2,1)} %refs_5_.1), channel_id=1, source_target_pairs={{0,4},{1,5},{2,6},{3,7},{4,0},{5,1},{6,2},{7,3},{8,12},{9,13},{10,... | collective-permute-start | bytes 786440 | tf_op jit(solution)/shard_map/ppermute | solution.py:22
  5.3 14.3 %collective-permute-start.1 = (bf16[128,1024]{1,0:T(8,128)(2,1)}, bf16[128,1024]{1,0:T(8,128)(2,1)S(1)}, u32[]{:S(2)}, u32[]{:S(2)}) collective-permute-start(bf16[128,1024]{1,0:T(8,128)(2,1)} %refs_5_.1), channel_id=1, source_target_pairs={{0,16},{1,17},{2,18},{3,19},{4,20},{5,21},{6,22},{7,23},{8,24},{9,... | collective-permute-start | bytes 786440 | tf_op jit(solution)/shard_map/ppermute | solution.py:22
  7.9 11.7 %collective-permute-start = (bf16[128,1024]{1,0:T(8,128)(2,1)}, bf16[128,1024]{1,0:T(8,128)(2,1)S(1)}, u32[]{:S(2)}, u32[]{:S(2)}) collective-permute-start(bf16[128,1024]{1,0:T(8,128)(2,1)} %refs_5_.1), channel_id=1, source_target_pairs={{0,2},{1,3},{2,0},{3,1},{4,6},{5,7},{6,4},{7,5},{8,10},{9,11},{10,... | collective-permute-start | bytes 786440 | tf_op jit(solution)/shard_map/ppermute | solution.py:22
  14.5 8.1 %collective-permute-start.3 = (bf16[128,1024]{1,0:T(8,128)(2,1)S(1)}, bf16[128,1024]{1,0:T(8,128)(2,1)S(1)}, u32[]{:S(2)}, u32[]{:S(2)}) collective-permute-start(bf16[128,1024]{1,0:T(8,128)(2,1)S(1)} %collective-permute-done.2.refs_4_.refs_6_), channel_id=1, source_target_pairs={{0,4},{1,5},{2,6},{3,7},{4,0},{5,1},{6,2},{7,3},{8,12},{9,13},{10,... | collective-permute-start | bytes 786440 | tf_op jit(solution)/shard_map/ppermute | solution.py:22
  17.2 7.2 %collective-permute-start.7 = (bf16[128,1024]{1,0:T(8,128)(2,1)}, bf16[128,1024]{1,0:T(8,128)(2,1)S(1)}, u32[]{:S(2)}, u32[]{:S(2)}) collective-permute-start(bf16[128,1024]{1,0:T(8,128)(2,1)} %refs_5_.1), channel_id=1, source_target_pairs={{0,1},{1,0},{2,3},{3,2},{4,5},{5,4},{6,7},{7,6},{8,9},{9,8},{10,11... | collective-permute-start | bytes 786440 | tf_op jit(solution)/shard_map/ppermute | solution.py:22
  17.2 8.8 %collective-permute-start.9 = (bf16[128,1024]{1,0:T(8,128)(2,1)S(1)}, bf16[128,1024]{1,0:T(8,128)(2,1)S(1)}, u32[]{:S(2)}, u32[]{:S(2)}) collective-permute-start(bf16[128,1024]{1,0:T(8,128)(2,1)S(1)} %collective-permute-done.6.refs_4_.refs_7_), channel_id=1, source_target_pairs={{0,1},{1,0},{2,3},{3,2},{4,5},{5,4},{6,7},{7,6},{8,9},{9,8},{10,11... | collective-permute-start | bytes 786440 | tf_op jit(solution)/shard_map/ppermute | solution.py:22
  19.5 6.5 %collective-permute-start.8 = (bf16[128,1024]{1,0:T(8,128)(2,1)S(1)}, bf16[128,1024]{1,0:T(8,128)(2,1)S(1)}, u32[]{:S(2)}, u32[]{:S(2)}) collective-permute-start(bf16[128,1024]{1,0:T(8,128)(2,1)S(1)} %collective-permute-done.2.refs_4_.refs_6_), channel_id=1, source_target_pairs={{0,1},{1,0},{2,3},{3,2},{4,5},{5,4},{6,7},{7,6},{8,9},{9,8},{10,11... | collective-permute-start | bytes 786440 | tf_op jit(solution)/shard_map/ppermute | solution.py:22
  19.6 8.7 %collective-permute-start.5 = (bf16[128,1024]{1,0:T(8,128)(2,1)S(1)}, bf16[128,1024]{1,0:T(8,128)(2,1)S(1)}, u32[]{:S(2)}, u32[]{:S(2)}) collective-permute-start(bf16[128,1024]{1,0:T(8,128)(2,1)S(1)} %collective-permute-done.1.refs_2_.refs_1_), channel_id=1, source_target_pairs={{0,2},{1,3},{2,0},{3,1},{4,6},{5,7},{6,4},{7,5},{8,10},{9,11},{10,... | collective-permute-start | bytes 786440 | tf_op jit(solution)/shard_map/ppermute | solution.py:22
  22.7 5.6 %collective-permute-start.4 = (bf16[128,1024]{1,0:T(8,128)(2,1)S(1)}, bf16[128,1024]{1,0:T(8,128)(2,1)S(1)}, u32[]{:S(2)}, u32[]{:S(2)}) collective-permute-start(bf16[128,1024]{1,0:T(8,128)(2,1)S(1)} %collective-permute-done.3.refs_3_.refs_8_), channel_id=1, source_target_pairs={{0,1},{1,0},{2,3},{3,2},{4,5},{5,4},{6,7},{7,6},{8,9},{9,8},{10,11... | collective-permute-start | bytes 786440 | tf_op jit(solution)/shard_map/ppermute | solution.py:22
  22.7 1.0 %copy-start = (bf16[128,1024]{1,0:T(8,128)(2,1)S(1)}, bf16[128,1024]{1,0:T(8,128)(2,1)}, u32[]{:S(2)}) copy-start(bf16[128,1024]{1,0:T(8,128)(2,1)} %refs_5_.1) | copy-start | bytes 786436
  26.0 2.2 %copy-start.1 = (s32[20]{0:T(128)S(1)}, s32[20]{0:T(128)}, u32[]{:S(2)}) copy-start(s32[20]{0:T(128)} %order_hbm.1) | copy-start | bytes 244
  30.0 4.1 %collective-permute-start.10 = (f32[80,128]{1,0:T(8,128)S(1)}, f32[80,128]{1,0:T(8,128)S(1)}, u32[]{:S(2)}, u32[]{:S(2)}) collective-permute-start(f32[80,128]{1,0:T(8,128)S(1)} %last_sums.1), channel_id=1, source_target_pairs={{0,2},{1,3},{2,0},{3,1},{4,6},{5,7},{6,4},{7,5},{8,10},{9,11},{10,... | collective-permute-start | bytes 122888 | tf_op jit(solution)/shard_map/ppermute | solution.py:22
  34.1 4.9 %collective-permute-start.11 = (f32[80,128]{1,0:T(8,128)S(1)}, f32[80,128]{1,0:T(8,128)S(1)}, u32[]{:S(2)}, u32[]{:S(2)}) collective-permute-start(f32[80,128]{1,0:T(8,128)S(1)} %add.9.conn_ref), channel_id=1, source_target_pairs={{0,16},{1,17},{2,18},{3,19},{4,20},{5,21},{6,22},{7,23},{8,24},{9,... | collective-permute-start | bytes 122888 | tf_op jit(solution)/shard_map/ppermute | solution.py:22
  39.9 3.2 %collective-permute-start.12 = (f32[20,128]{1,0:T(8,128)S(1)}, f32[20,128]{1,0:T(8,128)S(1)}, u32[]{:S(2)}, u32[]{:S(2)}) collective-permute-start(f32[20,128]{1,0:T(8,128)S(1)} %get-tuple-element.8), channel_id=1, source_target_pairs={{0,9},{1,8},{2,11},{3,10},{4,13},{5,12},{6,15},{7,14},{8,1},{9,0},... | collective-permute-start | bytes 30728 | tf_op jit(solution)/shard_map/ppermute | solution.py:22
  43.1 3.1 %collective-permute-start.13 = (f32[20,128]{1,0:T(8,128)S(1)}, f32[20,128]{1,0:T(8,128)S(1)}, u32[]{:S(2)}, u32[]{:S(2)}) collective-permute-start(f32[20,128]{1,0:T(8,128)S(1)} %add.10), channel_id=1, source_target_pairs={{0,5},{1,4},{2,7},{3,6},{4,1},{5,0},{6,3},{7,2},{8,13},{9,12},{10,... | collective-permute-start | bytes 30728 | tf_op jit(solution)/shard_map/ppermute | solution.py:22
  46.2 1.2 %collective-permute-start.14 = (f32[20,128]{1,0:T(8,128)S(1)}, f32[20,128]{1,0:T(8,128)S(1)}, u32[]{:S(2)}, u32[]{:S(2)}) collective-permute-start(f32[20,128]{1,0:T(8,128)S(1)} %add.11.hist_ref), channel_id=1, source_target_pairs={{0,1},{1,0},{2,3},{3,2},{4,5},{5,4},{6,7},{7,6},{8,9},{9,8},{10,11... | collective-permute-start | bytes 30728 | tf_op jit(solution)/shard_map/ppermute | solution.py:22

commit v5 on v4

--- a/solution.py
+++ b/solution.py
@@ -253,11 +253,15 @@
     panel_bits = [mask & ~core for mask in panel_masks]
 
     relayed = [k for k in partner if bin(k & ~core).count("1") > 1]
+    near = [k for k in keys if not k & far]
     waves = [
         ([0], [0]),
-        (front, [core] + sides),
-        (front[1:], [0]),
-        (front, [k ^ core for k in sides] + [low, low ^ core]),
+        (near, [core]),
+        (near[1:], [0]),
+        (near, sides),
+        ([far], [0, core] + sides),
+        (front, [low]),
+        (front, [k ^ core for k in sides] + [low ^ core]),
         (front, [k for k in relayed if not k & core]),
         (front, [k for k in relayed if k & core][:-1]),
     ]
@@ -268,18 +272,18 @@
         done.append(power_sums([panel[k] for k in panels], [partner[k] for k in partners], powers))
         for i, k in enumerate(panels):
             parts[k].append((n, i))
-    everyone = list(partner)
+    everyone = [k for k in partner if k != tail]
     early, late = everyone[CHUNK:], everyone[:CHUNK]
     if early:
         done.append(power_sums([panel[k] for k in rear], [partner[k] for k in early], powers))
     for i, k in enumerate(rear):
         parts[k] += [(len(done) - 1, i)] * bool(early) + [(REAR, i)]
-    for i, k in enumerate(front):
+    for i, k in enumerate(front + rear):
         parts[k].append((FRONT, i))
     conn = last_sums(
         panel_bits,
         power_order,
-        [panel[k] for k in front],
+        [panel[k] for k in front + rear],
         partner[tail],
         [panel[k] for k in rear],
         [partner[k] for k in late],

time: 48.2 us -> 48.2 us (level)
  waiting for transfers between devices: 23.7 us -> 22.3 us
  starting transfers between devices: 15 us -> 15.7 us
  Pallas kernels: 7.06 us -> 7.73 us
    ppermute x15, waiting for transfers between devices: 23.7 us -> 22.3 us  [swap(): return lax.ppermute(x, AXES, [(i, i ^ mask) for i in range(count)])]
    pallas_call x5 -> x8, Pallas kernels: 3.7 us -> 4.4 us  [power_sums(): pl.pallas_call(functools.partial(power_kernel, len(panels)), out_shape=ja...]
    ppermute x15, starting transfers between devices: 15 us -> 15.7 us  [swap(): return lax.ppermute(x, AXES, [(i, i ^ mask) for i in range(count)])]
  transfers between devices with their start and end apart: 15 -> 15, of which waited for: 9 -> 9; matrix products, arithmetic and copies ran while one was open for 1% -> 1% of each run, Pallas kernels for 8% -> 9%
where the time goes in v5:
time: 48.2 us; the launch traced here: 48.1 us
  waiting for transfers between devices  22.3 us (46%)
  starting transfers between devices  15.7 us (33%)
  Pallas kernels  7.73 us (16%)
  local copies, waits for them, and re-layouts  1.56 us (3%)
  between operations  0.75 us (2%)
    ppermute x15, waiting for transfers between devices, swap(): return lax.ppermute(x, AXES, [(i, i ^ mask) for i in range(count)])  22.3 us
    ppermute x15, starting transfers between devices, swap(): return lax.ppermute(x, AXES, [(i, i ^ mask) for i in range(count)])  15.7 us
    pallas_call x8, Pallas kernels, power_sums(): pl.pallas_call(functools.partial(power_kernel, len(panels)), out_shape=ja...  4.4 us
    pallas_call x1, Pallas kernels, last_sums(): pl.pallas_call(functools.partial(last_kernel, panel_bits, len(front), len...  1.73 us
    unnamed x5, local copies, waits for them, and re-layouts  1.56 us
  transfers between devices with their start and end apart: 15, of which 9 were waited for; matrix products, arithmetic and copies ran while one was open for 1% of the time, Pallas kernels for 9%

profile of v5, /device:TPU:0, one launch (start us, length us, event | category | flops | bytes accessed | tf_op | source)
XLA Modules:
  0.0 48.1 jit_solution(11418666167363157485)
XLA Ops:
  0.6 3.1 %collective-permute-start.3 = (bf16[128,1024]{1,0:T(8,128)(2,1)}, bf16[128,1024]{1,0:T(8,128)(2,1)S(1)}, u32[]{:S(2)}, u32[]{:S(2)}) collective-permute-start(bf16[128,1024]{1,0:T(8,128)(2,1)} %refs_6_.1), channel_id=1, source_target_pairs={{0,8},{1,9},{2,10},{3,11},{4,12},{5,13},{6,14},{7,15},{8,0},{9,1},... | collective-permute-start | bytes 786440 | tf_op jit(solution)/shard_map/ppermute | solution.py:22
  3.7 1.5 %collective-permute-start.6 = (bf16[128,1024]{1,0:T(8,128)(2,1)}, bf16[128,1024]{1,0:T(8,128)(2,1)S(1)}, u32[]{:S(2)}, u32[]{:S(2)}) collective-permute-start(bf16[128,1024]{1,0:T(8,128)(2,1)} %refs_6_.1), channel_id=1, source_target_pairs={{0,4},{1,5},{2,6},{3,7},{4,0},{5,1},{6,2},{7,3},{8,12},{9,13},{10,... | collective-permute-start | bytes 786440 | tf_op jit(solution)/shard_map/ppermute | solution.py:22
  5.3 2.6 %collective-permute-start.1 = (bf16[128,1024]{1,0:T(8,128)(2,1)}, bf16[128,1024]{1,0:T(8,128)(2,1)S(1)}, u32[]{:S(2)}, u32[]{:S(2)}) collective-permute-start(bf16[128,1024]{1,0:T(8,128)(2,1)} %refs_6_.1), channel_id=1, source_target_pairs={{0,16},{1,17},{2,18},{3,19},{4,20},{5,21},{6,22},{7,23},{8,24},{9,... | collective-permute-start | bytes 786440 | tf_op jit(solution)/shard_map/ppermute | solution.py:22
  7.9 1.5 %collective-permute-start = (bf16[128,1024]{1,0:T(8,128)(2,1)}, bf16[128,1024]{1,0:T(8,128)(2,1)S(1)}, u32[]{:S(2)}, u32[]{:S(2)}) collective-permute-start(bf16[128,1024]{1,0:T(8,128)(2,1)} %refs_6_.1), channel_id=1, source_target_pairs={{0,2},{1,3},{2,0},{3,1},{4,6},{5,7},{6,4},{7,5},{8,10},{9,11},{10,... | collective-permute-start | bytes 786440 | tf_op jit(solution)/shard_map/ppermute | solution.py:22
  9.3 5.2 %collective-permute-done.3.refs_3_.refs_7_ = bf16[128,1024]{1,0:T(8,128)(2,1)S(1)} collective-permute-done((bf16[128,1024]{1,0:T(8,128)(2,1)}, bf16[128,1024]{1,0:T(8,128)(2,1)S(1)}, u32[]{:S(2)}, u32[]{:S(2)}) %collective-permute-start.3) | collective-permute-done | bytes 262176 | tf_op jit(solution)/shard_map/ppermute | solution.py:22
  14.5 2.7 %collective-permute-start.4 = (bf16[128,1024]{1,0:T(8,128)(2,1)S(1)}, bf16[128,1024]{1,0:T(8,128)(2,1)S(1)}, u32[]{:S(2)}, u32[]{:S(2)}) collective-permute-start(bf16[128,1024]{1,0:T(8,128)(2,1)S(1)} %collective-permute-done.3.refs_3_.refs_7_), channel_id=1, source_target_pairs={{0,4},{1,5},{2,6},{3,7},{4,0},{5,1},{6,2},{7,3},{8,12},{9,13},{10,... | collective-permute-start | bytes 786440 | tf_op jit(solution)/shard_map/ppermute | solution.py:22
  17.2 0.0 collective-permute-start.7
  17.2 0.0 collective-permute-done.6.refs_2_.refs_3_.refs_8_
  17.2 0.5 %collective-permute-start.9 = (bf16[128,1024]{1,0:T(8,128)(2,1)S(1)}, bf16[128,1024]{1,0:T(8,128)(2,1)S(1)}, u32[]{:S(2)}, u32[]{:S(2)}) collective-permute-start(bf16[128,1024]{1,0:T(8,128)(2,1)S(1)} %collective-permute-done.6.refs_2_.refs_3_.refs_8_), channel_id=1, source_target_pairs={{0,1},{1,0},{2,3},{3,2},{4,5},{5,4},{6,7},{7,6},{8,9},{9,8},{10,11... | collective-permute-start | bytes 786440 | tf_op jit(solution)/shard_map/ppermute | solution.py:22
  17.7 1.8 %collective-permute-done.1.refs_0_.refs_2_ = bf16[128,1024]{1,0:T(8,128)(2,1)S(1)} collective-permute-done((bf16[128,1024]{1,0:T(8,128)(2,1)}, bf16[128,1024]{1,0:T(8,128)(2,1)S(1)}, u32[]{:S(2)}, u32[]{:S(2)}) %collective-permute-start.1) | collective-permute-done | bytes 262176 | tf_op jit(solution)/shard_map/ppermute | solution.py:22
  19.5 0.0 collective-permute-start.8
  19.5 0.0 collective-permute-done.refs_1_.refs_0_
  19.6 1.5 %collective-permute-start.2 = (bf16[128,1024]{1,0:T(8,128)(2,1)S(1)}, bf16[128,1024]{1,0:T(8,128)(2,1)S(1)}, u32[]{:S(2)}, u32[]{:S(2)}) collective-permute-start(bf16[128,1024]{1,0:T(8,128)(2,1)S(1)} %collective-permute-done.1.refs_0_.refs_2_), channel_id=1, source_target_pairs={{0,2},{1,3},{2,0},{3,1},{4,6},{5,7},{6,4},{7,5},{8,10},{9,11},{10,... | collective-permute-start | bytes 786440 | tf_op jit(solution)/shard_map/ppermute | solution.py:22
  21.0 1.6 %collective-permute-done.4.refs_3_.refs_9_ = bf16[128,1024]{1,0:T(8,128)(2,1)S(1)} collective-permute-done((bf16[128,1024]{1,0:T(8,128)(2,1)S(1)}, bf16[128,1024]{1,0:T(8,128)(2,1)S(1)}, u32[]{:S(2)}, u32[]{:S(2)}) %collective-permute-start.4) | collective-permute-done | bytes 262176 | tf_op jit(solution)/shard_map/ppermute | solution.py:22
  22.7 0.0 collective-permute-start.5
  22.7 0.0 copy-start
  22.7 0.9 %copy-done = bf16[128,1024]{1,0:T(8,128)(2,1)S(1)} copy-done((bf16[128,1024]{1,0:T(8,128)(2,1)S(1)}, bf16[128,1024]{1,0:T(8,128)(2,1)}, u32[]{:S(2)}) %copy-start) | copy-done | bytes 262168
  23.6 0.3 power_sums.8.refs_13_
  23.9 0.3 power_sums.10.refs_15_
  24.2 0.5 %power_sums.11.refs_16_ = f32[2,20,128]{2,1,0:T(8,128)S(1)} custom-call(bf16[128,1024]{1,0:T(8,128)(2,1)S(1)} %copy-done, bf16[128,1024]{1,0:T(8,128)(2,1)S(1)} %collective-permute-done.refs_1_.refs_0_, bf16[128,1024]{1,0:T(8,128)(2,1)S(1)} %collective-permute-done.6.refs_2_.refs_3_.refs_8_), custom_call_target="tpu_custom_call" | custom-call | flops 67108864 | tf_op jit(solution)/shard_map/power_sums/pallas_call | solution.py:94
  24.7 0.0 collective-permute-done.7.refs_2_.refs_10_
  24.8 0.5 %power_sums.9.refs_14_ = f32[2,20,128]{2,1,0:T(8,128)S(1)} custom-call(bf16[128,1024]{1,0:T(8,128)(2,1)S(1)} %copy-done, bf16[128,1024]{1,0:T(8,128)(2,1)S(1)} %collective-permute-done.refs_1_.refs_0_, bf16[128,1024]{1,0:T(8,128)(2,1)S(1)} %collective-permute-done.7.refs_2_.refs_10_), custom_call_target="tpu_custom_call" | custom-call | flops 67108864 | tf_op jit(solution)/shard_map/power_sums/pallas_call | solution.py:94
  25.2 0.6 %power_sums.12.refs_17_ = f32[1,20,128]{2,1,0:T(8,128)S(1)} custom-call(bf16[128,1024]{1,0:T(8,128)(2,1)S(1)} %collective-permute-done.1.refs_0_.refs_2_, bf16[128,1024]{1,0:T(8,128)(2,1)S(1)} %copy-done, bf16[128,1024]{1,0:T(8,128)(2,1)S(1)} %collective-permute-done.7.refs_2_.refs_10_, bf16[128,1024]{1,0:T(8,128)(2,1)S(1)} %collective-permute-done.6.refs_2_.refs_3_.refs_8_), custom_call_target="tpu_custom_call" | custom-call | flops 100663296 | tf_op jit(solution)/shard_map/power_sums/pallas_call | solution.py:94
  25.8 0.7 %power_sums.13.refs_18_ = f32[3,20,128]{2,1,0:T(8,128)S(1)} custom-call(bf16[128,1024]{1,0:T(8,128)(2,1)S(1)} %copy-done, bf16[128,1024]{1,0:T(8,128)(2,1)S(1)} %collective-permute-done.refs_1_.refs_0_, bf16[128,1024]{1,0:T(8,128)(2,1)S(1)} %collective-permute-done.1.refs_0_.refs_2_, bf16[128,1024]{1,0:T(8,128)(2,1)S(1)} %collective-permute-done.3.refs_3_.refs_7_), custom_call_target="tpu_custom_call" | custom-call | flops 100663296 | tf_op jit(solution)/shard_map/power_sums/pallas_call | solution.py:94
  26.5 0.7 %power_sums.15.refs_20_ = f32[3,20,128]{2,1,0:T(8,128)S(1)} custom-call(bf16[128,1024]{1,0:T(8,128)(2,1)S(1)} %copy-done, bf16[128,1024]{1,0:T(8,128)(2,1)S(1)} %collective-permute-done.refs_1_.refs_0_, bf16[128,1024]{1,0:T(8,128)(2,1)S(1)} %collective-permute-done.1.refs_0_.refs_2_, bf16[128,1024]{1,0:T(8,128)(2,1)S(1)} %collective-permute-done.4.refs_3_.refs_9_), custom_call_target="tpu_custom_call" | custom-call | flops 100663296 | tf_op jit(solution)/shard_map/power_sums/pallas_call | solution.py:94
  27.1 0.0 copy-start.1
  27.1 0.0 collective-permute-done.9.refs_3_.refs_12_
  27.2 0.0 collective-permute-done.8.refs_4_.refs_11_
  27.2 0.9 %power_sums.14.refs_19_ = f32[3,20,128]{2,1,0:T(8,128)S(1)} custom-call(bf16[128,1024]{1,0:T(8,128)(2,1)S(1)} %copy-done, bf16[128,1024]{1,0:T(8,128)(2,1)S(1)} %collective-permute-done.refs_1_.refs_0_, bf16[128,1024]{1,0:T(8,128)(2,1)S(1)} %collective-permute-done.1.refs_0_.refs_2_, bf16[128,1024]{1,0:T(8,128)(2,1)S(1)} %collective-permute-done.9.refs_3_.refs_12_, ...), custom_call_target="tpu_custom_call" | custom-call | flops 201326592 | tf_op jit(solution)/shard_map/power_sums/pallas_call | solution.py:94
  28.1 0.2 collective-permute-done.2.refs_3_.refs_5_
  28.3 0.0 collective-permute-done.5.refs_4_
  28.3 0.0 copy-done.1
  28.3 1.7 %last_sums.1 = f32[80,128]{1,0:T(8,128)S(1)} custom-call(s32[20]{0:T(128)S(1)} %copy-done.1, bf16[128,1024]{1,0:T(8,128)(2,1)S(1)} %copy-done, bf16[128,1024]{1,0:T(8,128)(2,1)S(1)} %collective-permute-done.refs_1_.refs_0_, bf16[128,1024]{1,0:T(8,128)(2,1)S(1)} %collective-permute-done.1.refs_0_.refs_2_, ...), custom_call_target="tpu_custom_call" | custom-call | flops 234881024 | tf_op jit(solution)/shard_map/last_sums/pallas_call | solution.py:141
  30.0 1.6 %collective-permute-start.10 = (f32[80,128]{1,0:T(8,128)S(1)}, f32[80,128]{1,0:T(8,128)S(1)}, u32[]{:S(2)}, u32[]{:S(2)}) collective-permute-start(f32[80,128]{1,0:T(8,128)S(1)} %last_sums.1), channel_id=1, source_target_pairs={{0,2},{1,3},{2,0},{3,1},{4,6},{5,7},{6,4},{7,5},{8,10},{9,11},{10,... | collective-permute-start | bytes 122888 | tf_op jit(solution)/shard_map/ppermute | solution.py:22
  31.6 2.5 %collective-permute-done.10 = f32[80,128]{1,0:T(8,128)S(1)} collective-permute-done((f32[80,128]{1,0:T(8,128)S(1)}, f32[80,128]{1,0:T(8,128)S(1)}, u32[]{:S(2)}, u32[]{:S(2)}) %collective-permute-start.10) | collective-permute-done | bytes 40992 | tf_op jit(solution)/shard_map/ppermute | solution.py:22
  34.1 0.5 %collective-permute-start.11 = (f32[80,128]{1,0:T(8,128)S(1)}, f32[80,128]{1,0:T(8,128)S(1)}, u32[]{:S(2)}, u32[]{:S(2)}) collective-permute-start(f32[80,128]{1,0:T(8,128)S(1)} %add.9.conn_ref), channel_id=1, source_target_pairs={{0,16},{1,17},{2,18},{3,19},{4,20},{5,21},{6,22},{7,23},{8,24},{9,... | collective-permute-start | bytes 122888 | tf_op jit(solution)/shard_map/ppermute | solution.py:22
  34.6 4.4 %collective-permute-done.11.other_ref = f32[80,128]{1,0:T(8,128)S(1)} collective-permute-done((f32[80,128]{1,0:T(8,128)S(1)}, f32[80,128]{1,0:T(8,128)S(1)}, u32[]{:S(2)}, u32[]{:S(2)}) %collective-permute-start.11) | collective-permute-done | bytes 40992 | tf_op jit(solution)/shard_map/ppermute | solution.py:22
  39.0 0.9 %histogram.1 = (f32[20,128]{1,0:T(8,128)S(1)}, f32[20,128]{1,0:T(8,128)S(1)}) custom-call(f32[80,128]{1,0:T(8,128)S(1)} %add.9.conn_ref, f32[80,128]{1,0:T(8,128)S(1)} %collective-permute-done.11.other_ref), custom_call_target="tpu_custom_call" | custom-call | tf_op jit(solution)/shard_map/histogram/pallas_call | solution.py:187
  39.9 0.0 collective-permute-start.12
  39.9 3.1 %collective-permute-done.12 = f32[20,128]{1,0:T(8,128)S(1)} collective-permute-done((f32[20,128]{1,0:T(8,128)S(1)}, f32[20,128]{1,0:T(8,128)S(1)}, u32[]{:S(2)}, u32[]{:S(2)}) %collective-permute-start.12) | collective-permute-done | bytes 10272 | tf_op jit(solution)/shard_map/ppermute | solution.py:22
  43.0 0.0 collective-permute-start.13
  43.0 3.1 %collective-permute-done.13 = f32[20,128]{1,0:T(8,128)S(1)} collective-permute-done((f32[20,128]{1,0:T(8,128)S(1)}, f32[20,128]{1,0:T(8,128)S(1)}, u32[]{:S(2)}, u32[]{:S(2)}) %collective-permute-start.13) | collective-permute-done | bytes 10272 | tf_op jit(solution)/shard_map/ppermute | solution.py:22
  46.2 0.1 collective-permute-start.14
  46.3 0.6 %copy.5 = f32[128,20]{0,1:T(8,128)} copy(f32[128,20]{0,1:T(8,128)S(1)} %bitcast.1) | data formatting | bytes 20480
  46.9 0.5 collective-permute-done.14.other_ref
  47.4 0.7 %scale_free_fit.1 = (f32[20]{0:T(128)}, f32[20]{0:T(128)}) custom-call(f32[20,128]{1,0:T(8,128)S(1)} %add.11.hist_ref, f32[20,128]{1,0:T(8,128)S(1)} %collective-permute-done.14.other_ref), custom_call_target="tpu_custom_call" | custom-call | tf_op jit(solution)/shard_map/scale_free_fit/pallas_call | solution.py:228
  (3 shorter events, 0.0 us)
Async XLA Ops:
  0.6 13.9 %collective-permute-start.3 = (bf16[128,1024]{1,0:T(8,128)(2,1)}, bf16[128,1024]{1,0:T(8,128)(2,1)S(1)}, u32[]{:S(2)}, u32[]{:S(2)}) collective-permute-start(bf16[128,1024]{1,0:T(8,128)(2,1)} %refs_6_.1), channel_id=1, source_target_pairs={{0,8},{1,9},{2,10},{3,11},{4,12},{5,13},{6,14},{7,15},{8,0},{9,1},... | collective-permute-start | bytes 786440 | tf_op jit(solution)/shard_map/ppermute | solution.py:22
  3.7 13.5 %collective-permute-start.6 = (bf16[128,1024]{1,0:T(8,128)(2,1)}, bf16[128,1024]{1,0:T(8,128)(2,1)S(1)}, u32[]{:S(2)}, u32[]{:S(2)}) collective-permute-start(bf16[128,1024]{1,0:T(8,128)(2,1)} %refs_6_.1), channel_id=1, source_target_pairs={{0,4},{1,5},{2,6},{3,7},{4,0},{5,1},{6,2},{7,3},{8,12},{9,13},{10,... | collective-permute-start | bytes 786440 | tf_op jit(solution)/shard_map/ppermute | solution.py:22
  5.3 14.3 %collective-permute-start.1 = (bf16[128,1024]{1,0:T(8,128)(2,1)}, bf16[128,1024]{1,0:T(8,128)(2,1)S(1)}, u32[]{:S(2)}, u32[]{:S(2)}) collective-permute-start(bf16[128,1024]{1,0:T(8,128)(2,1)} %refs_6_.1), channel_id=1, source_target_pairs={{0,16},{1,17},{2,18},{3,19},{4,20},{5,21},{6,22},{7,23},{8,24},{9,... | collective-permute-start | bytes 786440 | tf_op jit(solution)/shard_map/ppermute | solution.py:22
  7.9 11.7 %collective-permute-start = (bf16[128,1024]{1,0:T(8,128)(2,1)}, bf16[128,1024]{1,0:T(8,128)(2,1)S(1)}, u32[]{:S(2)}, u32[]{:S(2)}) collective-permute-start(bf16[128,1024]{1,0:T(8,128)(2,1)} %refs_6_.1), channel_id=1, source_target_pairs={{0,2},{1,3},{2,0},{3,1},{4,6},{5,7},{6,4},{7,5},{8,10},{9,11},{10,... | collective-permute-start | bytes 786440 | tf_op jit(solution)/shard_map/ppermute | solution.py:22
  14.5 8.1 %collective-permute-start.4 = (bf16[128,1024]{1,0:T(8,128)(2,1)S(1)}, bf16[128,1024]{1,0:T(8,128)(2,1)S(1)}, u32[]{:S(2)}, u32[]{:S(2)}) collective-permute-start(bf16[128,1024]{1,0:T(8,128)(2,1)S(1)} %collective-permute-done.3.refs_3_.refs_7_), channel_id=1, source_target_pairs={{0,4},{1,5},{2,6},{3,7},{4,0},{5,1},{6,2},{7,3},{8,12},{9,13},{10,... | collective-permute-start | bytes 786440 | tf_op jit(solution)/shard_map/ppermute | solution.py:22
  17.2 7.5 %collective-permute-start.7 = (bf16[128,1024]{1,0:T(8,128)(2,1)}, bf16[128,1024]{1,0:T(8,128)(2,1)S(1)}, u32[]{:S(2)}, u32[]{:S(2)}) collective-permute-start(bf16[128,1024]{1,0:T(8,128)(2,1)} %refs_6_.1), channel_id=1, source_target_pairs={{0,1},{1,0},{2,3},{3,2},{4,5},{5,4},{6,7},{7,6},{8,9},{9,8},{10,11... | collective-permute-start | bytes 786440 | tf_op jit(solution)/shard_map/ppermute | solution.py:22
  17.2 9.9 %collective-permute-start.9 = (bf16[128,1024]{1,0:T(8,128)(2,1)S(1)}, bf16[128,1024]{1,0:T(8,128)(2,1)S(1)}, u32[]{:S(2)}, u32[]{:S(2)}) collective-permute-start(bf16[128,1024]{1,0:T(8,128)(2,1)S(1)} %collective-permute-done.6.refs_2_.refs_3_.refs_8_), channel_id=1, source_target_pairs={{0,1},{1,0},{2,3},{3,2},{4,5},{5,4},{6,7},{7,6},{8,9},{9,8},{10,11... | collective-permute-start | bytes 786440 | tf_op jit(solution)/shard_map/ppermute | solution.py:22
  19.5 7.6 %collective-permute-start.8 = (bf16[128,1024]{1,0:T(8,128)(2,1)S(1)}, bf16[128,1024]{1,0:T(8,128)(2,1)S(1)}, u32[]{:S(2)}, u32[]{:S(2)}) collective-permute-start(bf16[128,1024]{1,0:T(8,128)(2,1)S(1)} %collective-permute-done.3.refs_3_.refs_7_), channel_id=1, source_target_pairs={{0,1},{1,0},{2,3},{3,2},{4,5},{5,4},{6,7},{7,6},{8,9},{9,8},{10,11... | collective-permute-start | bytes 786440 | tf_op jit(solution)/shard_map/ppermute | solution.py:22
  19.6 8.7 %collective-permute-start.2 = (bf16[128,1024]{1,0:T(8,128)(2,1)S(1)}, bf16[128,1024]{1,0:T(8,128)(2,1)S(1)}, u32[]{:S(2)}, u32[]{:S(2)}) collective-permute-start(bf16[128,1024]{1,0:T(8,128)(2,1)S(1)} %collective-permute-done.1.refs_0_.refs_2_), channel_id=1, source_target_pairs={{0,2},{1,3},{2,0},{3,1},{4,6},{5,7},{6,4},{7,5},{8,10},{9,11},{10,... | collective-permute-start | bytes 786440 | tf_op jit(solution)/shard_map/ppermute | solution.py:22
  22.7 5.6 %collective-permute-start.5 = (bf16[128,1024]{1,0:T(8,128)(2,1)S(1)}, bf16[128,1024]{1,0:T(8,128)(2,1)S(1)}, u32[]{:S(2)}, u32[]{:S(2)}) collective-permute-start(bf16[128,1024]{1,0:T(8,128)(2,1)S(1)} %collective-permute-done.4.refs_3_.refs_9_), channel_id=1, source_target_pairs={{0,1},{1,0},{2,3},{3,2},{4,5},{5,4},{6,7},{7,6},{8,9},{9,8},{10,11... | collective-permute-start | bytes 786440 | tf_op jit(solution)/shard_map/ppermute | solution.py:22
  22.7 1.0 %copy-start = (bf16[128,1024]{1,0:T(8,128)(2,1)S(1)}, bf16[128,1024]{1,0:T(8,128)(2,1)}, u32[]{:S(2)}) copy-start(bf16[128,1024]{1,0:T(8,128)(2,1)} %refs_6_.1) | copy-start | bytes 786436
  27.1 1.1 %copy-start.1 = (s32[20]{0:T(128)S(1)}, s32[20]{0:T(128)}, u32[]{:S(2)}) copy-start(s32[20]{0:T(128)} %order_hbm.1) | copy-start | bytes 244
  30.0 4.1 %collective-permute-start.10 = (f32[80,128]{1,0:T(8,128)S(1)}, f32[80,128]{1,0:T(8,128)S(1)}, u32[]{:S(2)}, u32[]{:S(2)}) collective-permute-start(f32[80,128]{1,0:T(8,128)S(1)} %last_sums.1), channel_id=1, source_target_pairs={{0,2},{1,3},{2,0},{3,1},{4,6},{5,7},{6,4},{7,5},{8,10},{9,11},{10,... | collective-permute-start | bytes 122888 | tf_op jit(solution)/shard_map/ppermute | solution.py:22
  34.1 4.9 %collective-permute-start.11 = (f32[80,128]{1,0:T(8,128)S(1)}, f32[80,128]{1,0:T(8,128)S(1)}, u32[]{:S(2)}, u32[]{:S(2)}) collective-permute-start(f32[80,128]{1,0:T(8,128)S(1)} %add.9.conn_ref), channel_id=1, source_target_pairs={{0,16},{1,17},{2,18},{3,19},{4,20},{5,21},{6,22},{7,23},{8,24},{9,... | collective-permute-start | bytes 122888 | tf_op jit(solution)/shard_map/ppermute | solution.py:22
  39.9 3.2 %collective-permute-start.12 = (f32[20,128]{1,0:T(8,128)S(1)}, f32[20,128]{1,0:T(8,128)S(1)}, u32[]{:S(2)}, u32[]{:S(2)}) collective-permute-start(f32[20,128]{1,0:T(8,128)S(1)} %get-tuple-element.8), channel_id=1, source_target_pairs={{0,9},{1,8},{2,11},{3,10},{4,13},{5,12},{6,15},{7,14},{8,1},{9,0},... | collective-permute-start | bytes 30728 | tf_op jit(solution)/shard_map/ppermute | solution.py:22
  43.0 3.1 %collective-permute-start.13 = (f32[20,128]{1,0:T(8,128)S(1)}, f32[20,128]{1,0:T(8,128)S(1)}, u32[]{:S(2)}, u32[]{:S(2)}) collective-permute-start(f32[20,128]{1,0:T(8,128)S(1)} %add.10), channel_id=1, source_target_pairs={{0,5},{1,4},{2,7},{3,6},{4,1},{5,0},{6,3},{7,2},{8,13},{9,12},{10,... | collective-permute-start | bytes 30728 | tf_op jit(solution)/shard_map/ppermute | solution.py:22
  46.2 1.2 %collective-permute-start.14 = (f32[20,128]{1,0:T(8,128)S(1)}, f32[20,128]{1,0:T(8,128)S(1)}, u32[]{:S(2)}, u32[]{:S(2)}) collective-permute-start(f32[20,128]{1,0:T(8,128)S(1)} %add.11.hist_ref), channel_id=1, source_target_pairs={{0,1},{1,0},{2,3},{3,2},{4,5},{5,4},{6,7},{7,6},{8,9},{9,8},{10,11... | collective-permute-start | bytes 30728 | tf_op jit(solution)/shard_map/ppermute | solution.py:22

commit v6 on v4

--- a/solution.py
+++ b/solution.py
@@ -119,10 +119,14 @@
     fetch = pltpu.make_async_copy(order_hbm, order, arrived)
     fetch.start()
     mine = own_slot(panel_bits)
+    for i, where in enumerate(parts):
+        values = [part_refs[a][b] for a, b in where if a >= 0]
+        if values:
+            natural[i] = functools.reduce(jnp.add, values)
     add_powers(front_refs, [tail_ref], front_total)
     add_powers(refs[:n_panel], refs[n_panel : n_panel + n_partner], total_ref)
     for i, where in enumerate(parts):
-        values = [part_refs[a][b] for a, b in where if a >= 0]
+        values = [natural[i]] if any(a >= 0 for a, _ in where) else []
         values += [jnp.sum(front_total[b], axis=1) for a, b in where if a == FRONT]
         values += [jnp.sum(total_ref[b], axis=1) for a, b in where if a == REAR]
         natural[i] = functools.reduce(jnp.add, values)
@@ -207,13 +211,13 @@
     def total(x):
         return jnp.sum(x, axis=1, keepdims=True)
 
-    weight_sum = total(hist)
+    share = 1.0 / total(hist)
     ylog = jnp.log(hist + 1.0) - log_total
-    xdev = centers - total(hist * centers) / weight_sum
-    ydev = ylog - total(hist * ylog) / weight_sum
-    sxx = jnp.maximum(total(hist * xdev * xdev) / weight_sum, 0.05)
-    syy = jnp.maximum(total(hist * ydev * ydev) / weight_sum, 0.05)
-    sxy = total(hist * xdev * ydev) / weight_sum
+    xdev = centers - total(hist * centers) * share
+    ydev = ylog - total(hist * ylog) * share
+    sxx = jnp.maximum(total(hist * xdev * xdev) * share, 0.05)
+    syy = jnp.maximum(total(hist * ydev * ydev) * share, 0.05)
+    sxy = total(hist * xdev * ydev) * share
     own = lax.broadcasted_iota(jnp.int32, (powers, BINS), 0) == lane
 
     def store(ref, column):

time: 48.2 us -> 48.2 us (level)
  no operation moved by 1% of the time
where the time goes in v6:
time: 48.2 us; the launch traced here: 48.1 us
  waiting for transfers between devices  23.7 us (49%)
  starting transfers between devices  15 us (31%)
  Pallas kernels  7.05 us (15%)
  local copies, waits for them, and re-layouts  1.56 us (3%)
  between operations  0.74 us (2%)
    ppermute x15, waiting for transfers between devices, swap(): return lax.ppermute(x, AXES, [(i, i ^ mask) for i in range(count)])  23.7 us
    ppermute x15, starting transfers between devices, swap(): return lax.ppermute(x, AXES, [(i, i ^ mask) for i in range(count)])  15 us
    pallas_call x5, Pallas kernels, power_sums(): pl.pallas_call(functools.partial(power_kernel, len(panels)), out_shape=ja...  3.7 us
    pallas_call x1, Pallas kernels, last_sums(): pl.pallas_call(functools.partial(last_kernel, panel_bits, len(front), len...  1.75 us
    unnamed x5, local copies, waits for them, and re-layouts  1.56 us
  transfers between devices with their start and end apart: 15, of which 9 were waited for; matrix products, arithmetic and copies ran while one was open for 1% of the time, Pallas kernels for 8%

profile of v6, /device:TPU:0, one launch (start us, length us, event | category | flops | bytes accessed | tf_op | source)
XLA Modules:
  0.0 48.1 jit_solution(10227796029384663945)
XLA Ops:
  0.6 3.1 %collective-permute-start.2 = (bf16[128,1024]{1,0:T(8,128)(2,1)}, bf16[128,1024]{1,0:T(8,128)(2,1)S(1)}, u32[]{:S(2)}, u32[]{:S(2)}) collective-permute-start(bf16[128,1024]{1,0:T(8,128)(2,1)} %refs_5_.1), channel_id=1, source_target_pairs={{0,8},{1,9},{2,10},{3,11},{4,12},{5,13},{6,14},{7,15},{8,0},{9,1},... | collective-permute-start | bytes 786440 | tf_op jit(solution)/shard_map/ppermute | solution.py:22
  3.7 1.5 %collective-permute-start.6 = (bf16[128,1024]{1,0:T(8,128)(2,1)}, bf16[128,1024]{1,0:T(8,128)(2,1)S(1)}, u32[]{:S(2)}, u32[]{:S(2)}) collective-permute-start(bf16[128,1024]{1,0:T(8,128)(2,1)} %refs_5_.1), channel_id=1, source_target_pairs={{0,4},{1,5},{2,6},{3,7},{4,0},{5,1},{6,2},{7,3},{8,12},{9,13},{10,... | collective-permute-start | bytes 786440 | tf_op jit(solution)/shard_map/ppermute | solution.py:22
  5.3 2.6 %collective-permute-start.1 = (bf16[128,1024]{1,0:T(8,128)(2,1)}, bf16[128,1024]{1,0:T(8,128)(2,1)S(1)}, u32[]{:S(2)}, u32[]{:S(2)}) collective-permute-start(bf16[128,1024]{1,0:T(8,128)(2,1)} %refs_5_.1), channel_id=1, source_target_pairs={{0,16},{1,17},{2,18},{3,19},{4,20},{5,21},{6,22},{7,23},{8,24},{9,... | collective-permute-start | bytes 786440 | tf_op jit(solution)/shard_map/ppermute | solution.py:22
  7.9 1.5 %collective-permute-start = (bf16[128,1024]{1,0:T(8,128)(2,1)}, bf16[128,1024]{1,0:T(8,128)(2,1)S(1)}, u32[]{:S(2)}, u32[]{:S(2)}) collective-permute-start(bf16[128,1024]{1,0:T(8,128)(2,1)} %refs_5_.1), channel_id=1, source_target_pairs={{0,2},{1,3},{2,0},{3,1},{4,6},{5,7},{6,4},{7,5},{8,10},{9,11},{10,... | collective-permute-start | bytes 786440 | tf_op jit(solution)/shard_map/ppermute | solution.py:22
  9.3 5.2 %collective-permute-done.2.refs_4_.refs_6_ = bf16[128,1024]{1,0:T(8,128)(2,1)S(1)} collective-permute-done((bf16[128,1024]{1,0:T(8,128)(2,1)}, bf16[128,1024]{1,0:T(8,128)(2,1)S(1)}, u32[]{:S(2)}, u32[]{:S(2)}) %collective-permute-start.2) | collective-permute-done | bytes 262176 | tf_op jit(solution)/shard_map/ppermute | solution.py:22
  14.5 2.7 %collective-permute-start.3 = (bf16[128,1024]{1,0:T(8,128)(2,1)S(1)}, bf16[128,1024]{1,0:T(8,128)(2,1)S(1)}, u32[]{:S(2)}, u32[]{:S(2)}) collective-permute-start(bf16[128,1024]{1,0:T(8,128)(2,1)S(1)} %collective-permute-done.2.refs_4_.refs_6_), channel_id=1, source_target_pairs={{0,4},{1,5},{2,6},{3,7},{4,0},{5,1},{6,2},{7,3},{8,12},{9,13},{10,... | collective-permute-start | bytes 786440 | tf_op jit(solution)/shard_map/ppermute | solution.py:22
  17.2 0.0 collective-permute-start.7
  17.2 0.0 collective-permute-done.6.refs_4_.refs_7_
  17.2 0.5 %collective-permute-start.9 = (bf16[128,1024]{1,0:T(8,128)(2,1)S(1)}, bf16[128,1024]{1,0:T(8,128)(2,1)S(1)}, u32[]{:S(2)}, u32[]{:S(2)}) collective-permute-start(bf16[128,1024]{1,0:T(8,128)(2,1)S(1)} %collective-permute-done.6.refs_4_.refs_7_), channel_id=1, source_target_pairs={{0,1},{1,0},{2,3},{3,2},{4,5},{5,4},{6,7},{7,6},{8,9},{9,8},{10,11... | collective-permute-start | bytes 786440 | tf_op jit(solution)/shard_map/ppermute | solution.py:22
  17.7 1.8 %collective-permute-done.1.refs_2_.refs_1_ = bf16[128,1024]{1,0:T(8,128)(2,1)S(1)} collective-permute-done((bf16[128,1024]{1,0:T(8,128)(2,1)}, bf16[128,1024]{1,0:T(8,128)(2,1)S(1)}, u32[]{:S(2)}, u32[]{:S(2)}) %collective-permute-start.1) | collective-permute-done | bytes 262176 | tf_op jit(solution)/shard_map/ppermute | solution.py:22
  19.5 0.0 collective-permute-start.8
  19.5 0.0 collective-permute-done.refs_1_.refs_0_
  19.6 1.5 %collective-permute-start.5 = (bf16[128,1024]{1,0:T(8,128)(2,1)S(1)}, bf16[128,1024]{1,0:T(8,128)(2,1)S(1)}, u32[]{:S(2)}, u32[]{:S(2)}) collective-permute-start(bf16[128,1024]{1,0:T(8,128)(2,1)S(1)} %collective-permute-done.1.refs_2_.refs_1_), channel_id=1, source_target_pairs={{0,2},{1,3},{2,0},{3,1},{4,6},{5,7},{6,4},{7,5},{8,10},{9,11},{10,... | collective-permute-start | bytes 786440 | tf_op jit(solution)/shard_map/ppermute | solution.py:22
  21.0 1.6 %collective-permute-done.3.refs_3_.refs_8_ = bf16[128,1024]{1,0:T(8,128)(2,1)S(1)} collective-permute-done((bf16[128,1024]{1,0:T(8,128)(2,1)S(1)}, bf16[128,1024]{1,0:T(8,128)(2,1)S(1)}, u32[]{:S(2)}, u32[]{:S(2)}) %collective-permute-start.3) | collective-permute-done | bytes 262176 | tf_op jit(solution)/shard_map/ppermute | solution.py:22
  22.7 0.0 collective-permute-start.4
  22.7 0.0 copy-start
  22.7 0.9 %copy-done = bf16[128,1024]{1,0:T(8,128)(2,1)S(1)} copy-done((bf16[128,1024]{1,0:T(8,128)(2,1)S(1)}, bf16[128,1024]{1,0:T(8,128)(2,1)}, u32[]{:S(2)}) %copy-start) | copy-done | bytes 262168
  23.6 0.3 power_sums.5.refs_13_
  23.9 0.5 %power_sums.7.refs_15_ = f32[2,20,128]{2,1,0:T(8,128)S(1)} custom-call(bf16[128,1024]{1,0:T(8,128)(2,1)S(1)} %collective-permute-done.refs_1_.refs_0_, bf16[128,1024]{1,0:T(8,128)(2,1)S(1)} %collective-permute-done.1.refs_2_.refs_1_, bf16[128,1024]{1,0:T(8,128)(2,1)S(1)} %copy-done), custom_call_target="tpu_custom_call" | custom-call | flops 67108864 | tf_op jit(solution)/shard_map/power_sums/pallas_call | solution.py:94
  24.4 0.0 collective-permute-done.7.refs_3_.refs_9_
  24.4 0.9 %power_sums.6.refs_14_ = f32[3,20,128]{2,1,0:T(8,128)S(1)} custom-call(bf16[128,1024]{1,0:T(8,128)(2,1)S(1)} %copy-done, bf16[128,1024]{1,0:T(8,128)(2,1)S(1)} %collective-permute-done.refs_1_.refs_0_, bf16[128,1024]{1,0:T(8,128)(2,1)S(1)} %collective-permute-done.1.refs_2_.refs_1_, bf16[128,1024]{1,0:T(8,128)(2,1)S(1)} %collective-permute-done.7.refs_3_.refs_9_, ...), custom_call_target="tpu_custom_call" | custom-call | flops 201326592 | tf_op jit(solution)/shard_map/power_sums/pallas_call | solution.py:94
  25.4 0.7 %power_sums.9.refs_17_ = f32[3,20,128]{2,1,0:T(8,128)S(1)} custom-call(bf16[128,1024]{1,0:T(8,128)(2,1)S(1)} %copy-done, bf16[128,1024]{1,0:T(8,128)(2,1)S(1)} %collective-permute-done.refs_1_.refs_0_, bf16[128,1024]{1,0:T(8,128)(2,1)S(1)} %collective-permute-done.1.refs_2_.refs_1_, bf16[128,1024]{1,0:T(8,128)(2,1)S(1)} %collective-permute-done.3.refs_3_.refs_8_), custom_call_target="tpu_custom_call" | custom-call | flops 100663296 | tf_op jit(solution)/shard_map/power_sums/pallas_call | solution.py:94
  26.0 0.0 copy-start.1
  26.1 0.0 collective-permute-done.9.refs_3_.refs_11_
  26.1 0.0 collective-permute-done.8.refs_5_.refs_10_
  26.1 1.3 %power_sums.8.refs_16_ = f32[3,20,128]{2,1,0:T(8,128)S(1)} custom-call(bf16[128,1024]{1,0:T(8,128)(2,1)S(1)} %copy-done, bf16[128,1024]{1,0:T(8,128)(2,1)S(1)} %collective-permute-done.refs_1_.refs_0_, bf16[128,1024]{1,0:T(8,128)(2,1)S(1)} %collective-permute-done.1.refs_2_.refs_1_, bf16[128,1024]{1,0:T(8,128)(2,1)S(1)} %collective-permute-done.9.refs_3_.refs_11_, ...), custom_call_target="tpu_custom_call" | custom-call | flops 301989888 | tf_op jit(solution)/shard_map/power_sums/pallas_call | solution.py:94
  27.4 0.9 %collective-permute-done.5.refs_4_ = bf16[128,1024]{1,0:T(8,128)(2,1)S(1)} collective-permute-done((bf16[128,1024]{1,0:T(8,128)(2,1)S(1)}, bf16[128,1024]{1,0:T(8,128)(2,1)S(1)}, u32[]{:S(2)}, u32[]{:S(2)}) %collective-permute-start.5) | collective-permute-done | bytes 262176 | tf_op jit(solution)/shard_map/ppermute | solution.py:22
  28.3 0.0 collective-permute-done.4.refs_3_.refs_12_
  28.3 0.0 copy-done.1
  28.3 1.8 %last_sums.1 = f32[80,128]{1,0:T(8,128)S(1)} custom-call(s32[20]{0:T(128)S(1)} %copy-done.1, bf16[128,1024]{1,0:T(8,128)(2,1)S(1)} %copy-done, bf16[128,1024]{1,0:T(8,128)(2,1)S(1)} %collective-permute-done.refs_1_.refs_0_, bf16[128,1024]{1,0:T(8,128)(2,1)S(1)} %collective-permute-done.1.refs_2_.refs_1_, ...), custom_call_target="tpu_custom_call" | custom-call | flops 268435456 | tf_op jit(solution)/shard_map/last_sums/pallas_call | solution.py:145
  30.0 1.6 %collective-permute-start.10 = (f32[80,128]{1,0:T(8,128)S(1)}, f32[80,128]{1,0:T(8,128)S(1)}, u32[]{:S(2)}, u32[]{:S(2)}) collective-permute-start(f32[80,128]{1,0:T(8,128)S(1)} %last_sums.1), channel_id=1, source_target_pairs={{0,2},{1,3},{2,0},{3,1},{4,6},{5,7},{6,4},{7,5},{8,10},{9,11},{10,... | collective-permute-start | bytes 122888 | tf_op jit(solution)/shard_map/ppermute | solution.py:22
  31.6 2.5 %collective-permute-done.10 = f32[80,128]{1,0:T(8,128)S(1)} collective-permute-done((f32[80,128]{1,0:T(8,128)S(1)}, f32[80,128]{1,0:T(8,128)S(1)}, u32[]{:S(2)}, u32[]{:S(2)}) %collective-permute-start.10) | collective-permute-done | bytes 40992 | tf_op jit(solution)/shard_map/ppermute | solution.py:22
  34.1 0.0 collective-permute-start.11
  34.1 4.9 %collective-permute-done.11.other_ref = f32[80,128]{1,0:T(8,128)S(1)} collective-permute-done((f32[80,128]{1,0:T(8,128)S(1)}, f32[80,128]{1,0:T(8,128)S(1)}, u32[]{:S(2)}, u32[]{:S(2)}) %collective-permute-start.11) | collective-permute-done | bytes 40992 | tf_op jit(solution)/shard_map/ppermute | solution.py:22
  39.0 0.9 %histogram.1 = (f32[20,128]{1,0:T(8,128)S(1)}, f32[20,128]{1,0:T(8,128)S(1)}) custom-call(f32[80,128]{1,0:T(8,128)S(1)} %add.9.conn_ref, f32[80,128]{1,0:T(8,128)S(1)} %collective-permute-done.11.other_ref), custom_call_target="tpu_custom_call" | custom-call | tf_op jit(solution)/shard_map/histogram/pallas_call | solution.py:191
  39.9 0.0 collective-permute-start.12
  40.0 3.1 %collective-permute-done.12 = f32[20,128]{1,0:T(8,128)S(1)} collective-permute-done((f32[20,128]{1,0:T(8,128)S(1)}, f32[20,128]{1,0:T(8,128)S(1)}, u32[]{:S(2)}, u32[]{:S(2)}) %collective-permute-start.12) | collective-permute-done | bytes 10272 | tf_op jit(solution)/shard_map/ppermute | solution.py:22
  43.1 0.0 collective-permute-start.13
  43.1 3.1 %collective-permute-done.13 = f32[20,128]{1,0:T(8,128)S(1)} collective-permute-done((f32[20,128]{1,0:T(8,128)S(1)}, f32[20,128]{1,0:T(8,128)S(1)}, u32[]{:S(2)}, u32[]{:S(2)}) %collective-permute-start.13) | collective-permute-done | bytes 10272 | tf_op jit(solution)/shard_map/ppermute | solution.py:22
  46.2 0.0 collective-permute-start.14
  46.2 0.6 %copy.5 = f32[128,20]{0,1:T(8,128)} copy(f32[128,20]{0,1:T(8,128)S(1)} %bitcast.1) | data formatting | bytes 20480
  46.8 0.6 %collective-permute-done.14.other_ref = f32[20,128]{1,0:T(8,128)S(1)} collective-permute-done((f32[20,128]{1,0:T(8,128)S(1)}, f32[20,128]{1,0:T(8,128)S(1)}, u32[]{:S(2)}, u32[]{:S(2)}) %collective-permute-start.14) | collective-permute-done | bytes 10272 | tf_op jit(solution)/shard_map/ppermute | solution.py:22
  47.4 0.7 %scale_free_fit.1 = (f32[20]{0:T(128)}, f32[20]{0:T(128)}) custom-call(f32[20,128]{1,0:T(8,128)S(1)} %add.11.hist_ref, f32[20,128]{1,0:T(8,128)S(1)} %collective-permute-done.14.other_ref), custom_call_target="tpu_custom_call" | custom-call | tf_op jit(solution)/shard_map/scale_free_fit/pallas_call | solution.py:232
  (3 shorter events, 0.0 us)
Async XLA Ops:
  0.6 13.9 %collective-permute-start.2 = (bf16[128,1024]{1,0:T(8,128)(2,1)}, bf16[128,1024]{1,0:T(8,128)(2,1)S(1)}, u32[]{:S(2)}, u32[]{:S(2)}) collective-permute-start(bf16[128,1024]{1,0:T(8,128)(2,1)} %refs_5_.1), channel_id=1, source_target_pairs={{0,8},{1,9},{2,10},{3,11},{4,12},{5,13},{6,14},{7,15},{8,0},{9,1},... | collective-permute-start | bytes 786440 | tf_op jit(solution)/shard_map/ppermute | solution.py:22
  3.7 13.5 %collective-permute-start.6 = (bf16[128,1024]{1,0:T(8,128)(2,1)}, bf16[128,1024]{1,0:T(8,128)(2,1)S(1)}, u32[]{:S(2)}, u32[]{:S(2)}) collective-permute-start(bf16[128,1024]{1,0:T(8,128)(2,1)} %refs_5_.1), channel_id=1, source_target_pairs={{0,4},{1,5},{2,6},{3,7},{4,0},{5,1},{6,2},{7,3},{8,12},{9,13},{10,... | collective-permute-start | bytes 786440 | tf_op jit(solution)/shard_map/ppermute | solution.py:22
  5.3 14.3 %collective-permute-start.1 = (bf16[128,1024]{1,0:T(8,128)(2,1)}, bf16[128,1024]{1,0:T(8,128)(2,1)S(1)}, u32[]{:S(2)}, u32[]{:S(2)}) collective-permute-start(bf16[128,1024]{1,0:T(8,128)(2,1)} %refs_5_.1), channel_id=1, source_target_pairs={{0,16},{1,17},{2,18},{3,19},{4,20},{5,21},{6,22},{7,23},{8,24},{9,... | collective-permute-start | bytes 786440 | tf_op jit(solution)/shard_map/ppermute | solution.py:22
  7.9 11.7 %collective-permute-start = (bf16[128,1024]{1,0:T(8,128)(2,1)}, bf16[128,1024]{1,0:T(8,128)(2,1)S(1)}, u32[]{:S(2)}, u32[]{:S(2)}) collective-permute-start(bf16[128,1024]{1,0:T(8,128)(2,1)} %refs_5_.1), channel_id=1, source_target_pairs={{0,2},{1,3},{2,0},{3,1},{4,6},{5,7},{6,4},{7,5},{8,10},{9,11},{10,... | collective-permute-start | bytes 786440 | tf_op jit(solution)/shard_map/ppermute | solution.py:22
  14.5 8.1 %collective-permute-start.3 = (bf16[128,1024]{1,0:T(8,128)(2,1)S(1)}, bf16[128,1024]{1,0:T(8,128)(2,1)S(1)}, u32[]{:S(2)}, u32[]{:S(2)}) collective-permute-start(bf16[128,1024]{1,0:T(8,128)(2,1)S(1)} %collective-permute-done.2.refs_4_.refs_6_), channel_id=1, source_target_pairs={{0,4},{1,5},{2,6},{3,7},{4,0},{5,1},{6,2},{7,3},{8,12},{9,13},{10,... | collective-permute-start | bytes 786440 | tf_op jit(solution)/shard_map/ppermute | solution.py:22
  17.2 7.2 %collective-permute-start.7 = (bf16[128,1024]{1,0:T(8,128)(2,1)}, bf16[128,1024]{1,0:T(8,128)(2,1)S(1)}, u32[]{:S(2)}, u32[]{:S(2)}) collective-permute-start(bf16[128,1024]{1,0:T(8,128)(2,1)} %refs_5_.1), channel_id=1, source_target_pairs={{0,1},{1,0},{2,3},{3,2},{4,5},{5,4},{6,7},{7,6},{8,9},{9,8},{10,11... | collective-permute-start | bytes 786440 | tf_op jit(solution)/shard_map/ppermute | solution.py:22
  17.2 8.8 %collective-permute-start.9 = (bf16[128,1024]{1,0:T(8,128)(2,1)S(1)}, bf16[128,1024]{1,0:T(8,128)(2,1)S(1)}, u32[]{:S(2)}, u32[]{:S(2)}) collective-permute-start(bf16[128,1024]{1,0:T(8,128)(2,1)S(1)} %collective-permute-done.6.refs_4_.refs_7_), channel_id=1, source_target_pairs={{0,1},{1,0},{2,3},{3,2},{4,5},{5,4},{6,7},{7,6},{8,9},{9,8},{10,11... | collective-permute-start | bytes 786440 | tf_op jit(solution)/shard_map/ppermute | solution.py:22
  19.5 6.5 %collective-permute-start.8 = (bf16[128,1024]{1,0:T(8,128)(2,1)S(1)}, bf16[128,1024]{1,0:T(8,128)(2,1)S(1)}, u32[]{:S(2)}, u32[]{:S(2)}) collective-permute-start(bf16[128,1024]{1,0:T(8,128)(2,1)S(1)} %collective-permute-done.2.refs_4_.refs_6_), channel_id=1, source_target_pairs={{0,1},{1,0},{2,3},{3,2},{4,5},{5,4},{6,7},{7,6},{8,9},{9,8},{10,11... | collective-permute-start | bytes 786440 | tf_op jit(solution)/shard_map/ppermute | solution.py:22
  19.6 8.7 %collective-permute-start.5 = (bf16[128,1024]{1,0:T(8,128)(2,1)S(1)}, bf16[128,1024]{1,0:T(8,128)(2,1)S(1)}, u32[]{:S(2)}, u32[]{:S(2)}) collective-permute-start(bf16[128,1024]{1,0:T(8,128)(2,1)S(1)} %collective-permute-done.1.refs_2_.refs_1_), channel_id=1, source_target_pairs={{0,2},{1,3},{2,0},{3,1},{4,6},{5,7},{6,4},{7,5},{8,10},{9,11},{10,... | collective-permute-start | bytes 786440 | tf_op jit(solution)/shard_map/ppermute | solution.py:22
  22.7 5.6 %collective-permute-start.4 = (bf16[128,1024]{1,0:T(8,128)(2,1)S(1)}, bf16[128,1024]{1,0:T(8,128)(2,1)S(1)}, u32[]{:S(2)}, u32[]{:S(2)}) collective-permute-start(bf16[128,1024]{1,0:T(8,128)(2,1)S(1)} %collective-permute-done.3.refs_3_.refs_8_), channel_id=1, source_target_pairs={{0,1},{1,0},{2,3},{3,2},{4,5},{5,4},{6,7},{7,6},{8,9},{9,8},{10,11... | collective-permute-start | bytes 786440 | tf_op jit(solution)/shard_map/ppermute | solution.py:22
  22.7 1.0 %copy-start = (bf16[128,1024]{1,0:T(8,128)(2,1)S(1)}, bf16[128,1024]{1,0:T(8,128)(2,1)}, u32[]{:S(2)}) copy-start(bf16[128,1024]{1,0:T(8,128)(2,1)} %refs_5_.1) | copy-start | bytes 786436
  26.0 2.2 %copy-start.1 = (s32[20]{0:T(128)S(1)}, s32[20]{0:T(128)}, u32[]{:S(2)}) copy-start(s32[20]{0:T(128)} %order_hbm.1) | copy-start | bytes 244
  30.0 4.1 %collective-permute-start.10 = (f32[80,128]{1,0:T(8,128)S(1)}, f32[80,128]{1,0:T(8,128)S(1)}, u32[]{:S(2)}, u32[]{:S(2)}) collective-permute-start(f32[80,128]{1,0:T(8,128)S(1)} %last_sums.1), channel_id=1, source_target_pairs={{0,2},{1,3},{2,0},{3,1},{4,6},{5,7},{6,4},{7,5},{8,10},{9,11},{10,... | collective-permute-start | bytes 122888 | tf_op jit(solution)/shard_map/ppermute | solution.py:22
  34.1 4.9 %collective-permute-start.11 = (f32[80,128]{1,0:T(8,128)S(1)}, f32[80,128]{1,0:T(8,128)S(1)}, u32[]{:S(2)}, u32[]{:S(2)}) collective-permute-start(f32[80,128]{1,0:T(8,128)S(1)} %add.9.conn_ref), channel_id=1, source_target_pairs={{0,16},{1,17},{2,18},{3,19},{4,20},{5,21},{6,22},{7,23},{8,24},{9,... | collective-permute-start | bytes 122888 | tf_op jit(solution)/shard_map/ppermute | solution.py:22
  39.9 3.2 %collective-permute-start.12 = (f32[20,128]{1,0:T(8,128)S(1)}, f32[20,128]{1,0:T(8,128)S(1)}, u32[]{:S(2)}, u32[]{:S(2)}) collective-permute-start(f32[20,128]{1,0:T(8,128)S(1)} %get-tuple-element.8), channel_id=1, source_target_pairs={{0,9},{1,8},{2,11},{3,10},{4,13},{5,12},{6,15},{7,14},{8,1},{9,0},... | collective-permute-start | bytes 30728 | tf_op jit(solution)/shard_map/ppermute | solution.py:22
  43.1 3.1 %collective-permute-start.13 = (f32[20,128]{1,0:T(8,128)S(1)}, f32[20,128]{1,0:T(8,128)S(1)}, u32[]{:S(2)}, u32[]{:S(2)}) collective-permute-start(f32[20,128]{1,0:T(8,128)S(1)} %add.10), channel_id=1, source_target_pairs={{0,5},{1,4},{2,7},{3,6},{4,1},{5,0},{6,3},{7,2},{8,13},{9,12},{10,... | collective-permute-start | bytes 30728 | tf_op jit(solution)/shard_map/ppermute | solution.py:22
  46.2 1.2 %collective-permute-start.14 = (f32[20,128]{1,0:T(8,128)S(1)}, f32[20,128]{1,0:T(8,128)S(1)}, u32[]{:S(2)}, u32[]{:S(2)}) collective-permute-start(f32[20,128]{1,0:T(8,128)S(1)} %add.11.hist_ref), channel_id=1, source_target_pairs={{0,1},{1,0},{2,3},{3,2},{4,5},{5,4},{6,7},{7,6},{8,9},{9,8},{10,11... | collective-permute-start | bytes 30728 | tf_op jit(solution)/shard_map/ppermute | solution.py:22
